TPU v7x, 32 devices: a whole 2x2x4 slice. The times are simulated.
32 devices in a mesh: groups: 2 (over y), ep: 16 (over z, x, core).
Axes of the slice: x: 2, y: 2, z: 4, core: 2. Of those that a mesh axis runs over, the one named last changes fastest.
Arguments:
- tokens: bfloat16 [128, 7168], P(('groups', 'ep')), parts along dimension 0, may hold values from -6 to 6
- routes: int32 [128, 1], P(('groups', 'ep')), parts along dimension 0, may hold values from 0 to 1; in each aligned block of 4 rows (0 to 3, 4 to 7, ...) at most 2 rows name the same one
- router_weight: bfloat16 [7168, 2], replicated, may hold values from -0.0625 to 0.0625
- w_gate: bfloat16 [7168, 4096], P(None, 'ep'), may hold values from -0.0625 to 0.0625
- w_up: bfloat16 [7168, 4096], P(None, 'ep'), may hold values from -0.0625 to 0.0625
- w_down: bfloat16 [4096, 7168], P('ep'), may hold values from -0.125 to 0.125
- latent_pool: bfloat16 [512, 4608], P(('groups', 'ep')), parts along dimension 0, may hold values from -8 to 8
- send_order: int32 [32, 16], P(('groups', 'ep')), parts along dimension 0, may hold values from 0 to 15, each once within a row
- block_table: int32 [32, 16], P(('groups', 'ep')), parts along dimension 0, may hold values from 0 to 15, each once within a row
- seq_lens: int32 [128], P(('groups', 'ep')), parts along dimension 0, may hold values from 1 to 32
- queries: bfloat16 [128, 73728], P(('groups', 'ep')), parts along dimension 0, may hold values from -10 to 10
Outputs:
- expert_out: bfloat16 [128, 7168], P(('groups', 'ep')), parts along dimension 0
- attended: bfloat16 [128, 65536], P(('groups', 'ep')), parts along dimension 0
There are 2 independent parts, one for each index of `groups`. A program takes and returns all parts, laid end to end along the dimension named above; an argument that names none is the same for every part. Nothing has to cross between parts.
Inputs may be any that keep to these rules, and one draw needn't show every extreme that they name: `routes`: among the 4 rows of one device no expert is named by more than 2 rows, a bound that some block reaches. `send_order`: each row is a permutation of 0 to 15. `block_table`: each row is a permutation of 0 to 15.
All inputs are finite; a program needn't handle non-finite values.
Results may differ from a plain program's by a relative error of at most 0.01.
Values may be sent and summed in bfloat16 or wider, within the bound.
No kernel may reach another device: no remote copies, remote signals or barrier semaphores. Data moves between devices by JAX's collectives and lax.ppermute only.
A program may use at most 128 MiB of HBM per device.

v0:
```python
import jax
import jax.numpy as jnp
from jax import lax
from jax.sharding import PartitionSpec as P

LATENT_RANK = 512
ROTARY_WIDTH = 64
BLOCK = 8


route_scale = 2.5
softmax_scale = 192.0 ** (-0.5)


def body(
    tokens,
    routes,
    router_weight,
    w_gate,
    w_up,
    w_down,
    latent_pool,
    send_order,
    block_table,
    seq_lens,
    queries,
):
    device_count = lax.axis_size("ep")
    tok_rows, width = tokens.shape
    experts = router_weight.shape[1]
    top_count = routes.shape[1]
    shard_count = device_count // experts
    capacity = tok_rows * top_count // experts + tok_rows * top_count // (4 * experts)
    scores = jax.nn.sigmoid(jnp.dot(tokens, router_weight, preferred_element_type=jnp.float32))
    chosen = jnp.sum(
        (routes[:, :, None] == jnp.arange(experts, dtype=jnp.int32)[None, None, :]).astype(
            jnp.float32
        ),
        axis=1,
    )
    weighted = scores * chosen
    gate_share = route_scale * weighted / jnp.sum(weighted, axis=-1, keepdims=True)
    earlier = jnp.cumsum(chosen, axis=0) - chosen
    slot_ids = jnp.arange(capacity, dtype=jnp.float32)
    placed = (
        (chosen.T[:, None, :] > 0.5) & (earlier.T[:, None, :] == slot_ids[None, :, None])
    ).astype(jnp.float32)
    packed = jnp.dot(
        placed.reshape(experts * capacity, tok_rows).astype(jnp.bfloat16),
        tokens,
        preferred_element_type=jnp.float32,
    ).astype(jnp.bfloat16)
    outgoing = jnp.broadcast_to(
        packed.reshape(experts, 1, capacity, width), (experts, shard_count, capacity, width)
    )
    outgoing = outgoing.reshape(device_count, capacity, width)
    received = lax.all_to_all(outgoing, "ep", split_axis=0, concat_axis=0, tiled=True)
    slot_count = received.shape[1]
    flat_rows = received.reshape(-1, width)
    gate_out = jnp.dot(flat_rows, w_gate, preferred_element_type=jnp.float32)
    up_out = jnp.dot(flat_rows, w_up, preferred_element_type=jnp.float32)
    hidden = (jax.nn.silu(gate_out) * up_out).astype(jnp.bfloat16)
    partial_value = jnp.dot(hidden, w_down, preferred_element_type=jnp.float32).astype(jnp.bfloat16)
    partial_value = partial_value.reshape(device_count, slot_count, width)
    returned_rows = lax.all_to_all(partial_value, "ep", split_axis=0, concat_axis=0, tiled=True)
    summed = jnp.sum(
        returned_rows.reshape(experts, shard_count, slot_count, width).astype(jnp.float32), axis=1
    )
    mixing = (placed * gate_share.T[:, None, :]).reshape(experts * capacity, tok_rows)
    expert_out = jnp.dot(
        mixing.T,
        summed.reshape(experts * capacity, width),
        precision=lax.Precision.HIGHEST,
        preferred_element_type=jnp.float32,
    ).astype(jnp.bfloat16)
    compressed_width = LATENT_RANK + ROTARY_WIDTH
    outgoing_blocks = jnp.take(latent_pool, send_order[0], axis=0)
    arrived = lax.all_to_all(outgoing_blocks, "ep", split_axis=0, concat_axis=0, tiled=True)
    sequence_total = seq_lens.shape[0]
    span_length = device_count // sequence_total * BLOCK
    cached_latent_rows = jnp.take(arrived, block_table[0], axis=0).reshape(
        sequence_total, span_length, compressed_width
    )
    attention_head_count = queries.shape[1] // compressed_width
    query_rows = queries.reshape(sequence_total, attention_head_count, compressed_width)
    logits = (
        jnp.einsum(
            "shc,slc->shl", query_rows, cached_latent_rows, preferred_element_type=jnp.float32
        )
        * softmax_scale
    )
    visible = jnp.arange(span_length, dtype=jnp.int32)[None, None, :] < seq_lens[:, None, None]
    logits = jnp.where(visible, logits, -1e30)
    row_peak = jnp.max(logits, axis=-1, keepdims=True)
    unnormed = jnp.exp(logits - row_peak)
    routing_weight = (unnormed / jnp.sum(unnormed, axis=-1, keepdims=True)).astype(jnp.bfloat16)
    attended = jnp.einsum(
        "djp,dpz->djz",
        routing_weight,
        cached_latent_rows[:, :, :LATENT_RANK],
        preferred_element_type=jnp.float32,
    )
    attended = attended.astype(jnp.bfloat16).reshape(
        sequence_total, attention_head_count * LATENT_RANK
    )
    return (expert_out, attended)


def solution(mesh):
    return jax.shard_map(
        body,
        mesh=mesh,
        in_specs=(
            P(("groups", "ep"), None),
            P(("groups", "ep"), None),
            P(),
            P(None, "ep"),
            P(None, "ep"),
            P("ep", None),
            P(("groups", "ep"), None),
            P(("groups", "ep"), None),
            P(("groups", "ep"), None),
            P(("groups", "ep")),
            P(("groups", "ep"), None),
        ),
        out_specs=(P(("groups", "ep"), None), P(("groups", "ep"), None)),
        check_vma=False,
    )
```

profile of v0, /device:TPU:0, one launch (start us, length us, event | category | flops | bytes accessed | tf_op | source)
XLA Modules:
  0.0 65.6 jit_solution(5185237046143555233)
XLA Ops:
  0.7 0.7 %compare_select_fusion.1 = s32[16]{0:T(128)S(1)} fusion(s32[1,16]{1,0:T(1,128)} %param.20), kind=kLoop, calls=%fused_computation.37 | loop fusion | flops 48 | bytes 128 | tf_op jit(solution)/shard_map/jit(_take)/jit(_where)/select_n | solution.py:77
  1.4 0.7 %compare_and_fusion.1 = pred[16]{0:T(512)(128)(4,1)S(1)} fusion(s32[1,16]{1,0:T(1,128)} %param.20), kind=kLoop, calls=%fused_computation.42 | loop fusion | flops 96 | bytes 80 | tf_op jit(solution)/shard_map/jit(_take)/and | solution.py:77
  2.1 0.6 gather_fusion
  3.3 0.7 %reduce = bf16[16,4608]{1,0:T(8,128)(2,1)S(1)} reduce(bf16[16,1,4608]{2,0,1:T(8,128)(2,1)S(1)} %select_bitcast_fusion, bf16[]{:T(256)} %broadcast.128), dimensions={1}, to_apply=%copy.17.reduce_sub_computation | reduce | bytes 294914 | tf_op jit(solution)/shard_map/all_to_all | solution.py:78
  4.0 0.7 %reshape.115 = bf16[16,2,2304]{2,1,0:T(2,128)(2,1)} reshape(bf16[16,4608]{1,0:T(8,128)(2,1)S(1)} %reduce) | data formatting | bytes 294912
  4.7 7.4 %all-to-all-start.2 = ((bf16[16,2,2304]{2,1,0:T(2,128)(2,1)}), bf16[16,2,2304]{2,1,0:T(2,128)(2,1)S(1)}, u32[]{:S(2)}, u32[]{:S(2)}) async-start(bf16[16,2,2304]{2,1,0:T(2,128)(2,1)} %reshape.115), calls=%async_computation.2 | async-start | bytes 294912 | tf_op jit(solution)/shard_map/all_to_all | solution.py:78
  12.1 0.7 %fusion.27 = f32[4,2]{0,1:T(2,128)S(1)} fusion(s32[4]{0:T(128)} %bitcast.52), kind=kLoop, calls=%fused_computation.55 | loop fusion | flops 16 | bytes 48 | tf_op jit(solution)/shard_map/convert_element_type | solution.py:36
  12.8 1.0 %select_reduce_fusion = (f32[4]{0:T(128)S(1)}, f32[4,2]{0,1:T(2,128)S(1)}) fusion(s32[4]{0:T(128)} %bitcast.53, bf16[4,7168]{1,0:T(4,128)(2,1)} %param.13, bf16[7168,2]{0,1:T(2,128)(2,1)} %param.15), kind=kOutput, calls=%fused_computation.52 | convolution fusion | flops 114732 | bytes 86080 | tf_op jit(solution)/shard_map/dot_general | solution.py:34
  14.0 0.7 %fusion.22 = (f32[2,4]{1,0:T(2,128)S(1)}, f32[2,4]{1,0:T(2,128)S(1)}) fusion(f32[4,2]{0,1:T(2,128)S(1)} %get-tuple-element.6, f32[4]{0:T(128)S(1)} %get-tuple-element.5, s32[4]{0:T(128)} %bitcast.54, f32[4,2]{0,1:T(2,128)S(1)} %reduce_window_sum.13), kind=kLoop, calls=%fused_computation.48 | loop fusion | flops 48 | bytes 160 | tf_op jit(solution)/shard_map/div | solution.py:42
  14.7 0.7 %convert_compare_fusion = pred[2,4]{1,0:T(4,128)(4,1)S(1)} fusion(s32[4]{0:T(128)} %bitcast.55), kind=kLoop, calls=%fused_computation.45 | loop fusion | flops 24 | bytes 24 | tf_op jit(solution)/shard_map/gt | solution.py:46
  15.4 1.0 %convolution_convert_fusion.1 = bf16[4,7168]{1,0:T(4,128)(2,1)S(1)} fusion(bf16[4,7168]{1,0:T(4,128)(2,1)} %param.13, pred[4,4]{1,0:T(4,128)(4,1)S(1)} %and.19, f32[4,4]{1,0:T(4,128)S(1)} %bitcast.51, f32[4]{0:T(128)S(1)} %eq.63), kind=kOutput, calls=%fused_computation.6 | convolution fusion | flops 258112 | bytes 114784 | tf_op jit(solution)/shard_map/dot_general | solution.py:48
  16.5 3.8 %all-to-all-done.2 = bf16[16,2,2304]{2,1,0:T(2,128)(2,1)S(1)} async-done(((bf16[16,2,2304]{2,1,0:T(2,128)(2,1)}), bf16[16,2,2304]{2,1,0:T(2,128)(2,1)S(1)}, u32[]{:S(2)}, u32[]{:S(2)}) %all-to-all-start.2) | async-done | bytes 147488 | tf_op jit(solution)/shard_map/all_to_all | solution.py:78
  20.3 1.0 %broadcast_in_dim.26 = bf16[2,8,2,7168]{3,2,1,0:T(2,128)(2,1)} broadcast(bf16[2,2,7168]{2,1,0:T(2,128)(2,1)S(1)} %broadcast_in_dim.21), dimensions={0,2,3} | broadcast | bytes 516096 | tf_op jit(solution)/shard_map/broadcast_in_dim | solution.py:53
  21.3 3.6 %all-to-all-start = ((bf16[16,2,7168]{2,1,0:T(2,128)(2,1)}), bf16[16,2,7168]{2,1,0:T(2,128)(2,1)S(1)}, u32[]{:S(2)}, u32[]{:S(2)}) async-start(bf16[16,2,7168]{2,1,0:T(2,128)(2,1)} %bitcast.4), calls=%async_computation | async-start | bytes 917504 | tf_op jit(solution)/shard_map/all_to_all | solution.py:57
  24.9 0.7 %reshape.89 = bf16[4,128,576]{2,1,0:T(8,128)(2,1)S(1)} reshape(bf16[4,73728]{1,0:T(4,128)(2,1)S(1)} %copy-done.1) | data formatting | bytes 1179648 | tf_op jit(solution)/shard_map/reshape | solution.py:85
  25.8 0.6 gather_fusion.1
  26.4 11.6 %all-to-all-done = bf16[16,2,7168]{2,1,0:T(2,128)(2,1)S(1)} async-done(((bf16[16,2,7168]{2,1,0:T(2,128)(2,1)}), bf16[16,2,7168]{2,1,0:T(2,128)(2,1)S(1)}, u32[]{:S(2)}, u32[]{:S(2)}) %all-to-all-start) | async-done | bytes 458784 | tf_op jit(solution)/shard_map/all_to_all | solution.py:57
  38.2 2.8 %fusion.31 = f32[32,256]{1,0:T(8,128)S(1)} fusion(bf16[32,7168]{1,0:T(8,128)(2,1)S(1)} %reshape.86, bf16[7168,256]{1,0:T(8,128)(2,1)} %param.16), kind=kOutput, calls=%fused_computation.60 | convolution fusion | flops 117440512 | bytes 4161536 | tf_op jit(solution)/shard_map/dot_general | solution.py:60
  41.0 5.2 %convolution_convert_fusion = bf16[32,7168]{1,0:T(8,128)(2,1)S(1)} fusion(bf16[256,7168]{1,0:T(8,128)(2,1)} %param.18, bf16[32,7168]{1,0:T(8,128)(2,1)S(1)} %reshape.86, bf16[7168,256]{1,0:T(8,128)(2,1)} %param.17, f32[32,256]{1,0:T(8,128)S(1)} %fusion.31), kind=kOutput, calls=%fused_computation.3 | convolution fusion | flops 235159552 | bytes 8290304 | tf_op jit(solution)/shard_map/dot_general | solution.py:63
  46.2 1.0 %reshape.87 = bf16[16,2,7168]{2,1,0:T(2,128)(2,1)} reshape(bf16[32,7168]{1,0:T(8,128)(2,1)S(1)} %convolution_convert_fusion) | data formatting | bytes 917504 | tf_op jit(solution)/shard_map/reshape | solution.py:64
  47.2 3.7 %all-to-all-start.1 = ((bf16[16,2,7168]{2,1,0:T(2,128)(2,1)}), bf16[16,2,7168]{2,1,0:T(2,128)(2,1)S(1)}, u32[]{:S(2)}, u32[]{:S(2)}) async-start(bf16[16,2,7168]{2,1,0:T(2,128)(2,1)} %reshape.87), calls=%async_computation.1 | async-start | bytes 917504 | tf_op jit(solution)/shard_map/all_to_all | solution.py:65
  51.9 1.2 %copy.21 = bf16[1,4,128,512]{3,1,2,0:T(4,128)(2,1)} copy(bf16[1,4,128,512]{3,2,1,0:T(8,128)(2,1)S(1)} %fusion.2) | data formatting | bytes 1048576
  53.1 11.0 %all-to-all-done.1 = bf16[16,2,7168]{2,1,0:T(2,128)(2,1)S(1)} async-done(((bf16[16,2,7168]{2,1,0:T(2,128)(2,1)}), bf16[16,2,7168]{2,1,0:T(2,128)(2,1)S(1)}, u32[]{:S(2)}, u32[]{:S(2)}) %all-to-all-start.1) | async-done | bytes 458784 | tf_op jit(solution)/shard_map/all_to_all | solution.py:65
  64.5 1.1 %fusion.1 = bf16[4,7168]{1,0:T(4,128)(2,1)} fusion(f32[2,2,7168]{2,1,0:T(2,128)S(1)} %convert_reduce_fusion, pred[2,4]{1,0:T(4,128)(4,1)S(1)} %convert_compare_fusion, f32[2,4]{1,0:T(2,128)S(1)} %get-tuple-element.3, f32[2,4]{1,0:T(2,128)S(1)} %get-tuple-element.4), kind=kOutput, calls=%fused_computation.5 | convolution fusion | flops 1404976 | bytes 172104 | tf_op jit(solution)/shard_map/dot_general | solution.py:70
  (30 shorter events, 2.7 us)
Async XLA Ops:
  0.6 1.4 %copy-start = (bf16[16,4608]{1,0:T(8,128)(2,1)S(1)}, bf16[16,4608]{1,0:T(8,128)(2,1)}, u32[]{:S(2)}) copy-start(bf16[16,4608]{1,0:T(8,128)(2,1)} %param.19) | copy-start | bytes 442372
  0.6 24.2 %copy-start.1 = (bf16[4,73728]{1,0:T(4,128)(2,1)S(1)}, bf16[4,73728]{1,0:T(4,128)(2,1)}, u32[]{:S(2)}) copy-start(bf16[4,73728]{1,0:T(4,128)(2,1)} %param.23) | copy-start | bytes 1769476
  0.7 24.9 %copy-start.2 = (s32[1,16]{1,0:T(1,128)S(1)}, s32[1,16]{1,0:T(1,128)}, u32[]{:S(2)}) copy-start(s32[1,16]{1,0:T(1,128)} %param.21) | copy-start | bytes 196
  0.7 24.9 %copy-start.3 = (s32[4]{0:T(128)S(1)}, s32[4]{0:T(128)}, u32[]{:S(2)}) copy-start(s32[4]{0:T(128)} %param.22) | copy-start | bytes 52
  4.7 15.6 %all-to-all-start.2 = ((bf16[16,2,2304]{2,1,0:T(2,128)(2,1)}), bf16[16,2,2304]{2,1,0:T(2,128)(2,1)S(1)}, u32[]{:S(2)}, u32[]{:S(2)}) async-start(bf16[16,2,2304]{2,1,0:T(2,128)(2,1)} %reshape.115), calls=%async_computation.2 | async-start | bytes 294912 | tf_op jit(solution)/shard_map/all_to_all | solution.py:78
  21.3 16.8 %all-to-all-start = ((bf16[16,2,7168]{2,1,0:T(2,128)(2,1)}), bf16[16,2,7168]{2,1,0:T(2,128)(2,1)S(1)}, u32[]{:S(2)}, u32[]{:S(2)}) async-start(bf16[16,2,7168]{2,1,0:T(2,128)(2,1)} %bitcast.4), calls=%async_computation | async-start | bytes 917504 | tf_op jit(solution)/shard_map/all_to_all | solution.py:57
  47.2 16.9 %all-to-all-start.1 = ((bf16[16,2,7168]{2,1,0:T(2,128)(2,1)}), bf16[16,2,7168]{2,1,0:T(2,128)(2,1)S(1)}, u32[]{:S(2)}, u32[]{:S(2)}) async-start(bf16[16,2,7168]{2,1,0:T(2,128)(2,1)} %reshape.87), calls=%async_computation.1 | async-start | bytes 917504 | tf_op jit(solution)/shard_map/all_to_all | solution.py:65
where the time goes:
time: 66.2 us; the launch traced here: 65.6 us
  waiting for transfers between devices  26.4 us (40%)
  starting transfers between devices  14.7 us (22%)
  matrix products  11.9 us (18%)
  local copies, waits for them, and re-layouts  6.95 us (10%)
  other arithmetic  4.91 us (7%)
  between operations  0.84 us (1%)
    all_to_all x1, waiting for transfers between devices, body(): lax.all_to_all(outgoing, 'ep', split_axis=0, concat_axis=0, tiled=True)  11.6 us
    all_to_all x1, waiting for transfers between devices, body(): lax.all_to_all(partial_value, 'ep', split_axis=0, concat_axis=0, tiled=True)  11 us
    all_to_all x1, starting transfers between devices, body(): lax.all_to_all(outgoing_blocks, 'ep', split_axis=0, concat_axis=0, tiled=...  7.39 us
    dot_general x1, matrix products, body(): jnp.dot(hidden, w_down, preferred_element_type=jnp.float32)  5.25 us
    all_to_all x1, waiting for transfers between devices, body(): lax.all_to_all(outgoing_blocks, 'ep', split_axis=0, concat_axis=0, tiled=...  3.75 us
    all_to_all x1, starting transfers between devices, body(): lax.all_to_all(partial_value, 'ep', split_axis=0, concat_axis=0, tiled=True)  3.72 us
    all_to_all x1, starting transfers between devices, body(): lax.all_to_all(outgoing, 'ep', split_axis=0, concat_axis=0, tiled=True)  3.56 us
    dot_general x1, matrix products, body(): gate_out = jnp.dot(flat_rows, w_gate, preferred_element_type=jnp.float32)  2.77 us
  transfers between devices with their start and end apart: 3, of which 3 were waited for; matrix products, arithmetic and copies ran while one was open for 12% of the time, Pallas kernels for 0%

commit v1 on v0

v1 whole, which is shorter than its diff:
```python
import functools

import jax
import jax.numpy as jnp
from jax import lax
from jax.experimental import pallas as pl
from jax.experimental.pallas import tpu as pltpu
from jax.sharding import PartitionSpec as P

LATENT_RANK = 512
ROTARY_WIDTH = 64
BLOCK = 8


route_scale = 2.5
softmax_scale = 192.0 ** (-0.5)


def vmem():
    return pl.BlockSpec(memory_space=pltpu.VMEM)


def smem():
    return pl.BlockSpec(memory_space=pltpu.SMEM)


def placements(routes_ref, mine, blocks, caps, axis):
    tok_rows, top = routes_ref.shape
    shape = (blocks * caps, 128) if axis == 0 else (tok_rows, blocks * caps)
    row = lax.broadcasted_iota(jnp.int32, shape, axis)
    expert = (row // caps) ^ mine
    slot = row % caps
    count = jnp.zeros(shape, jnp.int32)
    out = []
    for t in range(tok_rows):
        hit = expert == routes_ref[t, 0]
        for j in range(1, top):
            hit = hit | (expert == routes_ref[t, j])
        out.append(hit & (count == slot))
        count = count + hit.astype(jnp.int32)
    return out


def pack_kernel(caps, mine_ref, routes_ref, tokens_ref, *out_refs):
    blocks = len(out_refs)
    width = tokens_ref.shape[1]
    placed = placements(routes_ref, mine_ref[0], blocks, caps, 0)
    tokens = tokens_ref[...].astype(jnp.float32)
    rows = jnp.zeros((blocks * caps, width), jnp.float32)
    for t, hit in enumerate(placed):
        rows = rows + jnp.where(hit[:, :1], tokens[t : t + 1, :], 0.0)
    rows = rows.astype(jnp.bfloat16)
    for b in range(blocks):
        out_refs[b][...] = rows[b * caps : (b + 1) * caps, :]


def mix_kernel(caps, mine_ref, routes_ref, tokens_ref, centroids_ref, out_ref):
    tok_rows, top = routes_ref.shape
    experts = centroids_ref.shape[0]
    mine = mine_ref[0]
    scores = jax.nn.sigmoid(
        lax.dot_general(
            tokens_ref[...],
            centroids_ref[...],
            (((1,), (1,)), ((), ())),
            preferred_element_type=jnp.float32,
        )
    )
    expert = lax.broadcasted_iota(jnp.int32, (tok_rows, experts), 1)
    token = lax.broadcasted_iota(jnp.int32, (tok_rows, experts), 0)
    chosen = jnp.zeros((tok_rows, experts), jnp.float32)
    for t in range(tok_rows):
        for j in range(top):
            hit = (token == t) & (expert == routes_ref[t, j])
            chosen = jnp.where(hit, chosen + 1.0, chosen)
    weighted = scores * chosen
    share = route_scale * weighted / jnp.sum(weighted, axis=-1, keepdims=True)
    shape = (tok_rows, experts * caps)
    row = lax.broadcasted_iota(jnp.int32, shape, 1)
    row_expert = (row // caps) ^ mine
    row_share = jnp.zeros(shape, jnp.float32)
    for e in range(experts):
        row_share = jnp.where(row_expert == e, share[:, e : e + 1], row_share)
    placed = placements(routes_ref, mine, experts, caps, 1)
    row_token = lax.broadcasted_iota(jnp.int32, shape, 0)
    mixing = jnp.zeros(shape, jnp.float32)
    for t, hit in enumerate(placed):
        mixing = jnp.where((row_token == t) & hit, row_share, mixing)
    out_ref[...] = mixing


def ffn_kernel(
    chunks, near_ref, far_ref, gate_hbm, up_hbm, down_hbm, keep_ref, send_ref, gate, up, down, sems
):
    width, units = gate.shape
    step = width // chunks
    half = near_ref.shape[0]

    def copies(i):
        part = pl.ds(i * step, step)
        return (
            pltpu.make_async_copy(gate_hbm.at[part, :], gate.at[part, :], sems.at[0, i]),
            pltpu.make_async_copy(up_hbm.at[part, :], up.at[part, :], sems.at[1, i]),
        )

    def down_copy(i):
        part = pl.ds(i * step, step)
        return pltpu.make_async_copy(down_hbm.at[:, part], down.at[:, part], sems.at[2, i])

    for i in range(chunks):
        for copy in copies(i):
            copy.start()
    for i in range(chunks):
        down_copy(i).start()
    gate_sum = jnp.zeros((2 * half, units), jnp.float32)
    up_sum = jnp.zeros((2 * half, units), jnp.float32)
    for i in range(chunks):
        part = pl.ds(i * step, step)
        rows = jnp.concatenate([near_ref[:, part], far_ref[:, part]], axis=0)
        gate_copy, up_copy = copies(i)
        gate_copy.wait()
        gate_sum += jnp.dot(rows, gate[part, :], preferred_element_type=jnp.float32)
        up_copy.wait()
        up_sum += jnp.dot(rows, up[part, :], preferred_element_type=jnp.float32)
    hidden = (gate_sum * jax.nn.sigmoid(gate_sum) * up_sum).astype(jnp.bfloat16)
    for i in range(chunks):
        part = pl.ds(i * step, step)
        down_copy(i).wait()
        result = jnp.dot(hidden, down[:, part], preferred_element_type=jnp.float32)
        result = result.astype(jnp.bfloat16)
        keep_ref[:, part] = result[:half, :]
        send_ref[:, part] = result[half:, :]


def body(
    tokens,
    routes,
    router_weight,
    w_gate,
    w_up,
    w_down,
    latent_pool,
    send_order,
    block_table,
    seq_lens,
    queries,
):
    device_count = lax.axis_size("ep")
    tok_rows, width = tokens.shape
    experts = router_weight.shape[1]
    top_count = routes.shape[1]
    shard_count = device_count // experts
    capacity = tok_rows * top_count // experts + tok_rows * top_count // (4 * experts)
    mine = (lax.axis_index("ep") // shard_count).astype(jnp.int32).reshape(1)

    def exchange(value, mask):
        return lax.ppermute(value, "ep", [(i, i ^ mask) for i in range(device_count)])

    packed = pl.pallas_call(
        functools.partial(pack_kernel, capacity),
        out_shape=[jax.ShapeDtypeStruct((capacity, width), jnp.bfloat16)] * experts,
        in_specs=[smem(), smem(), vmem()],
        out_specs=[vmem()] * experts,
    )(mine, routes, tokens)
    crossed = [exchange(packed[b], b * shard_count) for b in range(1, experts)]
    rows = jnp.concatenate([packed[0]] + crossed, axis=0)
    near = jnp.concatenate([rows] + [exchange(rows, m) for m in range(2, shard_count, 2)], axis=0)
    far = exchange(near, 1)

    compressed_width = LATENT_RANK + ROTARY_WIDTH
    block_ids = jnp.arange(device_count, dtype=jnp.int32)
    picks = (send_order[0][:, None] == block_ids[None, :]).astype(jnp.bfloat16)
    outgoing_blocks = jnp.dot(picks, latent_pool, preferred_element_type=jnp.float32).astype(jnp.bfloat16)
    arrived = lax.all_to_all(outgoing_blocks, "ep", split_axis=0, concat_axis=0, tiled=True)

    half = near.shape[0]
    units = w_gate.shape[1]
    chunks = 7
    keep, send = pl.pallas_call(
        functools.partial(ffn_kernel, chunks),
        out_shape=[jax.ShapeDtypeStruct((half, width), jnp.bfloat16)] * 2,
        in_specs=[vmem(), vmem()] + [pl.BlockSpec(memory_space=pltpu.HBM)] * 3,
        out_specs=[vmem(), vmem()],
        scratch_shapes=[
            pltpu.VMEM((width, units), jnp.bfloat16),
            pltpu.VMEM((width, units), jnp.bfloat16),
            pltpu.VMEM((units, width), jnp.bfloat16),
            pltpu.SemaphoreType.DMA((3, chunks)),
        ],
        compiler_params=pltpu.CompilerParams(vmem_limit_bytes=24 * 1024 * 1024),
        cost_estimate=pl.CostEstimate(
            flops=12 * half * width * units, bytes_accessed=6 * width * units, transcendentals=0
        ),
    )(near, far, w_gate, w_up, w_down)

    paired = keep.astype(jnp.float32) + exchange(send, 1).astype(jnp.float32)
    slots = experts * capacity
    paired = paired.reshape(shard_count // 2, slots, width)
    total = paired[0]
    for k in range(1, shard_count // 2):
        total = total + exchange(paired[k].astype(jnp.bfloat16), 2 * k).astype(jnp.float32)
    total = total.reshape(experts, capacity, width)
    summed = [total[0]] + [
        exchange(total[b].astype(jnp.bfloat16), b * shard_count).astype(jnp.float32)
        for b in range(1, experts)
    ]
    mixing = pl.pallas_call(
        functools.partial(mix_kernel, capacity),
        out_shape=jax.ShapeDtypeStruct((tok_rows, slots), jnp.float32),
        in_specs=[smem(), smem(), vmem(), vmem()],
        out_specs=vmem(),
    )(mine, routes, tokens, router_weight.T)
    expert_out = jnp.zeros((tok_rows, width), jnp.float32)
    for b in range(experts):
        for c in range(capacity):
            r = b * capacity + c
            expert_out = expert_out + mixing[:, r : r + 1] * summed[b][c : c + 1, :]
    expert_out = expert_out.astype(jnp.bfloat16)

    sequence_total = seq_lens.shape[0]
    span_length = device_count // sequence_total * BLOCK
    cached_latent_rows = jnp.take(arrived, block_table[0], axis=0).reshape(
        sequence_total, span_length, compressed_width
    )
    attention_head_count = queries.shape[1] // compressed_width
    query_rows = queries.reshape(sequence_total, attention_head_count, compressed_width)
    logits = (
        jnp.einsum(
            "shc,slc->shl", query_rows, cached_latent_rows, preferred_element_type=jnp.float32
        )
        * softmax_scale
    )
    visible = jnp.arange(span_length, dtype=jnp.int32)[None, None, :] < seq_lens[:, None, None]
    logits = jnp.where(visible, logits, -1e30)
    row_peak = jnp.max(logits, axis=-1, keepdims=True)
    unnormed = jnp.exp(logits - row_peak)
    routing_weight = (unnormed / jnp.sum(unnormed, axis=-1, keepdims=True)).astype(jnp.bfloat16)
    attended = jnp.einsum(
        "djp,dpz->djz",
        routing_weight,
        cached_latent_rows[:, :, :LATENT_RANK],
        preferred_element_type=jnp.float32,
    )
    attended = attended.astype(jnp.bfloat16).reshape(
        sequence_total, attention_head_count * LATENT_RANK
    )
    return (expert_out, attended)


def solution(mesh):
    return jax.shard_map(
        body,
        mesh=mesh,
        in_specs=(
            P(("groups", "ep"), None),
            P(("groups", "ep"), None),
            P(),
            P(None, "ep"),
            P(None, "ep"),
            P("ep", None),
            P(("groups", "ep"), None),
            P(("groups", "ep"), None),
            P(("groups", "ep"), None),
            P(("groups", "ep")),
            P(("groups", "ep"), None),
        ),
        out_specs=(P(("groups", "ep"), None), P(("groups", "ep"), None)),
        check_vma=False,
    )
```

time: 66.2 us -> 59.5 us (0.90)
  waiting for transfers between devices: 26.4 us -> 10.1 us
  matrix products: 11.9 us -> 1.59 us
  local copies, waits for them, and re-layouts: 6.95 us -> 15.5 us
  Pallas kernels: 0 us -> 8.02 us
  starting transfers between devices: 14.7 us -> 17.8 us
    all_to_all x2 -> x0, waiting for transfers between devices: 22.6 us -> none  [the longest x1 11.6 us: body(): lax.all_to_all(outgoing, 'ep', split_axis=0, concat_axis=0, tiled=True)]
    ppermute x0 -> x10, starting transfers between devices: none -> 13.9 us  [exchange(): lax.ppermute(value, 'ep', [(i, i ^ mask) for i in range(device_count)])]
    dot_general x5 -> x1, matrix products: 11.1 us -> 0.88 us  [body(): jnp.dot(picks, latent_pool, preferred_element_type=jnp.float32)]
    ppermute x0 -> x10, waiting for transfers between devices: none -> 10.1 us  [exchange(): lax.ppermute(value, 'ep', [(i, i ^ mask) for i in range(device_count)])]
    pallas_call x0 -> x3, Pallas kernels: none -> 8.02 us  [the longest x1 4.63 us: body(): pl.pallas_call(functools.partial(ffn_kernel, chunks), out_shape=[jax.Shap...]
    unnamed x12 -> x14, local copies, waits for them, and re-layouts: 2.05 us -> 10 us
    all_to_all x2 -> x0, starting transfers between devices: 7.28 us -> none  [the longest x1 3.72 us: body(): lax.all_to_all(partial_value, 'ep', split_axis=0, concat_axis=0, tiled=True)]
    all_to_all x1, waiting for transfers between devices: 3.75 us -> 0.01 us  [body(): lax.all_to_all(outgoing_blocks, 'ep', split_axis=0, concat_axis=0, tiled=...]
  transfers between devices with their start and end apart: 3 -> 11, of which waited for: 3 -> 8; matrix products, arithmetic and copies ran while one was open for 12% -> 23% of each run, Pallas kernels for 0% -> 3%
where the time goes in v1:
time: 59.5 us; the launch traced here: 58.9 us
  starting transfers between devices  17.8 us (30%)
  local copies, waits for them, and re-layouts  15.5 us (26%)
  waiting for transfers between devices  10.1 us (17%)
  Pallas kernels  8.02 us (13%)
  other arithmetic  5.15 us (9%)
  matrix products  1.59 us (3%)
  between operations  0.8 us (1%)
    ppermute x10, starting transfers between devices, exchange(): lax.ppermute(value, 'ep', [(i, i ^ mask) for i in range(device_count)])  13.9 us
    ppermute x10, waiting for transfers between devices, exchange(): lax.ppermute(value, 'ep', [(i, i ^ mask) for i in range(device_count)])  10.1 us
    unnamed x14, local copies, waits for them, and re-layouts  10 us
    pallas_call x1, Pallas kernels, body(): pl.pallas_call(functools.partial(ffn_kernel, chunks), out_shape=[jax.Shap...  4.63 us
    all_to_all x1, starting transfers between devices, body(): lax.all_to_all(outgoing_blocks, 'ep', split_axis=0, concat_axis=0, tiled=...  3.89 us
    pallas_call x1, Pallas kernels, body(): pl.pallas_call(functools.partial(mix_kernel, capacity), out_shape=jax.Sha...  1.79 us
    reshape x1, local copies, waits for them, and re-layouts, body(): queries.reshape(sequence_total, attention_head_count, compressed_width)  1.74 us
    pallas_call x1, Pallas kernels, body(): pl.pallas_call(functools.partial(pack_kernel, capacity), out_shape=[jax.S...  1.6 us
  transfers between devices with their start and end apart: 11, of which 8 were waited for; matrix products, arithmetic and copies ran while one was open for 23% of the time, Pallas kernels for 3%

profile of v1, /device:TPU:0, one launch (start us, length us, event | category | flops | bytes accessed | tf_op | source)
XLA Modules:
  0.0 58.9 jit_solution(7947879824720135280)
XLA Ops:
  0.7 1.3 %copy.23.routes_ref = s32[4,1]{1,0:T(4,128)} copy(s32[4,1]{0,1:T(1,128)} %param.12) | data formatting | bytes 32 | tf_op args[1]
  2.0 1.6 %shard_map.123 = (bf16[2,7168]{1,0:T(2,128)(2,1)}, bf16[2,7168]{1,0:T(2,128)(2,1)}) custom-call(s32[1]{0:T(128)} %bitcast.mine_ref, s32[4,1]{1,0:T(4,128)} %copy.23.routes_ref, bf16[4,7168]{1,0:T(4,128)(2,1)} %tokens_ref.3), custom_call_target="tpu_custom_call" | custom-call | tf_op jit(solution)/shard_map/pallas_call | solution.py:159
  3.6 4.1 %collective-permute-start = (bf16[2,7168]{1,0:T(2,128)(2,1)}, bf16[2,7168]{1,0:T(2,128)(2,1)S(1)}, u32[]{:S(2)}, u32[]{:S(2)}) collective-permute-start(bf16[2,7168]{1,0:T(2,128)(2,1)} %get-tuple-element.7), channel_id=1, source_target_pairs={{0,8},{1,9},{2,10},{3,11},{4,12},{5,13},{6,14},{7,15},{8,0},{9,1},... | collective-permute-start | bytes 86024 | tf_op jit(solution)/shard_map/ppermute | solution.py:157
  7.7 0.9 %fusion.1 = bf16[16,1,4608]{2,0,1:T(8,128)(2,1)S(1)} fusion(bf16[16,4608]{1,0:T(8,128)(2,1)S(1)} %copy-done, s32[16]{0:T(128)} %bitcast.33), kind=kOutput, calls=%fused_computation.3 | convolution fusion | flops 2433280 | bytes 294976 | tf_op jit(solution)/shard_map/dot_general | solution.py:173
  10.5 3.9 %all-to-all-start = ((bf16[16,2,2304]{2,1,0:T(2,128)(2,1)}), bf16[16,2,2304]{2,1,0:T(2,128)(2,1)S(1)}, u32[]{:S(2)}, u32[]{:S(2)}) async-start(bf16[16,2,2304]{2,1,0:T(2,128)(2,1)} %reshape.117), calls=%async_computation | async-start | bytes 294912 | tf_op jit(solution)/shard_map/all_to_all | solution.py:174
  14.3 1.8 %shard_map.122 = f32[4,4]{1,0:T(4,128)} custom-call(s32[1]{0:T(128)} %bitcast.mine_ref, s32[4,1]{1,0:T(4,128)} %copy.23.routes_ref, bf16[4,7168]{1,0:T(4,128)(2,1)} %tokens_ref.3, bf16[2,7168]{1,0:T(2,128)(2,1)} %bitcast.32), custom_call_target="tpu_custom_call" | custom-call | tf_op jit(solution)/shard_map/pallas_call | solution.py:207
  17.3 1.3 %reduce.11 = s32[16]{0:T(128)S(1)} reduce(s32[1,16]{1,0:T(1,128)} %param.19, s32[]{:T(128)} %broadcast.71), dimensions={0}, to_apply=%param.19.reduce_sub_computation.3 | reduce | bytes 132 | tf_op args[8]
  19.4 1.0 %slice_reduce_fusion.3 = (f32[4]{0:T(128)S(1)}, f32[4]{0:T(128)S(1)}, f32[4]{0:T(128)S(1)}, f32[4]{0:T(128)S(1)}) fusion(f32[4,4]{1,0:T(4,128)} %shard_map.122), kind=kLoop, calls=%fused_computation.32 | loop fusion | bytes 128 | tf_op jit(solution)/shard_map/slice | solution.py:217
  20.6 1.7 %reshape.94 = bf16[4,128,576]{2,1,0:T(8,128)(2,1)S(1)} reshape(bf16[4,73728]{1,0:T(4,128)(2,1)} %param.21) | data formatting | bytes 1179648 | tf_op jit(solution)/shard_map/reshape | solution.py:226
  23.2 2.0 %collective-permute-start.1 = (bf16[4,7168]{1,0:T(4,128)(2,1)S(1)}, bf16[4,7168]{1,0:T(4,128)(2,1)S(1)}, u32[]{:S(2)}, u32[]{:S(2)}) collective-permute-start(bf16[4,7168]{1,0:T(4,128)(2,1)S(1)} %pad_maximum_fusion), channel_id=1, source_target_pairs={{0,2},{1,3},{2,0},{3,1},{4,6},{5,7},{6,4},{7,5},{8,10},{9,11},{10,... | collective-permute-start | bytes 172040 | tf_op jit(solution)/shard_map/ppermute | solution.py:157
  25.2 1.5 %collective-permute-start.2 = (bf16[4,7168]{1,0:T(4,128)(2,1)S(1)}, bf16[4,7168]{1,0:T(4,128)(2,1)S(1)}, u32[]{:S(2)}, u32[]{:S(2)}) collective-permute-start(bf16[4,7168]{1,0:T(4,128)(2,1)S(1)} %pad_maximum_fusion), channel_id=1, source_target_pairs={{0,4},{1,5},{2,6},{3,7},{4,0},{5,1},{6,2},{7,3},{8,12},{9,13},{10,... | collective-permute-start | bytes 172040 | tf_op jit(solution)/shard_map/ppermute | solution.py:157
  27.5 2.4 %collective-permute-done.2 = bf16[4,7168]{1,0:T(4,128)(2,1)S(1)} collective-permute-done((bf16[4,7168]{1,0:T(4,128)(2,1)S(1)}, bf16[4,7168]{1,0:T(4,128)(2,1)S(1)}, u32[]{:S(2)}, u32[]{:S(2)}) %collective-permute-start.2) | collective-permute-done | bytes 57376 | tf_op jit(solution)/shard_map/ppermute | solution.py:157
  29.9 1.8 %collective-permute-done.3 = bf16[4,7168]{1,0:T(4,128)(2,1)S(1)} collective-permute-done((bf16[4,7168]{1,0:T(4,128)(2,1)S(1)}, bf16[4,7168]{1,0:T(4,128)(2,1)S(1)}, u32[]{:S(2)}, u32[]{:S(2)}) %collective-permute-start.3) | collective-permute-done | bytes 57376 | tf_op jit(solution)/shard_map/ppermute | solution.py:157
  31.7 0.9 %concatenate.8.near_ref = bf16[16,7168]{1,0:T(8,128)(2,1)S(1)} concatenate(bf16[2,7168]{1,0:T(2,128)(2,1)} %get-tuple-element.6, bf16[2,7168]{1,0:T(2,128)(2,1)S(1)} %collective-permute-done, bf16[4,7168]{1,0:T(4,128)(2,1)S(1)} %collective-permute-done.1, bf16[4,7168]{1,0:T(4,128)(2,1)S(1)} %collective-permute-done.2, bf16[4,7168]{1,0:T(4,128)(2,1)S(1)} %collective-permute-done.3), dimensions={0} | concatenate | bytes 458752 | tf_op jit(solution)/shard_map/concatenate | solution.py:167
  34.2 2.0 %copy-done.1 = bf16[7168,256]{1,0:T(8,128)(2,1)S(1)} copy-done((bf16[7168,256]{1,0:T(8,128)(2,1)S(1)}, bf16[7168,256]{1,0:T(8,128)(2,1)}, u32[]{:S(2)}) %copy-start.1) | copy-done | bytes 3670040
  36.3 2.0 %copy-done.2 = bf16[7168,256]{1,0:T(8,128)(2,1)S(1)} copy-done((bf16[7168,256]{1,0:T(8,128)(2,1)S(1)}, bf16[7168,256]{1,0:T(8,128)(2,1)}, u32[]{:S(2)}) %copy-start.2) | copy-done | bytes 3670040
  38.3 2.0 %copy-done.3 = bf16[256,7168]{1,0:T(8,128)(2,1)S(1)} copy-done((bf16[256,7168]{1,0:T(8,128)(2,1)S(1)}, bf16[256,7168]{1,0:T(8,128)(2,1)}, u32[]{:S(2)}) %copy-start.3) | copy-done | bytes 3670040
  40.4 4.6 %shard_map.124 = (bf16[16,7168]{1,0:T(8,128)(2,1)S(1)}, bf16[16,7168]{1,0:T(8,128)(2,1)S(1)}) custom-call(bf16[16,7168]{1,0:T(8,128)(2,1)S(1)} %concatenate.8.near_ref, bf16[16,7168]{1,0:T(8,128)(2,1)S(1)} %collective-permute-done.4.far_ref, bf16[7168,256]{1,0:T(8,128)(2,1)S(1)} %copy-done.1, bf16[7168,256]{1,0:T(8,128)(2,1)S(1)} %copy-done.2, ...), custom_call_target="tpu_custom_call" | custom-call | flops 352321536 | bytes 11010048 | tf_op jit(solution)/shard_map/pallas_call | solution.py:179
  45.6 1.0 %collective-permute-done.5 = bf16[16,7168]{1,0:T(8,128)(2,1)S(1)} collective-permute-done((bf16[16,7168]{1,0:T(8,128)(2,1)S(1)}, bf16[16,7168]{1,0:T(8,128)(2,1)S(1)}, u32[]{:S(2)}, u32[]{:S(2)}) %collective-permute-start.5) | collective-permute-done | bytes 229408 | tf_op jit(solution)/shard_map/ppermute | solution.py:157
  48.0 2.2 %collective-permute-start.8 = (bf16[4,7168]{1,0:T(4,128)(2,1)S(1)}, bf16[4,7168]{1,0:T(4,128)(2,1)S(1)}, u32[]{:S(2)}, u32[]{:S(2)}) collective-permute-start(bf16[4,7168]{1,0:T(4,128)(2,1)S(1)} %get-tuple-element.17), channel_id=1, source_target_pairs={{0,6},{1,7},{2,4},{3,5},{4,2},{5,3},{6,0},{7,1},{8,14},{9,15},{10,... | collective-permute-start | bytes 172040 | tf_op jit(solution)/shard_map/ppermute | solution.py:157
  50.6 1.2 %copy.29 = bf16[1,4,128,512]{3,1,2,0:T(4,128)(2,1)} copy(bf16[1,4,128,512]{3,2,1,0:T(8,128)(2,1)S(1)} %fusion.2) | data formatting | bytes 1048576
  52.0 1.1 %collective-permute-done.8 = bf16[4,7168]{1,0:T(4,128)(2,1)S(1)} collective-permute-done((bf16[4,7168]{1,0:T(4,128)(2,1)S(1)}, bf16[4,7168]{1,0:T(4,128)(2,1)S(1)}, u32[]{:S(2)}, u32[]{:S(2)}) %collective-permute-start.8) | collective-permute-done | bytes 57376 | tf_op jit(solution)/shard_map/ppermute | solution.py:157
  53.2 2.4 %collective-permute-start.9 = (bf16[2,7168]{1,0:T(2,128)(2,1)S(1)}, bf16[2,7168]{1,0:T(2,128)(2,1)S(1)}, u32[]{:S(2)}, u32[]{:S(2)}) collective-permute-start(bf16[2,7168]{1,0:T(2,128)(2,1)S(1)} %slice.94), channel_id=1, source_target_pairs={{0,8},{1,9},{2,10},{3,11},{4,12},{5,13},{6,14},{7,15},{8,0},{9,1},... | collective-permute-start | bytes 86024 | tf_op jit(solution)/shard_map/ppermute | solution.py:157
  55.7 2.4 %collective-permute-done.9 = bf16[2,7168]{1,0:T(2,128)(2,1)S(1)} collective-permute-done((bf16[2,7168]{1,0:T(2,128)(2,1)S(1)}, bf16[2,7168]{1,0:T(2,128)(2,1)S(1)}, u32[]{:S(2)}, u32[]{:S(2)}) %collective-permute-start.9) | collective-permute-done | bytes 28704 | tf_op jit(solution)/shard_map/ppermute | solution.py:157
  (42 shorter events, 10.8 us)
Async XLA Ops:
  0.6 7.0 %copy-start = (bf16[16,4608]{1,0:T(8,128)(2,1)S(1)}, bf16[16,4608]{1,0:T(8,128)(2,1)}, u32[]{:S(2)}) copy-start(bf16[16,4608]{1,0:T(8,128)(2,1)} %param.17) | copy-start | bytes 442372
  3.6 18.8 %collective-permute-start = (bf16[2,7168]{1,0:T(2,128)(2,1)}, bf16[2,7168]{1,0:T(2,128)(2,1)S(1)}, u32[]{:S(2)}, u32[]{:S(2)}) collective-permute-start(bf16[2,7168]{1,0:T(2,128)(2,1)} %get-tuple-element.7), channel_id=1, source_target_pairs={{0,8},{1,9},{2,10},{3,11},{4,12},{5,13},{6,14},{7,15},{8,0},{9,1},... | collective-permute-start | bytes 86024 | tf_op jit(solution)/shard_map/ppermute | solution.py:157
  10.5 22.3 %all-to-all-start = ((bf16[16,2,2304]{2,1,0:T(2,128)(2,1)}), bf16[16,2,2304]{2,1,0:T(2,128)(2,1)S(1)}, u32[]{:S(2)}, u32[]{:S(2)}) async-start(bf16[16,2,2304]{2,1,0:T(2,128)(2,1)} %reshape.117), calls=%async_computation | async-start | bytes 294912 | tf_op jit(solution)/shard_map/all_to_all | solution.py:174
  23.2 4.3 %collective-permute-start.1 = (bf16[4,7168]{1,0:T(4,128)(2,1)S(1)}, bf16[4,7168]{1,0:T(4,128)(2,1)S(1)}, u32[]{:S(2)}, u32[]{:S(2)}) collective-permute-start(bf16[4,7168]{1,0:T(4,128)(2,1)S(1)} %pad_maximum_fusion), channel_id=1, source_target_pairs={{0,2},{1,3},{2,0},{3,1},{4,6},{5,7},{6,4},{7,5},{8,10},{9,11},{10,... | collective-permute-start | bytes 172040 | tf_op jit(solution)/shard_map/ppermute | solution.py:157
  25.2 4.7 %collective-permute-start.2 = (bf16[4,7168]{1,0:T(4,128)(2,1)S(1)}, bf16[4,7168]{1,0:T(4,128)(2,1)S(1)}, u32[]{:S(2)}, u32[]{:S(2)}) collective-permute-start(bf16[4,7168]{1,0:T(4,128)(2,1)S(1)} %pad_maximum_fusion), channel_id=1, source_target_pairs={{0,4},{1,5},{2,6},{3,7},{4,0},{5,1},{6,2},{7,3},{8,12},{9,13},{10,... | collective-permute-start | bytes 172040 | tf_op jit(solution)/shard_map/ppermute | solution.py:157
  26.7 5.1 %collective-permute-start.3 = (bf16[4,7168]{1,0:T(4,128)(2,1)S(1)}, bf16[4,7168]{1,0:T(4,128)(2,1)S(1)}, u32[]{:S(2)}, u32[]{:S(2)}) collective-permute-start(bf16[4,7168]{1,0:T(4,128)(2,1)S(1)} %pad_maximum_fusion), channel_id=1, source_target_pairs={{0,6},{1,7},{2,4},{3,5},{4,2},{5,3},{6,0},{7,1},{8,14},{9,15},{10,... | collective-permute-start | bytes 172040 | tf_op jit(solution)/shard_map/ppermute | solution.py:157
  32.7 1.6 %collective-permute-start.4 = (bf16[16,7168]{1,0:T(8,128)(2,1)S(1)}, bf16[16,7168]{1,0:T(8,128)(2,1)S(1)}, u32[]{:S(2)}, u32[]{:S(2)}) collective-permute-start(bf16[16,7168]{1,0:T(8,128)(2,1)S(1)} %concatenate.8.near_ref), channel_id=1, source_target_pairs={{0,1},{1,0},{2,3},{3,2},{4,5},{5,4},{6,7},{7,6},{8,9},{9,8},{10,11... | collective-permute-start | bytes 688136 | tf_op jit(solution)/shard_map/ppermute | solution.py:157
  34.2 2.0 %copy-start.1 = (bf16[7168,256]{1,0:T(8,128)(2,1)S(1)}, bf16[7168,256]{1,0:T(8,128)(2,1)}, u32[]{:S(2)}) copy-start(bf16[7168,256]{1,0:T(8,128)(2,1)} %gate_hbm.1) | copy-start | bytes 11010052
  36.3 2.0 %copy-start.2 = (bf16[7168,256]{1,0:T(8,128)(2,1)S(1)}, bf16[7168,256]{1,0:T(8,128)(2,1)}, u32[]{:S(2)}) copy-start(bf16[7168,256]{1,0:T(8,128)(2,1)} %up_hbm.1) | copy-start | bytes 11010052
  38.3 2.0 %copy-start.3 = (bf16[256,7168]{1,0:T(8,128)(2,1)S(1)}, bf16[256,7168]{1,0:T(8,128)(2,1)}, u32[]{:S(2)}) copy-start(bf16[256,7168]{1,0:T(8,128)(2,1)} %down_hbm.1) | copy-start | bytes 11010052
  45.0 1.6 %collective-permute-start.5 = (bf16[16,7168]{1,0:T(8,128)(2,1)S(1)}, bf16[16,7168]{1,0:T(8,128)(2,1)S(1)}, u32[]{:S(2)}, u32[]{:S(2)}) collective-permute-start(bf16[16,7168]{1,0:T(8,128)(2,1)S(1)} %get-tuple-element.9), channel_id=1, source_target_pairs={{0,1},{1,0},{2,3},{3,2},{4,5},{5,4},{6,7},{7,6},{8,9},{9,8},{10,11... | collective-permute-start | bytes 688136 | tf_op jit(solution)/shard_map/ppermute | solution.py:157
  46.7 5.1 %collective-permute-start.6 = (bf16[4,7168]{1,0:T(4,128)(2,1)S(1)}, bf16[4,7168]{1,0:T(4,128)(2,1)S(1)}, u32[]{:S(2)}, u32[]{:S(2)}) collective-permute-start(bf16[4,7168]{1,0:T(4,128)(2,1)S(1)} %get-tuple-element.16), channel_id=1, source_target_pairs={{0,2},{1,3},{2,0},{3,1},{4,6},{5,7},{6,4},{7,5},{8,10},{9,11},{10,... | collective-permute-start | bytes 172040 | tf_op jit(solution)/shard_map/ppermute | solution.py:157
  47.3 4.7 %collective-permute-start.7 = (bf16[4,7168]{1,0:T(4,128)(2,1)S(1)}, bf16[4,7168]{1,0:T(4,128)(2,1)S(1)}, u32[]{:S(2)}, u32[]{:S(2)}) collective-permute-start(bf16[4,7168]{1,0:T(4,128)(2,1)S(1)} %get-tuple-element.18), channel_id=1, source_target_pairs={{0,4},{1,5},{2,6},{3,7},{4,0},{5,1},{6,2},{7,3},{8,12},{9,13},{10,... | collective-permute-start | bytes 172040 | tf_op jit(solution)/shard_map/ppermute | solution.py:157
  48.0 5.1 %collective-permute-start.8 = (bf16[4,7168]{1,0:T(4,128)(2,1)S(1)}, bf16[4,7168]{1,0:T(4,128)(2,1)S(1)}, u32[]{:S(2)}, u32[]{:S(2)}) collective-permute-start(bf16[4,7168]{1,0:T(4,128)(2,1)S(1)} %get-tuple-element.17), channel_id=1, source_target_pairs={{0,6},{1,7},{2,4},{3,5},{4,2},{5,3},{6,0},{7,1},{8,14},{9,15},{10,... | collective-permute-start | bytes 172040 | tf_op jit(solution)/shard_map/ppermute | solution.py:157
  53.2 4.8 %collective-permute-start.9 = (bf16[2,7168]{1,0:T(2,128)(2,1)S(1)}, bf16[2,7168]{1,0:T(2,128)(2,1)S(1)}, u32[]{:S(2)}, u32[]{:S(2)}) collective-permute-start(bf16[2,7168]{1,0:T(2,128)(2,1)S(1)} %slice.94), channel_id=1, source_target_pairs={{0,8},{1,9},{2,10},{3,11},{4,12},{5,13},{6,14},{7,15},{8,0},{9,1},... | collective-permute-start | bytes 86024 | tf_op jit(solution)/shard_map/ppermute | solution.py:157

commit v2 on v1

--- a/solution.py
+++ b/solution.py
@@ -7,6 +7,7 @@
 from jax.experimental.pallas import tpu as pltpu
 from jax.sharding import PartitionSpec as P
 
+
 LATENT_RANK = 512
 ROTARY_WIDTH = 64
 BLOCK = 8
@@ -24,8 +25,12 @@
     return pl.BlockSpec(memory_space=pltpu.SMEM)
 
 
+def in_hbm(value):
+    return pltpu.with_memory_space_constraint(value, pltpu.HBM)
+
+
 def placements(routes_ref, mine, blocks, caps, axis):
-    tok_rows, top = routes_ref.shape
+    top, tok_rows = routes_ref.shape
     shape = (blocks * caps, 128) if axis == 0 else (tok_rows, blocks * caps)
     row = lax.broadcasted_iota(jnp.int32, shape, axis)
     expert = (row // caps) ^ mine
@@ -33,9 +38,9 @@
     count = jnp.zeros(shape, jnp.int32)
     out = []
     for t in range(tok_rows):
-        hit = expert == routes_ref[t, 0]
+        hit = expert == routes_ref[0, t]
         for j in range(1, top):
-            hit = hit | (expert == routes_ref[t, j])
+            hit = hit | (expert == routes_ref[j, t])
         out.append(hit & (count == slot))
         count = count + hit.astype(jnp.int32)
     return out
@@ -55,7 +60,7 @@
 
 
 def mix_kernel(caps, mine_ref, routes_ref, tokens_ref, centroids_ref, out_ref):
-    tok_rows, top = routes_ref.shape
+    top, tok_rows = routes_ref.shape
     experts = centroids_ref.shape[0]
     mine = mine_ref[0]
     scores = jax.nn.sigmoid(
@@ -71,7 +76,7 @@
     chosen = jnp.zeros((tok_rows, experts), jnp.float32)
     for t in range(tok_rows):
         for j in range(top):
-            hit = (token == t) & (expert == routes_ref[t, j])
+            hit = (token == t) & (expert == routes_ref[j, t])
             chosen = jnp.where(hit, chosen + 1.0, chosen)
     weighted = scores * chosen
     share = route_scale * weighted / jnp.sum(weighted, axis=-1, keepdims=True)
@@ -87,6 +92,59 @@
     for t, hit in enumerate(placed):
         mixing = jnp.where((row_token == t) & hit, row_share, mixing)
     out_ref[...] = mixing
+
+
+def outgoing_kernel(order_ref, pool_ref, out_ref):
+    count, _, half = out_ref.shape
+    blocks = pool_ref.shape[0]
+    row = lax.broadcasted_iota(jnp.int32, (2 * count, blocks), 0)
+    block = lax.broadcasted_iota(jnp.int32, (2 * count, blocks), 1)
+    wanted = jnp.zeros((2 * count, blocks), jnp.int32)
+    for d in range(count):
+        wanted = jnp.where(row // 2 == d, order_ref[0, d], wanted)
+    hit = block == wanted
+    result = jnp.zeros((2 * count, half), jnp.float32)
+    for r in range(2):
+        picks = jnp.where(hit & (row % 2 == r), 1.0, 0.0).astype(jnp.bfloat16)
+        result = result + jnp.dot(
+            picks, pool_ref[:, r * half : (r + 1) * half], preferred_element_type=jnp.float32
+        )
+    result = result.astype(jnp.bfloat16)
+    for d in range(count):
+        out_ref[d] = result[2 * d : 2 * d + 2, :]
+
+
+def attention_kernel(table_ref, lens_ref, queries_ref, arrived_ref, out_ref):
+    sequences, _, entries = queries_ref.shape
+    rows = arrived_ref.shape[0]
+    per_row = BLOCK // 2
+    per_sequence = rows // 2 // sequences
+    arrived = arrived_ref[...]
+    cache = jnp.concatenate(
+        [arrived[:, i * entries : (i + 1) * entries] for i in range(per_row)], axis=0
+    )
+    keys = cache.shape[0]
+    key = lax.broadcasted_iota(jnp.int32, (1, keys), 1)
+    source = (key % rows) // 2
+    token = (key % 2) * per_row + key // rows
+    for s in range(sequences):
+        position = jnp.full((1, keys), per_sequence * BLOCK, jnp.int32)
+        for b in range(per_sequence):
+            position = jnp.where(
+                source == table_ref[0, s * per_sequence + b], b * BLOCK + token, position
+            )
+        visible = position < lens_ref[s]
+        logits = lax.dot_general(
+            queries_ref[s], cache, (((1,), (1,)), ((), ())), preferred_element_type=jnp.float32
+        )
+        logits = jnp.where(visible, logits * softmax_scale, -1e30)
+        peak = jnp.max(logits, axis=-1, keepdims=True)
+        unnormed = jnp.exp(logits - peak)
+        unnormed = jnp.where(visible, unnormed, 0.0)
+        weights = (unnormed / jnp.sum(unnormed, axis=-1, keepdims=True)).astype(jnp.bfloat16)
+        out_ref[s] = jnp.dot(
+            weights, cache[:, :LATENT_RANK], preferred_element_type=jnp.float32
+        ).astype(jnp.bfloat16)
 
 
 def ffn_kernel(
@@ -132,7 +190,7 @@
         send_ref[:, part] = result[half:, :]
 
 
-def body(
+def layer(
     tokens,
     routes,
     router_weight,
@@ -156,30 +214,46 @@
     def exchange(value, mask):
         return lax.ppermute(value, "ep", [(i, i ^ mask) for i in range(device_count)])
 
-    packed = pl.pallas_call(
+    def kernel(body, **options):
+        def call(*operands):
+            return pl.pallas_call(body, **options)(*operands)
+
+        return call
+
+    small = pltpu.CompilerParams(vmem_limit_bytes=8 * 1024 * 1024)
+    routes = routes.T
+
+    packed = kernel(
         functools.partial(pack_kernel, capacity),
         out_shape=[jax.ShapeDtypeStruct((capacity, width), jnp.bfloat16)] * experts,
         in_specs=[smem(), smem(), vmem()],
         out_specs=[vmem()] * experts,
-    )(mine, routes, tokens)
+        compiler_params=small,
+    )(mine, in_hbm(routes), in_hbm(tokens))
     crossed = [exchange(packed[b], b * shard_count) for b in range(1, experts)]
     rows = jnp.concatenate([packed[0]] + crossed, axis=0)
-    near = jnp.concatenate([rows] + [exchange(rows, m) for m in range(2, shard_count, 2)], axis=0)
+    spread = [exchange(rows, m) for m in range(2, shard_count, 2)]
+    near = jnp.concatenate([rows] + spread, axis=0)
     far = exchange(near, 1)
 
     compressed_width = LATENT_RANK + ROTARY_WIDTH
-    block_ids = jnp.arange(device_count, dtype=jnp.int32)
-    picks = (send_order[0][:, None] == block_ids[None, :]).astype(jnp.bfloat16)
-    outgoing_blocks = jnp.dot(picks, latent_pool, preferred_element_type=jnp.float32).astype(jnp.bfloat16)
-    arrived = lax.all_to_all(outgoing_blocks, "ep", split_axis=0, concat_axis=0, tiled=True)
+    half_block = latent_pool.shape[1] // 2
+    outgoing = kernel(
+        outgoing_kernel,
+        out_shape=jax.ShapeDtypeStruct((device_count, 2, half_block), jnp.bfloat16),
+        in_specs=[smem(), vmem()],
+        out_specs=vmem(),
+        compiler_params=small,
+    )(in_hbm(send_order), in_hbm(latent_pool))
+    arrived = lax.all_to_all(outgoing, "ep", split_axis=0, concat_axis=0, tiled=True)
 
     half = near.shape[0]
     units = w_gate.shape[1]
     chunks = 7
-    keep, send = pl.pallas_call(
+    keep, send = kernel(
         functools.partial(ffn_kernel, chunks),
         out_shape=[jax.ShapeDtypeStruct((half, width), jnp.bfloat16)] * 2,
-        in_specs=[vmem(), vmem()] + [pl.BlockSpec(memory_space=pltpu.HBM)] * 3,
+        in_specs=[vmem(), vmem()] + [pl.BlockSpec(memory_space=pl.ANY)] * 3,
         out_specs=[vmem(), vmem()],
         scratch_shapes=[
             pltpu.VMEM((width, units), jnp.bfloat16),
@@ -187,7 +261,7 @@
             pltpu.VMEM((units, width), jnp.bfloat16),
             pltpu.SemaphoreType.DMA((3, chunks)),
         ],
-        compiler_params=pltpu.CompilerParams(vmem_limit_bytes=24 * 1024 * 1024),
+        compiler_params=pltpu.CompilerParams(vmem_limit_bytes=54000000),
         cost_estimate=pl.CostEstimate(
             flops=12 * half * width * units, bytes_accessed=6 * width * units, transcendentals=0
         ),
@@ -204,12 +278,13 @@
         exchange(total[b].astype(jnp.bfloat16), b * shard_count).astype(jnp.float32)
         for b in range(1, experts)
     ]
-    mixing = pl.pallas_call(
+    mixing = kernel(
         functools.partial(mix_kernel, capacity),
         out_shape=jax.ShapeDtypeStruct((tok_rows, slots), jnp.float32),
         in_specs=[smem(), smem(), vmem(), vmem()],
         out_specs=vmem(),
-    )(mine, routes, tokens, router_weight.T)
+        compiler_params=small,
+    )(mine, in_hbm(routes), in_hbm(tokens), in_hbm(router_weight.T))
     expert_out = jnp.zeros((tok_rows, width), jnp.float32)
     for b in range(experts):
         for c in range(capacity):
@@ -218,38 +293,24 @@
     expert_out = expert_out.astype(jnp.bfloat16)
 
     sequence_total = seq_lens.shape[0]
-    span_length = device_count // sequence_total * BLOCK
-    cached_latent_rows = jnp.take(arrived, block_table[0], axis=0).reshape(
-        sequence_total, span_length, compressed_width
-    )
     attention_head_count = queries.shape[1] // compressed_width
     query_rows = queries.reshape(sequence_total, attention_head_count, compressed_width)
-    logits = (
-        jnp.einsum(
-            "shc,slc->shl", query_rows, cached_latent_rows, preferred_element_type=jnp.float32
-        )
-        * softmax_scale
-    )
-    visible = jnp.arange(span_length, dtype=jnp.int32)[None, None, :] < seq_lens[:, None, None]
-    logits = jnp.where(visible, logits, -1e30)
-    row_peak = jnp.max(logits, axis=-1, keepdims=True)
-    unnormed = jnp.exp(logits - row_peak)
-    routing_weight = (unnormed / jnp.sum(unnormed, axis=-1, keepdims=True)).astype(jnp.bfloat16)
-    attended = jnp.einsum(
-        "djp,dpz->djz",
-        routing_weight,
-        cached_latent_rows[:, :, :LATENT_RANK],
-        preferred_element_type=jnp.float32,
-    )
-    attended = attended.astype(jnp.bfloat16).reshape(
-        sequence_total, attention_head_count * LATENT_RANK
-    )
+    attended = kernel(
+        attention_kernel,
+        out_shape=jax.ShapeDtypeStruct(
+            (sequence_total, attention_head_count, LATENT_RANK), jnp.bfloat16
+        ),
+        in_specs=[smem(), smem(), vmem(), vmem()],
+        out_specs=vmem(),
+        compiler_params=pltpu.CompilerParams(vmem_limit_bytes=32 * 1024 * 1024),
+    )(block_table, seq_lens, query_rows, arrived.reshape(2 * device_count, half_block))
+    attended = attended.reshape(sequence_total, attention_head_count * LATENT_RANK)
     return (expert_out, attended)
 
 
 def solution(mesh):
     return jax.shard_map(
-        body,
+        layer,
         mesh=mesh,
         in_specs=(
             P(("groups", "ep"), None),

time: 59.5 us -> 47.1 us (0.79)
  local copies, waits for them, and re-layouts: 15.5 us -> 2.54 us
  other arithmetic: 5.15 us -> 0.93 us
  waiting for transfers between devices: 10.1 us -> 14.1 us
  Pallas kernels: 8.02 us -> 11.4 us
  matrix products: 1.59 us -> 0 us
  starting transfers between devices: 17.8 us -> 17 us
    unnamed x14 -> x7, local copies, waits for them, and re-layouts: 10 us -> 1.22 us
    pallas_call x3 -> x5, Pallas kernels: 8.02 us -> 11.4 us  [call(): return pl.pallas_call(body, **options)(*operands)]
    all_to_all x1, waiting for transfers between devices: 0.01 us -> 2.34 us  [layer(): lax.all_to_all(outgoing, 'ep', split_axis=0, concat_axis=0, tiled=True)]
    ppermute x10, starting transfers between devices: 13.9 us -> 12.1 us  [exchange(): lax.ppermute(value, 'ep', [(i, i ^ mask) for i in range(device_count)])]
    ppermute x10, waiting for transfers between devices: 10.1 us -> 11.7 us  [exchange(): lax.ppermute(value, 'ep', [(i, i ^ mask) for i in range(device_count)])]
    unnamed x1 -> x0, other arithmetic: 1.28 us -> none
    dot_general x2 -> x0, matrix products: 1.22 us -> none  [the longest x1 0.88 us: body(): jnp.dot(picks, latent_pool, preferred_element_type=jnp.float32)]
    all_to_all x1, starting transfers between devices: 3.89 us -> 4.98 us  [layer(): lax.all_to_all(outgoing, 'ep', split_axis=0, concat_axis=0, tiled=True)]
  transfers between devices with their start and end apart: 11 -> 11, of which waited for: 8 -> 7; matrix products, arithmetic and copies ran while one was open for 23% -> 5% of each run, Pallas kernels for 3% -> 11%
where the time goes in v2:
time: 47.1 us; the launch traced here: 46.8 us
  starting transfers between devices  17 us (36%)
  waiting for transfers between devices  14.1 us (30%)
  Pallas kernels  11.4 us (24%)
  local copies, waits for them, and re-layouts  2.54 us (5%)
  other arithmetic  0.93 us (2%)
  between operations  0.81 us (2%)
    ppermute x10, starting transfers between devices, exchange(): lax.ppermute(value, 'ep', [(i, i ^ mask) for i in range(device_count)])  12.1 us
    ppermute x10, waiting for transfers between devices, exchange(): lax.ppermute(value, 'ep', [(i, i ^ mask) for i in range(device_count)])  11.7 us
    pallas_call x5, Pallas kernels, call(): return pl.pallas_call(body, **options)(*operands)  11.4 us
    all_to_all x1, starting transfers between devices, layer(): lax.all_to_all(outgoing, 'ep', split_axis=0, concat_axis=0, tiled=True)  4.98 us
    all_to_all x1, waiting for transfers between devices, layer(): lax.all_to_all(outgoing, 'ep', split_axis=0, concat_axis=0, tiled=True)  2.34 us
    unnamed x7, local copies, waits for them, and re-layouts  1.22 us
  transfers between devices with their start and end apart: 11, of which 7 were waited for; matrix products, arithmetic and copies ran while one was open for 5% of the time, Pallas kernels for 11%

profile of v2, /device:TPU:0, one launch (start us, length us, event | category | flops | bytes accessed | tf_op | source)
XLA Modules:
  0.0 46.8 jit_solution(17216288421942869471)
XLA Ops:
  0.6 1.0 %shard_map.123 = (bf16[2,7168]{1,0:T(2,128)(2,1)S(1)}, bf16[2,7168]{1,0:T(2,128)(2,1)S(1)}) custom-call(s32[1]{0:T(128)} %bitcast.mine_ref, s32[1,4]{1,0:T(1,128)} %bitcast.16, bf16[4,7168]{1,0:T(4,128)(2,1)} %tokens_ref.3), custom_call_target="tpu_custom_call" | custom-call | tf_op jit(solution)/shard_map/pallas_call | solution.py:219
  1.6 4.1 %collective-permute-start = (bf16[2,7168]{1,0:T(2,128)(2,1)S(1)}, bf16[2,7168]{1,0:T(2,128)(2,1)S(1)}, u32[]{:S(2)}, u32[]{:S(2)}) collective-permute-start(bf16[2,7168]{1,0:T(2,128)(2,1)S(1)} %get-tuple-element.7), channel_id=1, source_target_pairs={{0,8},{1,9},{2,10},{3,11},{4,12},{5,13},{6,14},{7,15},{8,0},{9,1},... | collective-permute-start | bytes 86024 | tf_op jit(solution)/shard_map/ppermute | solution.py:215
  5.8 1.9 %collective-permute-done = bf16[2,7168]{1,0:T(2,128)(2,1)S(1)} collective-permute-done((bf16[2,7168]{1,0:T(2,128)(2,1)S(1)}, bf16[2,7168]{1,0:T(2,128)(2,1)S(1)}, u32[]{:S(2)}, u32[]{:S(2)}) %collective-permute-start) | collective-permute-done | bytes 28704 | tf_op jit(solution)/shard_map/ppermute | solution.py:215
  7.7 2.9 %collective-permute-start.3 = (bf16[4,7168]{1,0:T(4,128)(2,1)S(1)}, bf16[4,7168]{1,0:T(4,128)(2,1)S(1)}, u32[]{:S(2)}, u32[]{:S(2)}) collective-permute-start(bf16[4,7168]{1,0:T(4,128)(2,1)S(1)} %pad_maximum_fusion), channel_id=1, source_target_pairs={{0,6},{1,7},{2,4},{3,5},{4,2},{5,3},{6,0},{7,1},{8,14},{9,15},{10,... | collective-permute-start | bytes 172040 | tf_op jit(solution)/shard_map/ppermute | solution.py:215
  10.6 0.6 %collective-permute-start.2 = (bf16[4,7168]{1,0:T(4,128)(2,1)S(1)}, bf16[4,7168]{1,0:T(4,128)(2,1)S(1)}, u32[]{:S(2)}, u32[]{:S(2)}) collective-permute-start(bf16[4,7168]{1,0:T(4,128)(2,1)S(1)} %pad_maximum_fusion), channel_id=1, source_target_pairs={{0,4},{1,5},{2,6},{3,7},{4,0},{5,1},{6,2},{7,3},{8,12},{9,13},{10,... | collective-permute-start | bytes 172040 | tf_op jit(solution)/shard_map/ppermute | solution.py:215
  11.2 1.7 %collective-permute-done.3 = bf16[4,7168]{1,0:T(4,128)(2,1)S(1)} collective-permute-done((bf16[4,7168]{1,0:T(4,128)(2,1)S(1)}, bf16[4,7168]{1,0:T(4,128)(2,1)S(1)}, u32[]{:S(2)}, u32[]{:S(2)}) %collective-permute-start.3) | collective-permute-done | bytes 57376 | tf_op jit(solution)/shard_map/ppermute | solution.py:215
  13.0 1.8 %collective-permute-done.2 = bf16[4,7168]{1,0:T(4,128)(2,1)S(1)} collective-permute-done((bf16[4,7168]{1,0:T(4,128)(2,1)S(1)}, bf16[4,7168]{1,0:T(4,128)(2,1)S(1)}, u32[]{:S(2)}, u32[]{:S(2)}) %collective-permute-start.2) | collective-permute-done | bytes 57376 | tf_op jit(solution)/shard_map/ppermute | solution.py:215
  14.8 0.6 %collective-permute-done.1 = bf16[4,7168]{1,0:T(4,128)(2,1)S(1)} collective-permute-done((bf16[4,7168]{1,0:T(4,128)(2,1)S(1)}, bf16[4,7168]{1,0:T(4,128)(2,1)S(1)}, u32[]{:S(2)}, u32[]{:S(2)}) %collective-permute-start.1) | collective-permute-done | bytes 57376 | tf_op jit(solution)/shard_map/ppermute | solution.py:215
  15.7 1.5 %collective-permute-done.4.far_ref = bf16[16,7168]{1,0:T(8,128)(2,1)S(1)} collective-permute-done((bf16[16,7168]{1,0:T(8,128)(2,1)S(1)}, bf16[16,7168]{1,0:T(8,128)(2,1)S(1)}, u32[]{:S(2)}, u32[]{:S(2)}) %collective-permute-start.4) | collective-permute-done | bytes 229408 | tf_op jit(solution)/shard_map/ppermute | solution.py:215
  17.2 5.2 %shard_map.124 = (bf16[16,7168]{1,0:T(8,128)(2,1)S(1)}, bf16[16,7168]{1,0:T(8,128)(2,1)S(1)}) custom-call(bf16[16,7168]{1,0:T(8,128)(2,1)S(1)} %concatenate.8.near_ref, bf16[16,7168]{1,0:T(8,128)(2,1)S(1)} %collective-permute-done.4.far_ref, bf16[7168,256]{1,0:T(8,128)(2,1)} %gate_hbm.1, bf16[7168,256]{1,0:T(8,128)(2,1)} %up_hbm.1, bf16[256,7168]{1,0:T(8,128)(2,1)} %down_hbm.1), custom_call_target="tpu_custom_call" | custom-call | flops 352321536 | bytes 11010048 | tf_op jit(solution)/shard_map/pallas_call | solution.py:219
  22.4 0.2 collective-permute-start.5
  22.6 1.8 %shard_map.125 = bf16[16,2,2304]{2,1,0:T(2,128)(2,1)} custom-call(s32[1,16]{1,0:T(1,128)} %order_ref.1, bf16[16,4608]{1,0:T(8,128)(2,1)} %pool_ref.1), custom_call_target="tpu_custom_call" | custom-call | tf_op jit(solution)/shard_map/pallas_call | solution.py:219
  24.4 5.0 %all-to-all-start = ((bf16[16,2,2304]{2,1,0:T(2,128)(2,1)}), bf16[16,2,2304]{2,1,0:T(2,128)(2,1)S(1)}, u32[]{:S(2)}, u32[]{:S(2)}) async-start(bf16[16,2,2304]{2,1,0:T(2,128)(2,1)} %shard_map.125), calls=%async_computation | async-start | bytes 294912 | tf_op jit(solution)/shard_map/all_to_all | solution.py:248
  29.4 1.2 %shard_map.122 = f32[4,4]{1,0:T(4,128)S(1)} custom-call(s32[1]{0:T(128)} %bitcast.mine_ref, s32[1,4]{1,0:T(1,128)} %bitcast.17, bf16[4,7168]{1,0:T(4,128)(2,1)} %tokens_ref.3, bf16[2,7168]{1,0:T(2,128)(2,1)} %bitcast.15), custom_call_target="tpu_custom_call" | custom-call | tf_op jit(solution)/shard_map/pallas_call | solution.py:219
  30.6 0.7 %reshape.32.queries_ref = bf16[4,128,576]{2,1,0:T(8,128)(2,1)S(1)} reshape(bf16[4,73728]{1,0:T(4,128)(2,1)S(1)} %copy-done.2) | data formatting | bytes 1179648 | tf_op jit(solution)/shard_map/reshape | solution.py:297
  31.4 2.0 %collective-permute-start.6 = (bf16[4,7168]{1,0:T(4,128)(2,1)S(1)}, bf16[4,7168]{1,0:T(4,128)(2,1)S(1)}, u32[]{:S(2)}, u32[]{:S(2)}) collective-permute-start(bf16[4,7168]{1,0:T(4,128)(2,1)S(1)} %get-tuple-element.16), channel_id=1, source_target_pairs={{0,2},{1,3},{2,0},{3,1},{4,6},{5,7},{6,4},{7,5},{8,10},{9,11},{10,... | collective-permute-start | bytes 172040 | tf_op jit(solution)/shard_map/ppermute | solution.py:215
  33.4 1.5 %collective-permute-start.8 = (bf16[4,7168]{1,0:T(4,128)(2,1)S(1)}, bf16[4,7168]{1,0:T(4,128)(2,1)S(1)}, u32[]{:S(2)}, u32[]{:S(2)}) collective-permute-start(bf16[4,7168]{1,0:T(4,128)(2,1)S(1)} %get-tuple-element.17), channel_id=1, source_target_pairs={{0,6},{1,7},{2,4},{3,5},{4,2},{5,3},{6,0},{7,1},{8,14},{9,15},{10,... | collective-permute-start | bytes 172040 | tf_op jit(solution)/shard_map/ppermute | solution.py:215
  35.0 0.2 slice_reduce_fusion.3
  35.2 2.3 %all-to-all-done = bf16[16,2,2304]{2,1,0:T(2,128)(2,1)S(1)} async-done(((bf16[16,2,2304]{2,1,0:T(2,128)(2,1)}), bf16[16,2,2304]{2,1,0:T(2,128)(2,1)S(1)}, u32[]{:S(2)}, u32[]{:S(2)}) %all-to-all-start) | async-done | bytes 147488 | tf_op jit(solution)/shard_map/all_to_all | solution.py:248
  37.6 2.2 %shard_map.126 = bf16[4,128,512]{2,1,0:T(8,128)(2,1)S(1)} custom-call(s32[1,16]{1,0:T(1,128)S(1)} %copy-done, s32[4]{0:T(128)S(1)} %copy-done.1, bf16[4,128,576]{2,1,0:T(8,128)(2,1)S(1)} %reshape.32.queries_ref, bf16[32,2304]{1,0:T(8,128)(2,1)S(1)} %reshape.33.arrived_ref), custom_call_target="tpu_custom_call" | custom-call | tf_op jit(solution)/shard_map/pallas_call | solution.py:219
  39.9 1.2 %copy.13 = bf16[1,4,128,512]{3,1,2,0:T(4,128)(2,1)} copy(bf16[1,4,128,512]{3,2,1,0:T(8,128)(2,1)S(1)} %bitcast.9) | data formatting | bytes 1048576
  41.2 0.6 %collective-permute-start.9 = (bf16[2,7168]{1,0:T(2,128)(2,1)S(1)}, bf16[2,7168]{1,0:T(2,128)(2,1)S(1)}, u32[]{:S(2)}, u32[]{:S(2)}) collective-permute-start(bf16[2,7168]{1,0:T(2,128)(2,1)S(1)} %slice.85), channel_id=1, source_target_pairs={{0,8},{1,9},{2,10},{3,11},{4,12},{5,13},{6,14},{7,15},{8,0},{9,1},... | collective-permute-start | bytes 86024 | tf_op jit(solution)/shard_map/ppermute | solution.py:215
  41.8 4.2 %collective-permute-done.9 = bf16[2,7168]{1,0:T(2,128)(2,1)S(1)} collective-permute-done((bf16[2,7168]{1,0:T(2,128)(2,1)S(1)}, bf16[2,7168]{1,0:T(2,128)(2,1)S(1)}, u32[]{:S(2)}, u32[]{:S(2)}) %collective-permute-start.9) | collective-permute-done | bytes 28704 | tf_op jit(solution)/shard_map/ppermute | solution.py:215
  46.0 0.8 %add_convert_fusion = bf16[4,7168]{1,0:T(4,128)(2,1)} fusion(f32[7168]{0:T(1024)S(1)} %bitcast.14, f32[4]{0:T(128)S(1)} %get-tuple-element.11, f32[7168]{0:T(1024)S(1)} %bitcast.13, f32[4]{0:T(128)S(1)} %get-tuple-element.12, f32[7168]{0:T(1024)S(1)} %bitcast.12, f32[4]{0:T(128)S(1)} %get-tuple-element.13, f32[7168]{0:T(1024)S(1)} %bitcast.11, ...), kind=kLoop, calls=%fused_computation.4 | loop fusion | flops 229376 | bytes 172096 | tf_op jit(solution)/shard_map/convert_element_type | solution.py:293
  (22 shorter events, 0.9 us)
Async XLA Ops:
  1.6 6.0 %collective-permute-start = (bf16[2,7168]{1,0:T(2,128)(2,1)S(1)}, bf16[2,7168]{1,0:T(2,128)(2,1)S(1)}, u32[]{:S(2)}, u32[]{:S(2)}) collective-permute-start(bf16[2,7168]{1,0:T(2,128)(2,1)S(1)} %get-tuple-element.7), channel_id=1, source_target_pairs={{0,8},{1,9},{2,10},{3,11},{4,12},{5,13},{6,14},{7,15},{8,0},{9,1},... | collective-permute-start | bytes 86024 | tf_op jit(solution)/shard_map/ppermute | solution.py:215
  7.7 5.3 %collective-permute-start.3 = (bf16[4,7168]{1,0:T(4,128)(2,1)S(1)}, bf16[4,7168]{1,0:T(4,128)(2,1)S(1)}, u32[]{:S(2)}, u32[]{:S(2)}) collective-permute-start(bf16[4,7168]{1,0:T(4,128)(2,1)S(1)} %pad_maximum_fusion), channel_id=1, source_target_pairs={{0,6},{1,7},{2,4},{3,5},{4,2},{5,3},{6,0},{7,1},{8,14},{9,15},{10,... | collective-permute-start | bytes 172040 | tf_op jit(solution)/shard_map/ppermute | solution.py:215
  10.6 4.2 %collective-permute-start.2 = (bf16[4,7168]{1,0:T(4,128)(2,1)S(1)}, bf16[4,7168]{1,0:T(4,128)(2,1)S(1)}, u32[]{:S(2)}, u32[]{:S(2)}) collective-permute-start(bf16[4,7168]{1,0:T(4,128)(2,1)S(1)} %pad_maximum_fusion), channel_id=1, source_target_pairs={{0,4},{1,5},{2,6},{3,7},{4,0},{5,1},{6,2},{7,3},{8,12},{9,13},{10,... | collective-permute-start | bytes 172040 | tf_op jit(solution)/shard_map/ppermute | solution.py:215
  11.2 4.2 %collective-permute-start.1 = (bf16[4,7168]{1,0:T(4,128)(2,1)S(1)}, bf16[4,7168]{1,0:T(4,128)(2,1)S(1)}, u32[]{:S(2)}, u32[]{:S(2)}) collective-permute-start(bf16[4,7168]{1,0:T(4,128)(2,1)S(1)} %pad_maximum_fusion), channel_id=1, source_target_pairs={{0,2},{1,3},{2,0},{3,1},{4,6},{5,7},{6,4},{7,5},{8,10},{9,11},{10,... | collective-permute-start | bytes 172040 | tf_op jit(solution)/shard_map/ppermute | solution.py:215
  15.6 15.0 %copy-start.2 = (bf16[4,73728]{1,0:T(4,128)(2,1)S(1)}, bf16[4,73728]{1,0:T(4,128)(2,1)}, u32[]{:S(2)}) copy-start(bf16[4,73728]{1,0:T(4,128)(2,1)} %param.21) | copy-start | bytes 1769476
  15.6 1.6 %collective-permute-start.4 = (bf16[16,7168]{1,0:T(8,128)(2,1)S(1)}, bf16[16,7168]{1,0:T(8,128)(2,1)S(1)}, u32[]{:S(2)}, u32[]{:S(2)}) collective-permute-start(bf16[16,7168]{1,0:T(8,128)(2,1)S(1)} %concatenate.8.near_ref), channel_id=1, source_target_pairs={{0,1},{1,0},{2,3},{3,2},{4,5},{5,4},{6,7},{7,6},{8,9},{9,8},{10,11... | collective-permute-start | bytes 688136 | tf_op jit(solution)/shard_map/ppermute | solution.py:215
  22.3 15.3 %copy-start = (s32[1,16]{1,0:T(1,128)S(1)}, s32[1,16]{1,0:T(1,128)}, u32[]{:S(2)}) copy-start(s32[1,16]{1,0:T(1,128)} %table_ref.1) | copy-start | bytes 196
  22.3 15.3 %copy-start.1 = (s32[4]{0:T(128)S(1)}, s32[4]{0:T(128)}, u32[]{:S(2)}) copy-start(s32[4]{0:T(128)} %lens_ref.1) | copy-start | bytes 52
  22.4 8.9 %collective-permute-start.5 = (bf16[16,7168]{1,0:T(8,128)(2,1)S(1)}, bf16[16,7168]{1,0:T(8,128)(2,1)S(1)}, u32[]{:S(2)}, u32[]{:S(2)}) collective-permute-start(bf16[16,7168]{1,0:T(8,128)(2,1)S(1)} %get-tuple-element.9), channel_id=1, source_target_pairs={{0,1},{1,0},{2,3},{3,2},{4,5},{5,4},{6,7},{7,6},{8,9},{9,8},{10,11... | collective-permute-start | bytes 688136 | tf_op jit(solution)/shard_map/ppermute | solution.py:215
  24.4 13.2 %all-to-all-start = ((bf16[16,2,2304]{2,1,0:T(2,128)(2,1)}), bf16[16,2,2304]{2,1,0:T(2,128)(2,1)S(1)}, u32[]{:S(2)}, u32[]{:S(2)}) async-start(bf16[16,2,2304]{2,1,0:T(2,128)(2,1)} %shard_map.125), calls=%async_computation | async-start | bytes 294912 | tf_op jit(solution)/shard_map/all_to_all | solution.py:248
  31.4 9.6 %collective-permute-start.6 = (bf16[4,7168]{1,0:T(4,128)(2,1)S(1)}, bf16[4,7168]{1,0:T(4,128)(2,1)S(1)}, u32[]{:S(2)}, u32[]{:S(2)}) collective-permute-start(bf16[4,7168]{1,0:T(4,128)(2,1)S(1)} %get-tuple-element.16), channel_id=1, source_target_pairs={{0,2},{1,3},{2,0},{3,1},{4,6},{5,7},{6,4},{7,5},{8,10},{9,11},{10,... | collective-permute-start | bytes 172040 | tf_op jit(solution)/shard_map/ppermute | solution.py:215
  33.4 7.7 %collective-permute-start.8 = (bf16[4,7168]{1,0:T(4,128)(2,1)S(1)}, bf16[4,7168]{1,0:T(4,128)(2,1)S(1)}, u32[]{:S(2)}, u32[]{:S(2)}) collective-permute-start(bf16[4,7168]{1,0:T(4,128)(2,1)S(1)} %get-tuple-element.17), channel_id=1, source_target_pairs={{0,6},{1,7},{2,4},{3,5},{4,2},{5,3},{6,0},{7,1},{8,14},{9,15},{10,... | collective-permute-start | bytes 172040 | tf_op jit(solution)/shard_map/ppermute | solution.py:215
  34.9 6.2 %collective-permute-start.7 = (bf16[4,7168]{1,0:T(4,128)(2,1)S(1)}, bf16[4,7168]{1,0:T(4,128)(2,1)S(1)}, u32[]{:S(2)}, u32[]{:S(2)}) collective-permute-start(bf16[4,7168]{1,0:T(4,128)(2,1)S(1)} %get-tuple-element.18), channel_id=1, source_target_pairs={{0,4},{1,5},{2,6},{3,7},{4,0},{5,1},{6,2},{7,3},{8,12},{9,13},{10,... | collective-permute-start | bytes 172040 | tf_op jit(solution)/shard_map/ppermute | solution.py:215
  41.2 4.8 %collective-permute-start.9 = (bf16[2,7168]{1,0:T(2,128)(2,1)S(1)}, bf16[2,7168]{1,0:T(2,128)(2,1)S(1)}, u32[]{:S(2)}, u32[]{:S(2)}) collective-permute-start(bf16[2,7168]{1,0:T(2,128)(2,1)S(1)} %slice.85), channel_id=1, source_target_pairs={{0,8},{1,9},{2,10},{3,11},{4,12},{5,13},{6,14},{7,15},{8,0},{9,1},... | collective-permute-start | bytes 86024 | tf_op jit(solution)/shard_map/ppermute | solution.py:215

commit v3 on v2

--- a/solution.py
+++ b/solution.py
@@ -94,39 +94,71 @@
     out_ref[...] = mixing
 
 
-def outgoing_kernel(order_ref, pool_ref, out_ref):
-    count, _, half = out_ref.shape
+def outgoing_kernel(shards, me_ref, order_ref, pool_ref, *out_refs):
+    rows = out_refs[0].shape[0]
     blocks = pool_ref.shape[0]
-    row = lax.broadcasted_iota(jnp.int32, (2 * count, blocks), 0)
-    block = lax.broadcasted_iota(jnp.int32, (2 * count, blocks), 1)
-    wanted = jnp.zeros((2 * count, blocks), jnp.int32)
-    for d in range(count):
-        wanted = jnp.where(row // 2 == d, order_ref[0, d], wanted)
-    hit = block == wanted
-    result = jnp.zeros((2 * count, half), jnp.float32)
-    for r in range(2):
-        picks = jnp.where(hit & (row % 2 == r), 1.0, 0.0).astype(jnp.bfloat16)
-        result = result + jnp.dot(
-            picks, pool_ref[:, r * half : (r + 1) * half], preferred_element_type=jnp.float32
-        )
-    result = result.astype(jnp.bfloat16)
-    for d in range(count):
-        out_ref[d] = result[2 * d : 2 * d + 2, :]
-
-
-def attention_kernel(table_ref, lens_ref, queries_ref, arrived_ref, out_ref):
+    total = rows * len(out_refs)
+    row = lax.broadcasted_iota(jnp.int32, (total, blocks), 0)
+    block = lax.broadcasted_iota(jnp.int32, (total, blocks), 1)
+    wanted = jnp.zeros((total, blocks), jnp.int32)
+    for i in range(total):
+        target = shards * (i % rows // 2) + 2 * (i // rows) + i % 2
+        wanted = jnp.where(row == i, order_ref[0, me_ref[0] ^ target], wanted)
+    picks = jnp.where(block == wanted, 1.0, 0.0).astype(jnp.bfloat16)
+    result = jnp.dot(picks, pool_ref[...], preferred_element_type=jnp.float32)
+    for m, out_ref in enumerate(out_refs):
+        out_ref[...] = result[m * rows : (m + 1) * rows, :].astype(jnp.bfloat16)
+
+
+def join_kernel(groups, *refs):
+    row_refs, rest = refs[:groups], refs[groups:]
+    block_refs, out_refs = rest[: len(rest) // 2], rest[len(rest) // 2 :]
+    caps, width = row_refs[0].shape
+    for block_ref, out_ref in zip(block_refs, out_refs):
+        for b, row_ref in enumerate(row_refs):
+            out_ref[b * caps : (b + 1) * caps, :width] = row_ref[...]
+        out_ref[:, width:] = block_ref[...]
+
+
+def leaving_kernel(shift, *refs):
+    groups = refs[0].shape[0] // 2
+    for b, out_ref in enumerate(refs[len(refs) - groups + 1 :], 1):
+        for m, in_ref in enumerate(refs[: len(refs) - groups + 1]):
+            out_ref[2 * m : 2 * m + 2, :] = in_ref[2 * b : 2 * b + 2, shift:]
+
+
+def attention_kernel(
+    groups, shards, shift, me_ref, table_ref, lens_ref, queries_ref, *refs
+):
+    *arrived_refs, out_ref, arrived = refs
     sequences, _, entries = queries_ref.shape
-    rows = arrived_ref.shape[0]
-    per_row = BLOCK // 2
-    per_sequence = rows // 2 // sequences
-    arrived = arrived_ref[...]
+    pairs = shards // 2
+    side = groups * shards
+    for a in range(2):
+        near_refs = arrived_refs[a * pairs : (a + 1) * pairs]
+        far_refs = arrived_refs[2 * pairs + a * (groups - 1) : 2 * pairs + (a + 1) * (groups - 1)]
+        for m, near_ref in enumerate(near_refs):
+            arrived[a * side + 2 * m : a * side + 2 * m + 2, :] = near_ref[:2, shift:]
+        for b, far_ref in enumerate(far_refs, 1):
+            start = a * side + b * shards
+            arrived[start : start + shards, :] = far_ref[...]
+    count = side
+    half = count // 2
+    row = lax.broadcasted_iota(jnp.int32, (count, 2 * count), 0)
+    column = lax.broadcasted_iota(jnp.int32, (count, 2 * count), 1)
+    picks = jnp.where(column == 2 * row + row // half, 1.0, 0.0).astype(jnp.bfloat16)
+    blocks = jnp.dot(picks, arrived[...], preferred_element_type=jnp.float32).astype(jnp.bfloat16)
     cache = jnp.concatenate(
-        [arrived[:, i * entries : (i + 1) * entries] for i in range(per_row)], axis=0
+        [blocks[:, i * entries : (i + 1) * entries] for i in range(BLOCK)], axis=0
     )
     keys = cache.shape[0]
     key = lax.broadcasted_iota(jnp.int32, (1, keys), 1)
-    source = (key % rows) // 2
-    token = (key % 2) * per_row + key // rows
+    token = key // count
+    place = key % count
+    source = me_ref[0] ^ (
+        place // half + 2 * (place % pairs) + shards * (place % half // pairs)
+    )
+    per_sequence = count // sequences
     for s in range(sequences):
         position = jnp.full((1, keys), per_sequence * BLOCK, jnp.int32)
         for b in range(per_sequence):
@@ -147,44 +179,24 @@
         ).astype(jnp.bfloat16)
 
 
-def ffn_kernel(
-    chunks, near_ref, far_ref, gate_hbm, up_hbm, down_hbm, keep_ref, send_ref, gate, up, down, sems
-):
-    width, units = gate.shape
+def ffn_kernel(chunks, gate_ref, up_ref, down_ref, *refs):
+    *row_refs, keep_ref, send_ref, rows = refs
+    width, units = gate_ref.shape
     step = width // chunks
-    half = near_ref.shape[0]
-
-    def copies(i):
-        part = pl.ds(i * step, step)
-        return (
-            pltpu.make_async_copy(gate_hbm.at[part, :], gate.at[part, :], sems.at[0, i]),
-            pltpu.make_async_copy(up_hbm.at[part, :], up.at[part, :], sems.at[1, i]),
-        )
-
-    def down_copy(i):
-        part = pl.ds(i * step, step)
-        return pltpu.make_async_copy(down_hbm.at[:, part], down.at[:, part], sems.at[2, i])
-
-    for i in range(chunks):
-        for copy in copies(i):
-            copy.start()
-    for i in range(chunks):
-        down_copy(i).start()
+    half = keep_ref.shape[0]
+    height = row_refs[0].shape[0]
+    for i, row_ref in enumerate(row_refs):
+        rows[i * height : (i + 1) * height, :] = row_ref[:, :width]
     gate_sum = jnp.zeros((2 * half, units), jnp.float32)
     up_sum = jnp.zeros((2 * half, units), jnp.float32)
     for i in range(chunks):
         part = pl.ds(i * step, step)
-        rows = jnp.concatenate([near_ref[:, part], far_ref[:, part]], axis=0)
-        gate_copy, up_copy = copies(i)
-        gate_copy.wait()
-        gate_sum += jnp.dot(rows, gate[part, :], preferred_element_type=jnp.float32)
-        up_copy.wait()
-        up_sum += jnp.dot(rows, up[part, :], preferred_element_type=jnp.float32)
+        gate_sum += jnp.dot(rows[:, part], gate_ref[part, :], preferred_element_type=jnp.float32)
+        up_sum += jnp.dot(rows[:, part], up_ref[part, :], preferred_element_type=jnp.float32)
     hidden = (gate_sum * jax.nn.sigmoid(gate_sum) * up_sum).astype(jnp.bfloat16)
     for i in range(chunks):
         part = pl.ds(i * step, step)
-        down_copy(i).wait()
-        result = jnp.dot(hidden, down[:, part], preferred_element_type=jnp.float32)
+        result = jnp.dot(hidden, down_ref[:, part], preferred_element_type=jnp.float32)
         result = result.astype(jnp.bfloat16)
         keep_ref[:, part] = result[:half, :]
         send_ref[:, part] = result[half:, :]
@@ -209,7 +221,8 @@
     top_count = routes.shape[1]
     shard_count = device_count // experts
     capacity = tok_rows * top_count // experts + tok_rows * top_count // (4 * experts)
-    mine = (lax.axis_index("ep") // shard_count).astype(jnp.int32).reshape(1)
+    me = lax.axis_index("ep").astype(jnp.int32).reshape(1)
+    mine = me // shard_count
 
     def exchange(value, mask):
         return lax.ppermute(value, "ep", [(i, i ^ mask) for i in range(device_count)])
@@ -231,44 +244,58 @@
         compiler_params=small,
     )(mine, in_hbm(routes), in_hbm(tokens))
     crossed = [exchange(packed[b], b * shard_count) for b in range(1, experts)]
-    rows = jnp.concatenate([packed[0]] + crossed, axis=0)
-    spread = [exchange(rows, m) for m in range(2, shard_count, 2)]
-    near = jnp.concatenate([rows] + spread, axis=0)
-    far = exchange(near, 1)
+    slots = experts * capacity
+    assert capacity == 2
 
     compressed_width = LATENT_RANK + ROTARY_WIDTH
-    half_block = latent_pool.shape[1] // 2
+    block_width = latent_pool.shape[1]
+    pairs = shard_count // 2
     outgoing = kernel(
-        outgoing_kernel,
-        out_shape=jax.ShapeDtypeStruct((device_count, 2, half_block), jnp.bfloat16),
-        in_specs=[smem(), vmem()],
-        out_specs=vmem(),
-        compiler_params=small,
-    )(in_hbm(send_order), in_hbm(latent_pool))
-    arrived = lax.all_to_all(outgoing, "ep", split_axis=0, concat_axis=0, tiled=True)
-
-    half = near.shape[0]
+        functools.partial(outgoing_kernel, shard_count),
+        out_shape=[jax.ShapeDtypeStruct((2 * experts, block_width), jnp.bfloat16)] * pairs,
+        in_specs=[smem(), smem(), vmem()],
+        out_specs=[vmem()] * pairs,
+        compiler_params=small,
+    )(me, in_hbm(send_order), in_hbm(latent_pool))
+    joined = kernel(
+        functools.partial(join_kernel, experts),
+        cost_estimate=pl.CostEstimate(
+            flops=8 * 10**9, bytes_accessed=8 * 10**7, transcendentals=0
+        ),
+        out_shape=[jax.ShapeDtypeStruct((slots, width + block_width), jnp.bfloat16)] * pairs,
+        in_specs=[vmem()] * (experts + pairs),
+        out_specs=[vmem()] * pairs,
+        compiler_params=small,
+    )(packed[0], *crossed, *outgoing)
+    near = [joined[0]] + [exchange(joined[m], 2 * m) for m in range(1, pairs)]
+    far = [exchange(piece, 1) for piece in near]
+    leaving = kernel(
+        functools.partial(leaving_kernel, width),
+        out_shape=[jax.ShapeDtypeStruct((shard_count, block_width), jnp.bfloat16)]
+        * (experts - 1),
+        in_specs=[vmem()] * pairs,
+        out_specs=[vmem()] * (experts - 1),
+        compiler_params=small,
+    )(*near)
+    entered = [exchange(leaving[b - 1], b * shard_count) for b in range(1, experts)]
+    arrived = near + far + entered + [exchange(piece, 1) for piece in entered]
+
+    half = slots * shard_count // 2
     units = w_gate.shape[1]
     chunks = 7
     keep, send = kernel(
         functools.partial(ffn_kernel, chunks),
         out_shape=[jax.ShapeDtypeStruct((half, width), jnp.bfloat16)] * 2,
-        in_specs=[vmem(), vmem()] + [pl.BlockSpec(memory_space=pl.ANY)] * 3,
+        in_specs=[vmem()] * (3 + shard_count),
         out_specs=[vmem(), vmem()],
-        scratch_shapes=[
-            pltpu.VMEM((width, units), jnp.bfloat16),
-            pltpu.VMEM((width, units), jnp.bfloat16),
-            pltpu.VMEM((units, width), jnp.bfloat16),
-            pltpu.SemaphoreType.DMA((3, chunks)),
-        ],
-        compiler_params=pltpu.CompilerParams(vmem_limit_bytes=54000000),
+        scratch_shapes=[pltpu.VMEM((2 * half, width), jnp.bfloat16)],
+        compiler_params=pltpu.CompilerParams(vmem_limit_bytes=16 * 1024 * 1024),
         cost_estimate=pl.CostEstimate(
             flops=12 * half * width * units, bytes_accessed=6 * width * units, transcendentals=0
         ),
-    )(near, far, w_gate, w_up, w_down)
+    )(w_gate, w_up, w_down, *near, *far)
 
     paired = keep.astype(jnp.float32) + exchange(send, 1).astype(jnp.float32)
-    slots = experts * capacity
     paired = paired.reshape(shard_count // 2, slots, width)
     total = paired[0]
     for k in range(1, shard_count // 2):
@@ -296,14 +323,15 @@
     attention_head_count = queries.shape[1] // compressed_width
     query_rows = queries.reshape(sequence_total, attention_head_count, compressed_width)
     attended = kernel(
-        attention_kernel,
+        functools.partial(attention_kernel, experts, shard_count, width),
         out_shape=jax.ShapeDtypeStruct(
             (sequence_total, attention_head_count, LATENT_RANK), jnp.bfloat16
         ),
-        in_specs=[smem(), smem(), vmem(), vmem()],
+        in_specs=[smem()] * 3 + [vmem()] * (1 + len(arrived)),
         out_specs=vmem(),
+        scratch_shapes=[pltpu.VMEM((2 * device_count, block_width), jnp.bfloat16)],
         compiler_params=pltpu.CompilerParams(vmem_limit_bytes=32 * 1024 * 1024),
-    )(block_table, seq_lens, query_rows, arrived.reshape(2 * device_count, half_block))
+    )(me, block_table, seq_lens, query_rows, *arrived)
     attended = attended.reshape(sequence_total, attention_head_count * LATENT_RANK)
     return (expert_out, attended)
 

time: 47.1 us -> 41 us (0.87)
  Pallas kernels: 11.4 us -> 7.89 us
  waiting for transfers between devices: 14.1 us -> 12.9 us
  starting transfers between devices: 17 us -> 16.1 us
    all_to_all x1 -> x0, starting transfers between devices: 4.98 us -> none  [layer(): lax.all_to_all(outgoing, 'ep', split_axis=0, concat_axis=0, tiled=True)]
    ppermute x10 -> x15, starting transfers between devices: 12.1 us -> 16.1 us  [exchange(): lax.ppermute(value, 'ep', [(i, i ^ mask) for i in range(device_count)])]
    pallas_call x5 -> x7, Pallas kernels: 11.4 us -> 7.89 us  [call(): return pl.pallas_call(body, **options)(*operands)]
    all_to_all x1 -> x0, waiting for transfers between devices: 2.34 us -> none  [layer(): lax.all_to_all(outgoing, 'ep', split_axis=0, concat_axis=0, tiled=True)]
    ppermute x10 -> x15, waiting for transfers between devices: 11.7 us -> 12.9 us  [exchange(): lax.ppermute(value, 'ep', [(i, i ^ mask) for i in range(device_count)])]
    unnamed x7 -> x13, local copies, waits for them, and re-layouts: 1.22 us -> 1.22 us
  transfers between devices with their start and end apart: 11 -> 15, of which waited for: 7 -> 7; matrix products, arithmetic and copies ran while one was open for 5% -> 6% of each run, Pallas kernels for 11% -> 12%
where the time goes in v3:
time: 41 us; the launch traced here: 40.8 us
  starting transfers between devices  16.1 us (39%)
  waiting for transfers between devices  12.9 us (31%)
  Pallas kernels  7.89 us (19%)
  local copies, waits for them, and re-layouts  2.29 us (6%)
  other arithmetic  0.87 us (2%)
  between operations  0.79 us (2%)
    ppermute x15, starting transfers between devices, exchange(): lax.ppermute(value, 'ep', [(i, i ^ mask) for i in range(device_count)])  16.1 us
    ppermute x15, waiting for transfers between devices, exchange(): lax.ppermute(value, 'ep', [(i, i ^ mask) for i in range(device_count)])  12.9 us
    pallas_call x7, Pallas kernels, call(): return pl.pallas_call(body, **options)(*operands)  7.89 us
    unnamed x13, local copies, waits for them, and re-layouts  1.22 us
  transfers between devices with their start and end apart: 15, of which 7 were waited for; matrix products, arithmetic and copies ran while one was open for 6% of the time, Pallas kernels for 12%

profile of v3, /device:TPU:0, one launch (start us, length us, event | category | flops | bytes accessed | tf_op | source)
XLA Modules:
  0.0 40.8 jit_solution(4778355881440258431)
XLA Ops:
  0.6 1.0 %shard_map.123 = (bf16[2,7168]{1,0:T(2,128)(2,1)S(1)}, bf16[2,7168]{1,0:T(2,128)(2,1)S(1)}) custom-call(s32[1]{0:T(128)S(6)} %select_n.5.mine_ref, s32[1,4]{1,0:T(1,128)} %bitcast.16, bf16[4,7168]{1,0:T(4,128)(2,1)} %tokens_ref.3), custom_call_target="tpu_custom_call" | custom-call | tf_op jit(solution)/shard_map/pallas_call | solution.py:232
  1.6 4.1 %collective-permute-start = (bf16[2,7168]{1,0:T(2,128)(2,1)S(1)}, bf16[2,7168]{1,0:T(2,128)(2,1)S(1)}, u32[]{:S(2)}, u32[]{:S(2)}) collective-permute-start(bf16[2,7168]{1,0:T(2,128)(2,1)S(1)} %get-tuple-element.15), channel_id=1, source_target_pairs={{0,8},{1,9},{2,10},{3,11},{4,12},{5,13},{6,14},{7,15},{8,0},{9,1},... | collective-permute-start | bytes 86024 | tf_op jit(solution)/shard_map/ppermute | solution.py:228
  5.8 1.1 %shard_map.124 = (bf16[4,4608]{1,0:T(4,128)(2,1)S(1)}, bf16[4,4608]{1,0:T(4,128)(2,1)S(1)}, bf16[4,4608]{1,0:T(4,128)(2,1)S(1)}, bf16[4,4608]{1,0:T(4,128)(2,1)S(1)}) custom-call(s32[1]{0:T(128)} %bitcast.me_ref, s32[1,16]{1,0:T(1,128)} %order_ref.1, bf16[16,4608]{1,0:T(8,128)(2,1)} %pool_ref.1), custom_call_target="tpu_custom_call" | custom-call | tf_op jit(solution)/shard_map/pallas_call | solution.py:232
  6.9 0.8 %collective-permute-done.refs_1_ = bf16[2,7168]{1,0:T(2,128)(2,1)S(1)} collective-permute-done((bf16[2,7168]{1,0:T(2,128)(2,1)S(1)}, bf16[2,7168]{1,0:T(2,128)(2,1)S(1)}, u32[]{:S(2)}, u32[]{:S(2)}) %collective-permute-start) | collective-permute-done | bytes 28704 | tf_op jit(solution)/shard_map/ppermute | solution.py:228
  7.7 2.1 %collective-permute-start.1 = (bf16[4,11776]{1,0:T(4,128)(2,1)S(1)}, bf16[4,11776]{1,0:T(4,128)(2,1)S(1)}, u32[]{:S(2)}, u32[]{:S(2)}) collective-permute-start(bf16[4,11776]{1,0:T(4,128)(2,1)S(1)} %get-tuple-element.21), channel_id=1, source_target_pairs={{0,2},{1,3},{2,0},{3,1},{4,6},{5,7},{6,4},{7,5},{8,10},{9,11},{10,... | collective-permute-start | bytes 282632 | tf_op jit(solution)/shard_map/ppermute | solution.py:228
  9.7 1.4 %collective-permute-start.2 = (bf16[4,11776]{1,0:T(4,128)(2,1)S(1)}, bf16[4,11776]{1,0:T(4,128)(2,1)S(1)}, u32[]{:S(2)}, u32[]{:S(2)}) collective-permute-start(bf16[4,11776]{1,0:T(4,128)(2,1)S(1)} %get-tuple-element.22), channel_id=1, source_target_pairs={{0,4},{1,5},{2,6},{3,7},{4,0},{5,1},{6,2},{7,3},{8,12},{9,13},{10,... | collective-permute-start | bytes 282632 | tf_op jit(solution)/shard_map/ppermute | solution.py:228
  11.3 1.5 %collective-permute-done.1.refs_1_ = bf16[4,11776]{1,0:T(4,128)(2,1)S(1)} collective-permute-done((bf16[4,11776]{1,0:T(4,128)(2,1)S(1)}, bf16[4,11776]{1,0:T(4,128)(2,1)S(1)}, u32[]{:S(2)}, u32[]{:S(2)}) %collective-permute-start.1) | collective-permute-done | bytes 94240 | tf_op jit(solution)/shard_map/ppermute | solution.py:228
  12.8 1.5 %collective-permute-done.2.refs_2_ = bf16[4,11776]{1,0:T(4,128)(2,1)S(1)} collective-permute-done((bf16[4,11776]{1,0:T(4,128)(2,1)S(1)}, bf16[4,11776]{1,0:T(4,128)(2,1)S(1)}, u32[]{:S(2)}, u32[]{:S(2)}) %collective-permute-start.2) | collective-permute-done | bytes 94240 | tf_op jit(solution)/shard_map/ppermute | solution.py:228
  14.3 2.3 %collective-permute-done.3.refs_3_ = bf16[4,11776]{1,0:T(4,128)(2,1)S(1)} collective-permute-done((bf16[4,11776]{1,0:T(4,128)(2,1)S(1)}, bf16[4,11776]{1,0:T(4,128)(2,1)S(1)}, u32[]{:S(2)}, u32[]{:S(2)}) %collective-permute-start.3) | collective-permute-done | bytes 94240 | tf_op jit(solution)/shard_map/ppermute | solution.py:228
  16.6 1.3 %collective-permute-done.7.refs_7_ = bf16[4,11776]{1,0:T(4,128)(2,1)S(1)} collective-permute-done((bf16[4,11776]{1,0:T(4,128)(2,1)S(1)}, bf16[4,11776]{1,0:T(4,128)(2,1)S(1)}, u32[]{:S(2)}, u32[]{:S(2)}) %collective-permute-start.7) | collective-permute-done | bytes 94240 | tf_op jit(solution)/shard_map/ppermute | solution.py:228
  17.9 2.1 %shard_map.126 = (bf16[16,7168]{1,0:T(8,128)(2,1)S(1)}, bf16[16,7168]{1,0:T(8,128)(2,1)S(1)}) custom-call(bf16[7168,256]{1,0:T(8,128)(2,1)S(1)} %copy-done, bf16[7168,256]{1,0:T(8,128)(2,1)S(1)} %copy-done.1, bf16[256,7168]{1,0:T(8,128)(2,1)S(1)} %copy-done.2, bf16[4,11776]{1,0:T(4,128)(2,1)S(1)} %get-tuple-element.20.refs_0_, ...), custom_call_target="tpu_custom_call" | custom-call | flops 352321536 | bytes 11010048 | tf_op jit(solution)/shard_map/pallas_call | solution.py:232
  20.0 0.2 collective-permute-start.8
  20.2 2.8 %collective-permute-start.13 = (bf16[8,4608]{1,0:T(8,128)(2,1)S(1)}, bf16[8,4608]{1,0:T(8,128)(2,1)S(1)}, u32[]{:S(2)}, u32[]{:S(2)}) collective-permute-start(bf16[8,4608]{1,0:T(8,128)(2,1)S(1)} %shard_map.127), channel_id=1, source_target_pairs={{0,8},{1,9},{2,10},{3,11},{4,12},{5,13},{6,14},{7,15},{8,0},{9,1},... | collective-permute-start | bytes 221192 | tf_op jit(solution)/shard_map/ppermute | solution.py:228
  23.1 0.7 %reshape.33.queries_ref = bf16[4,128,576]{2,1,0:T(8,128)(2,1)S(1)} reshape(bf16[4,73728]{1,0:T(4,128)(2,1)S(1)} %copy-done.5) | data formatting | bytes 1179648 | tf_op jit(solution)/shard_map/reshape | solution.py:324
  23.8 1.2 %shard_map.122 = f32[4,4]{1,0:T(4,128)S(1)} custom-call(s32[1]{0:T(128)S(6)} %select_n.5.mine_ref, s32[1,4]{1,0:T(1,128)} %bitcast.17, bf16[4,7168]{1,0:T(4,128)(2,1)} %tokens_ref.3, bf16[2,7168]{1,0:T(2,128)(2,1)} %bitcast.15), custom_call_target="tpu_custom_call" | custom-call | tf_op jit(solution)/shard_map/pallas_call | solution.py:232
  25.0 2.4 %collective-permute-done.13.refs_8_ = bf16[8,4608]{1,0:T(8,128)(2,1)S(1)} collective-permute-done((bf16[8,4608]{1,0:T(8,128)(2,1)S(1)}, bf16[8,4608]{1,0:T(8,128)(2,1)S(1)}, u32[]{:S(2)}, u32[]{:S(2)}) %collective-permute-start.13) | collective-permute-done | bytes 73760 | tf_op jit(solution)/shard_map/ppermute | solution.py:228
  27.7 2.0 %collective-permute-start.11 = (bf16[4,7168]{1,0:T(4,128)(2,1)S(1)}, bf16[4,7168]{1,0:T(4,128)(2,1)S(1)}, u32[]{:S(2)}, u32[]{:S(2)}) collective-permute-start(bf16[4,7168]{1,0:T(4,128)(2,1)S(1)} %get-tuple-element.33), channel_id=1, source_target_pairs={{0,6},{1,7},{2,4},{3,5},{4,2},{5,3},{6,0},{7,1},{8,14},{9,15},{10,... | collective-permute-start | bytes 172040 | tf_op jit(solution)/shard_map/ppermute | solution.py:228
  29.7 1.5 %collective-permute-start.9 = (bf16[4,7168]{1,0:T(4,128)(2,1)S(1)}, bf16[4,7168]{1,0:T(4,128)(2,1)S(1)}, u32[]{:S(2)}, u32[]{:S(2)}) collective-permute-start(bf16[4,7168]{1,0:T(4,128)(2,1)S(1)} %get-tuple-element.32), channel_id=1, source_target_pairs={{0,2},{1,3},{2,0},{3,1},{4,6},{5,7},{6,4},{7,5},{8,10},{9,11},{10,... | collective-permute-start | bytes 172040 | tf_op jit(solution)/shard_map/ppermute | solution.py:228
  31.2 0.2 slice_reduce_fusion.3
  31.4 2.4 %shard_map.128 = bf16[4,128,512]{2,1,0:T(8,128)(2,1)S(1)} custom-call(s32[1]{0:T(128)} %bitcast.me_ref, s32[1,16]{1,0:T(1,128)S(1)} %copy-done.3, s32[4]{0:T(128)S(1)} %copy-done.4, bf16[4,128,576]{2,1,0:T(8,128)(2,1)S(1)} %reshape.33.queries_ref, bf16[4,11776]{1,0:T(4,128)(2,1)S(1)} %get-tuple-element.20.refs_0_, ...), custom_call_target="tpu_custom_call" | custom-call | tf_op jit(solution)/shard_map/pallas_call | solution.py:232
  33.8 1.2 %copy.13 = bf16[1,4,128,512]{3,1,2,0:T(4,128)(2,1)} copy(bf16[1,4,128,512]{3,2,1,0:T(8,128)(2,1)S(1)} %bitcast.9) | data formatting | bytes 1048576
  35.2 1.7 %collective-permute-start.12 = (bf16[2,7168]{1,0:T(2,128)(2,1)S(1)}, bf16[2,7168]{1,0:T(2,128)(2,1)S(1)}, u32[]{:S(2)}, u32[]{:S(2)}) collective-permute-start(bf16[2,7168]{1,0:T(2,128)(2,1)S(1)} %slice.85), channel_id=1, source_target_pairs={{0,8},{1,9},{2,10},{3,11},{4,12},{5,13},{6,14},{7,15},{8,0},{9,1},... | collective-permute-start | bytes 86024 | tf_op jit(solution)/shard_map/ppermute | solution.py:228
  36.9 3.1 %collective-permute-done.12 = bf16[2,7168]{1,0:T(2,128)(2,1)S(1)} collective-permute-done((bf16[2,7168]{1,0:T(2,128)(2,1)S(1)}, bf16[2,7168]{1,0:T(2,128)(2,1)S(1)}, u32[]{:S(2)}, u32[]{:S(2)}) %collective-permute-start.12) | collective-permute-done | bytes 28704 | tf_op jit(solution)/shard_map/ppermute | solution.py:228
  40.0 0.8 %add_convert_fusion = bf16[4,7168]{1,0:T(4,128)(2,1)} fusion(f32[7168]{0:T(1024)S(1)} %bitcast.14, f32[4]{0:T(128)S(1)} %get-tuple-element.27, f32[7168]{0:T(1024)S(1)} %bitcast.13, f32[4]{0:T(128)S(1)} %get-tuple-element.28, f32[7168]{0:T(1024)S(1)} %bitcast.12, f32[4]{0:T(128)S(1)} %get-tuple-element.29, f32[7168]{0:T(1024)S(1)} %bitcast.11, ...), kind=kLoop, calls=%fused_computation.4 | loop fusion | flops 229376 | bytes 172096 | tf_op jit(solution)/shard_map/convert_element_type | solution.py:320
  (35 shorter events, 0.7 us)
Async XLA Ops:
  1.6 6.0 %collective-permute-start = (bf16[2,7168]{1,0:T(2,128)(2,1)S(1)}, bf16[2,7168]{1,0:T(2,128)(2,1)S(1)}, u32[]{:S(2)}, u32[]{:S(2)}) collective-permute-start(bf16[2,7168]{1,0:T(2,128)(2,1)S(1)} %get-tuple-element.15), channel_id=1, source_target_pairs={{0,8},{1,9},{2,10},{3,11},{4,12},{5,13},{6,14},{7,15},{8,0},{9,1},... | collective-permute-start | bytes 86024 | tf_op jit(solution)/shard_map/ppermute | solution.py:228
  7.6 10.3 %copy-start = (bf16[7168,256]{1,0:T(8,128)(2,1)S(1)}, bf16[7168,256]{1,0:T(8,128)(2,1)}, u32[]{:S(2)}) copy-start(bf16[7168,256]{1,0:T(8,128)(2,1)} %gate_ref.1) | copy-start | bytes 11010052
  7.6 10.3 %copy-start.1 = (bf16[7168,256]{1,0:T(8,128)(2,1)S(1)}, bf16[7168,256]{1,0:T(8,128)(2,1)}, u32[]{:S(2)}) copy-start(bf16[7168,256]{1,0:T(8,128)(2,1)} %up_ref.1) | copy-start | bytes 11010052
  7.6 10.3 %copy-start.2 = (bf16[256,7168]{1,0:T(8,128)(2,1)S(1)}, bf16[256,7168]{1,0:T(8,128)(2,1)}, u32[]{:S(2)}) copy-start(bf16[256,7168]{1,0:T(8,128)(2,1)} %down_ref.1) | copy-start | bytes 11010052
  7.7 5.2 %collective-permute-start.1 = (bf16[4,11776]{1,0:T(4,128)(2,1)S(1)}, bf16[4,11776]{1,0:T(4,128)(2,1)S(1)}, u32[]{:S(2)}, u32[]{:S(2)}) collective-permute-start(bf16[4,11776]{1,0:T(4,128)(2,1)S(1)} %get-tuple-element.21), channel_id=1, source_target_pairs={{0,2},{1,3},{2,0},{3,1},{4,6},{5,7},{6,4},{7,5},{8,10},{9,11},{10,... | collective-permute-start | bytes 282632 | tf_op jit(solution)/shard_map/ppermute | solution.py:228
  9.7 4.6 %collective-permute-start.2 = (bf16[4,11776]{1,0:T(4,128)(2,1)S(1)}, bf16[4,11776]{1,0:T(4,128)(2,1)S(1)}, u32[]{:S(2)}, u32[]{:S(2)}) collective-permute-start(bf16[4,11776]{1,0:T(4,128)(2,1)S(1)} %get-tuple-element.22), channel_id=1, source_target_pairs={{0,4},{1,5},{2,6},{3,7},{4,0},{5,1},{6,2},{7,3},{8,12},{9,13},{10,... | collective-permute-start | bytes 282632 | tf_op jit(solution)/shard_map/ppermute | solution.py:228
  11.1 5.5 %collective-permute-start.3 = (bf16[4,11776]{1,0:T(4,128)(2,1)S(1)}, bf16[4,11776]{1,0:T(4,128)(2,1)S(1)}, u32[]{:S(2)}, u32[]{:S(2)}) collective-permute-start(bf16[4,11776]{1,0:T(4,128)(2,1)S(1)} %get-tuple-element.23), channel_id=1, source_target_pairs={{0,6},{1,7},{2,4},{3,5},{4,2},{5,3},{6,0},{7,1},{8,14},{9,15},{10,... | collective-permute-start | bytes 282632 | tf_op jit(solution)/shard_map/ppermute | solution.py:228
  11.3 11.8 %copy-start.5 = (bf16[4,73728]{1,0:T(4,128)(2,1)S(1)}, bf16[4,73728]{1,0:T(4,128)(2,1)}, u32[]{:S(2)}) copy-start(bf16[4,73728]{1,0:T(4,128)(2,1)} %param.21) | copy-start | bytes 1769476
  11.3 20.1 %copy-start.3 = (s32[1,16]{1,0:T(1,128)S(1)}, s32[1,16]{1,0:T(1,128)}, u32[]{:S(2)}) copy-start(s32[1,16]{1,0:T(1,128)} %table_ref.1) | copy-start | bytes 196
  11.3 20.1 %copy-start.4 = (s32[4]{0:T(128)S(1)}, s32[4]{0:T(128)}, u32[]{:S(2)}) copy-start(s32[4]{0:T(128)} %lens_ref.1) | copy-start | bytes 52
  11.3 5.3 %collective-permute-start.4 = (bf16[4,11776]{1,0:T(4,128)(2,1)S(1)}, bf16[4,11776]{1,0:T(4,128)(2,1)S(1)}, u32[]{:S(2)}, u32[]{:S(2)}) collective-permute-start(bf16[4,11776]{1,0:T(4,128)(2,1)S(1)} %get-tuple-element.20.refs_0_), channel_id=1, source_target_pairs={{0,1},{1,0},{2,3},{3,2},{4,5},{5,4},{6,7},{7,6},{8,9},{9,8},{10,11... | collective-permute-start | bytes 282632 | tf_op jit(solution)/shard_map/ppermute | solution.py:228
  12.8 3.8 %collective-permute-start.5 = (bf16[4,11776]{1,0:T(4,128)(2,1)S(1)}, bf16[4,11776]{1,0:T(4,128)(2,1)S(1)}, u32[]{:S(2)}, u32[]{:S(2)}) collective-permute-start(bf16[4,11776]{1,0:T(4,128)(2,1)S(1)} %collective-permute-done.1.refs_1_), channel_id=1, source_target_pairs={{0,1},{1,0},{2,3},{3,2},{4,5},{5,4},{6,7},{7,6},{8,9},{9,8},{10,11... | collective-permute-start | bytes 282632 | tf_op jit(solution)/shard_map/ppermute | solution.py:228
  14.3 2.3 %collective-permute-start.6 = (bf16[4,11776]{1,0:T(4,128)(2,1)S(1)}, bf16[4,11776]{1,0:T(4,128)(2,1)S(1)}, u32[]{:S(2)}, u32[]{:S(2)}) collective-permute-start(bf16[4,11776]{1,0:T(4,128)(2,1)S(1)} %collective-permute-done.2.refs_2_), channel_id=1, source_target_pairs={{0,1},{1,0},{2,3},{3,2},{4,5},{5,4},{6,7},{7,6},{8,9},{9,8},{10,11... | collective-permute-start | bytes 282632 | tf_op jit(solution)/shard_map/ppermute | solution.py:228
  16.6 1.3 %collective-permute-start.7 = (bf16[4,11776]{1,0:T(4,128)(2,1)S(1)}, bf16[4,11776]{1,0:T(4,128)(2,1)S(1)}, u32[]{:S(2)}, u32[]{:S(2)}) collective-permute-start(bf16[4,11776]{1,0:T(4,128)(2,1)S(1)} %collective-permute-done.3.refs_3_), channel_id=1, source_target_pairs={{0,1},{1,0},{2,3},{3,2},{4,5},{5,4},{6,7},{7,6},{8,9},{9,8},{10,11... | collective-permute-start | bytes 282632 | tf_op jit(solution)/shard_map/ppermute | solution.py:228
  20.0 7.5 %collective-permute-start.8 = (bf16[16,7168]{1,0:T(8,128)(2,1)S(1)}, bf16[16,7168]{1,0:T(8,128)(2,1)S(1)}, u32[]{:S(2)}, u32[]{:S(2)}) collective-permute-start(bf16[16,7168]{1,0:T(8,128)(2,1)S(1)} %get-tuple-element.25), channel_id=1, source_target_pairs={{0,1},{1,0},{2,3},{3,2},{4,5},{5,4},{6,7},{7,6},{8,9},{9,8},{10,11... | collective-permute-start | bytes 688136 | tf_op jit(solution)/shard_map/ppermute | solution.py:228
  20.2 7.1 %collective-permute-start.13 = (bf16[8,4608]{1,0:T(8,128)(2,1)S(1)}, bf16[8,4608]{1,0:T(8,128)(2,1)S(1)}, u32[]{:S(2)}, u32[]{:S(2)}) collective-permute-start(bf16[8,4608]{1,0:T(8,128)(2,1)S(1)} %shard_map.127), channel_id=1, source_target_pairs={{0,8},{1,9},{2,10},{3,11},{4,12},{5,13},{6,14},{7,15},{8,0},{9,1},... | collective-permute-start | bytes 221192 | tf_op jit(solution)/shard_map/ppermute | solution.py:228
  27.4 4.0 %collective-permute-start.14 = (bf16[8,4608]{1,0:T(8,128)(2,1)S(1)}, bf16[8,4608]{1,0:T(8,128)(2,1)S(1)}, u32[]{:S(2)}, u32[]{:S(2)}) collective-permute-start(bf16[8,4608]{1,0:T(8,128)(2,1)S(1)} %collective-permute-done.13.refs_8_), channel_id=1, source_target_pairs={{0,1},{1,0},{2,3},{3,2},{4,5},{5,4},{6,7},{7,6},{8,9},{9,8},{10,11... | collective-permute-start | bytes 221192 | tf_op jit(solution)/shard_map/ppermute | solution.py:228
  27.6 7.4 %collective-permute-start.10 = (bf16[4,7168]{1,0:T(4,128)(2,1)S(1)}, bf16[4,7168]{1,0:T(4,128)(2,1)S(1)}, u32[]{:S(2)}, u32[]{:S(2)}) collective-permute-start(bf16[4,7168]{1,0:T(4,128)(2,1)S(1)} %get-tuple-element.34), channel_id=1, source_target_pairs={{0,4},{1,5},{2,6},{3,7},{4,0},{5,1},{6,2},{7,3},{8,12},{9,13},{10,... | collective-permute-start | bytes 172040 | tf_op jit(solution)/shard_map/ppermute | solution.py:228
  27.7 7.4 %collective-permute-start.11 = (bf16[4,7168]{1,0:T(4,128)(2,1)S(1)}, bf16[4,7168]{1,0:T(4,128)(2,1)S(1)}, u32[]{:S(2)}, u32[]{:S(2)}) collective-permute-start(bf16[4,7168]{1,0:T(4,128)(2,1)S(1)} %get-tuple-element.33), channel_id=1, source_target_pairs={{0,6},{1,7},{2,4},{3,5},{4,2},{5,3},{6,0},{7,1},{8,14},{9,15},{10,... | collective-permute-start | bytes 172040 | tf_op jit(solution)/shard_map/ppermute | solution.py:228
  29.7 5.4 %collective-permute-start.9 = (bf16[4,7168]{1,0:T(4,128)(2,1)S(1)}, bf16[4,7168]{1,0:T(4,128)(2,1)S(1)}, u32[]{:S(2)}, u32[]{:S(2)}) collective-permute-start(bf16[4,7168]{1,0:T(4,128)(2,1)S(1)} %get-tuple-element.32), channel_id=1, source_target_pairs={{0,2},{1,3},{2,0},{3,1},{4,6},{5,7},{6,4},{7,5},{8,10},{9,11},{10,... | collective-permute-start | bytes 172040 | tf_op jit(solution)/shard_map/ppermute | solution.py:228
  35.2 4.8 %collective-permute-start.12 = (bf16[2,7168]{1,0:T(2,128)(2,1)S(1)}, bf16[2,7168]{1,0:T(2,128)(2,1)S(1)}, u32[]{:S(2)}, u32[]{:S(2)}) collective-permute-start(bf16[2,7168]{1,0:T(2,128)(2,1)S(1)} %slice.85), channel_id=1, source_target_pairs={{0,8},{1,9},{2,10},{3,11},{4,12},{5,13},{6,14},{7,15},{8,0},{9,1},... | collective-permute-start | bytes 86024 | tf_op jit(solution)/shard_map/ppermute | solution.py:228

commit v4 on v3

--- a/solution.py
+++ b/solution.py
@@ -131,7 +131,7 @@
     groups, shards, shift, me_ref, table_ref, lens_ref, queries_ref, *refs
 ):
     *arrived_refs, out_ref, arrived = refs
-    sequences, _, entries = queries_ref.shape
+    sequences, heads, entries = queries_ref.shape
     pairs = shards // 2
     side = groups * shards
     for a in range(2):
@@ -159,24 +159,26 @@
         place // half + 2 * (place % pairs) + shards * (place % half // pairs)
     )
     per_sequence = count // sequences
+    visible = []
     for s in range(sequences):
         position = jnp.full((1, keys), per_sequence * BLOCK, jnp.int32)
         for b in range(per_sequence):
             position = jnp.where(
                 source == table_ref[0, s * per_sequence + b], b * BLOCK + token, position
             )
-        visible = position < lens_ref[s]
-        logits = lax.dot_general(
-            queries_ref[s], cache, (((1,), (1,)), ((), ())), preferred_element_type=jnp.float32
-        )
-        logits = jnp.where(visible, logits * softmax_scale, -1e30)
-        peak = jnp.max(logits, axis=-1, keepdims=True)
-        unnormed = jnp.exp(logits - peak)
-        unnormed = jnp.where(visible, unnormed, 0.0)
-        weights = (unnormed / jnp.sum(unnormed, axis=-1, keepdims=True)).astype(jnp.bfloat16)
-        out_ref[s] = jnp.dot(
-            weights, cache[:, :LATENT_RANK], preferred_element_type=jnp.float32
-        ).astype(jnp.bfloat16)
+        shown = jnp.where(position < lens_ref[s], 1.0, 0.0)
+        visible.append(jnp.broadcast_to(shown, (heads, keys)))
+    visible = jnp.concatenate(visible, axis=0) > 0.5
+    queries = queries_ref[...].reshape(sequences * heads, entries)
+    logits = lax.dot_general(
+        queries, cache, (((1,), (1,)), ((), ())), preferred_element_type=jnp.float32
+    )
+    logits = jnp.where(visible, logits * softmax_scale, -1e30)
+    peak = jnp.max(logits, axis=-1, keepdims=True)
+    unnormed = jnp.where(visible, jnp.exp(logits - peak), 0.0)
+    weights = (unnormed / jnp.sum(unnormed, axis=-1, keepdims=True)).astype(jnp.bfloat16)
+    attended = jnp.dot(weights, cache[:, :LATENT_RANK], preferred_element_type=jnp.float32)
+    out_ref[...] = attended.astype(jnp.bfloat16).reshape(sequences, heads, LATENT_RANK)
 
 
 def ffn_kernel(chunks, gate_ref, up_ref, down_ref, *refs):

time: 41 us -> 40.8 us (level)
  starting transfers between devices: 16.1 us -> 16.7 us
  Pallas kernels: 7.89 us -> 7.31 us
    ppermute x15, starting transfers between devices: 16.1 us -> 16.7 us  [exchange(): lax.ppermute(value, 'ep', [(i, i ^ mask) for i in range(device_count)])]
    pallas_call x7, Pallas kernels: 7.89 us -> 7.31 us  [call(): return pl.pallas_call(body, **options)(*operands)]
  transfers between devices with their start and end apart: 15 -> 15, of which waited for: 7 -> 7; matrix products, arithmetic and copies ran while one was open for 6% -> 6% of each run, Pallas kernels for 12% -> 10%
where the time goes in v4:
time: 40.8 us; the launch traced here: 40.5 us
  starting transfers between devices  16.7 us (41%)
  waiting for transfers between devices  12.6 us (31%)
  Pallas kernels  7.31 us (18%)
  local copies, waits for them, and re-layouts  2.29 us (6%)
  other arithmetic  0.87 us (2%)
  between operations  0.79 us (2%)
    ppermute x15, starting transfers between devices, exchange(): lax.ppermute(value, 'ep', [(i, i ^ mask) for i in range(device_count)])  16.7 us
    ppermute x15, waiting for transfers between devices, exchange(): lax.ppermute(value, 'ep', [(i, i ^ mask) for i in range(device_count)])  12.6 us
    pallas_call x7, Pallas kernels, call(): return pl.pallas_call(body, **options)(*operands)  7.31 us
    unnamed x13, local copies, waits for them, and re-layouts  1.22 us
  transfers between devices with their start and end apart: 15, of which 7 were waited for; matrix products, arithmetic and copies ran while one was open for 6% of the time, Pallas kernels for 10%

profile of v4, /device:TPU:0, one launch (start us, length us, event | category | flops | bytes accessed | tf_op | source)
XLA Modules:
  0.0 40.5 jit_solution(14929738355324185311)
XLA Ops:
  0.6 1.0 %shard_map.123 = (bf16[2,7168]{1,0:T(2,128)(2,1)S(1)}, bf16[2,7168]{1,0:T(2,128)(2,1)S(1)}) custom-call(s32[1]{0:T(128)S(6)} %select_n.5.mine_ref, s32[1,4]{1,0:T(1,128)} %bitcast.16, bf16[4,7168]{1,0:T(4,128)(2,1)} %tokens_ref.3), custom_call_target="tpu_custom_call" | custom-call | tf_op jit(solution)/shard_map/pallas_call | solution.py:234
  1.6 4.1 %collective-permute-start = (bf16[2,7168]{1,0:T(2,128)(2,1)S(1)}, bf16[2,7168]{1,0:T(2,128)(2,1)S(1)}, u32[]{:S(2)}, u32[]{:S(2)}) collective-permute-start(bf16[2,7168]{1,0:T(2,128)(2,1)S(1)} %get-tuple-element.15), channel_id=1, source_target_pairs={{0,8},{1,9},{2,10},{3,11},{4,12},{5,13},{6,14},{7,15},{8,0},{9,1},... | collective-permute-start | bytes 86024 | tf_op jit(solution)/shard_map/ppermute | solution.py:230
  5.8 1.1 %shard_map.124 = (bf16[4,4608]{1,0:T(4,128)(2,1)S(1)}, bf16[4,4608]{1,0:T(4,128)(2,1)S(1)}, bf16[4,4608]{1,0:T(4,128)(2,1)S(1)}, bf16[4,4608]{1,0:T(4,128)(2,1)S(1)}) custom-call(s32[1]{0:T(128)} %bitcast.me_ref, s32[1,16]{1,0:T(1,128)} %order_ref.1, bf16[16,4608]{1,0:T(8,128)(2,1)} %pool_ref.1), custom_call_target="tpu_custom_call" | custom-call | tf_op jit(solution)/shard_map/pallas_call | solution.py:234
  6.9 0.8 %collective-permute-done.refs_1_ = bf16[2,7168]{1,0:T(2,128)(2,1)S(1)} collective-permute-done((bf16[2,7168]{1,0:T(2,128)(2,1)S(1)}, bf16[2,7168]{1,0:T(2,128)(2,1)S(1)}, u32[]{:S(2)}, u32[]{:S(2)}) %collective-permute-start) | collective-permute-done | bytes 28704 | tf_op jit(solution)/shard_map/ppermute | solution.py:230
  7.7 2.1 %collective-permute-start.1 = (bf16[4,11776]{1,0:T(4,128)(2,1)S(1)}, bf16[4,11776]{1,0:T(4,128)(2,1)S(1)}, u32[]{:S(2)}, u32[]{:S(2)}) collective-permute-start(bf16[4,11776]{1,0:T(4,128)(2,1)S(1)} %get-tuple-element.21), channel_id=1, source_target_pairs={{0,2},{1,3},{2,0},{3,1},{4,6},{5,7},{6,4},{7,5},{8,10},{9,11},{10,... | collective-permute-start | bytes 282632 | tf_op jit(solution)/shard_map/ppermute | solution.py:230
  9.7 1.4 %collective-permute-start.2 = (bf16[4,11776]{1,0:T(4,128)(2,1)S(1)}, bf16[4,11776]{1,0:T(4,128)(2,1)S(1)}, u32[]{:S(2)}, u32[]{:S(2)}) collective-permute-start(bf16[4,11776]{1,0:T(4,128)(2,1)S(1)} %get-tuple-element.22), channel_id=1, source_target_pairs={{0,4},{1,5},{2,6},{3,7},{4,0},{5,1},{6,2},{7,3},{8,12},{9,13},{10,... | collective-permute-start | bytes 282632 | tf_op jit(solution)/shard_map/ppermute | solution.py:230
  11.3 1.5 %collective-permute-done.1.refs_1_ = bf16[4,11776]{1,0:T(4,128)(2,1)S(1)} collective-permute-done((bf16[4,11776]{1,0:T(4,128)(2,1)S(1)}, bf16[4,11776]{1,0:T(4,128)(2,1)S(1)}, u32[]{:S(2)}, u32[]{:S(2)}) %collective-permute-start.1) | collective-permute-done | bytes 94240 | tf_op jit(solution)/shard_map/ppermute | solution.py:230
  12.8 1.5 %collective-permute-done.2.refs_2_ = bf16[4,11776]{1,0:T(4,128)(2,1)S(1)} collective-permute-done((bf16[4,11776]{1,0:T(4,128)(2,1)S(1)}, bf16[4,11776]{1,0:T(4,128)(2,1)S(1)}, u32[]{:S(2)}, u32[]{:S(2)}) %collective-permute-start.2) | collective-permute-done | bytes 94240 | tf_op jit(solution)/shard_map/ppermute | solution.py:230
  14.3 2.3 %collective-permute-done.3.refs_3_ = bf16[4,11776]{1,0:T(4,128)(2,1)S(1)} collective-permute-done((bf16[4,11776]{1,0:T(4,128)(2,1)S(1)}, bf16[4,11776]{1,0:T(4,128)(2,1)S(1)}, u32[]{:S(2)}, u32[]{:S(2)}) %collective-permute-start.3) | collective-permute-done | bytes 94240 | tf_op jit(solution)/shard_map/ppermute | solution.py:230
  16.6 1.3 %collective-permute-done.7.refs_7_ = bf16[4,11776]{1,0:T(4,128)(2,1)S(1)} collective-permute-done((bf16[4,11776]{1,0:T(4,128)(2,1)S(1)}, bf16[4,11776]{1,0:T(4,128)(2,1)S(1)}, u32[]{:S(2)}, u32[]{:S(2)}) %collective-permute-start.7) | collective-permute-done | bytes 94240 | tf_op jit(solution)/shard_map/ppermute | solution.py:230
  17.9 2.1 %shard_map.126 = (bf16[16,7168]{1,0:T(8,128)(2,1)S(1)}, bf16[16,7168]{1,0:T(8,128)(2,1)S(1)}) custom-call(bf16[7168,256]{1,0:T(8,128)(2,1)S(1)} %copy-done, bf16[7168,256]{1,0:T(8,128)(2,1)S(1)} %copy-done.1, bf16[256,7168]{1,0:T(8,128)(2,1)S(1)} %copy-done.2, bf16[4,11776]{1,0:T(4,128)(2,1)S(1)} %get-tuple-element.20.refs_0_, ...), custom_call_target="tpu_custom_call" | custom-call | flops 352321536 | bytes 11010048 | tf_op jit(solution)/shard_map/pallas_call | solution.py:234
  20.0 0.2 collective-permute-start.8
  20.2 2.8 %collective-permute-start.13 = (bf16[8,4608]{1,0:T(8,128)(2,1)S(1)}, bf16[8,4608]{1,0:T(8,128)(2,1)S(1)}, u32[]{:S(2)}, u32[]{:S(2)}) collective-permute-start(bf16[8,4608]{1,0:T(8,128)(2,1)S(1)} %shard_map.127), channel_id=1, source_target_pairs={{0,8},{1,9},{2,10},{3,11},{4,12},{5,13},{6,14},{7,15},{8,0},{9,1},... | collective-permute-start | bytes 221192 | tf_op jit(solution)/shard_map/ppermute | solution.py:230
  23.1 0.7 %reshape.33.queries_ref = bf16[4,128,576]{2,1,0:T(8,128)(2,1)S(1)} reshape(bf16[4,73728]{1,0:T(4,128)(2,1)S(1)} %copy-done.5) | data formatting | bytes 1179648 | tf_op jit(solution)/shard_map/reshape | solution.py:326
  23.8 1.2 %shard_map.122 = f32[4,4]{1,0:T(4,128)S(1)} custom-call(s32[1]{0:T(128)S(6)} %select_n.5.mine_ref, s32[1,4]{1,0:T(1,128)} %bitcast.17, bf16[4,7168]{1,0:T(4,128)(2,1)} %tokens_ref.3, bf16[2,7168]{1,0:T(2,128)(2,1)} %bitcast.15), custom_call_target="tpu_custom_call" | custom-call | tf_op jit(solution)/shard_map/pallas_call | solution.py:234
  25.0 2.4 %collective-permute-done.13.refs_8_ = bf16[8,4608]{1,0:T(8,128)(2,1)S(1)} collective-permute-done((bf16[8,4608]{1,0:T(8,128)(2,1)S(1)}, bf16[8,4608]{1,0:T(8,128)(2,1)S(1)}, u32[]{:S(2)}, u32[]{:S(2)}) %collective-permute-start.13) | collective-permute-done | bytes 73760 | tf_op jit(solution)/shard_map/ppermute | solution.py:230
  27.7 2.0 %collective-permute-start.11 = (bf16[4,7168]{1,0:T(4,128)(2,1)S(1)}, bf16[4,7168]{1,0:T(4,128)(2,1)S(1)}, u32[]{:S(2)}, u32[]{:S(2)}) collective-permute-start(bf16[4,7168]{1,0:T(4,128)(2,1)S(1)} %get-tuple-element.33), channel_id=1, source_target_pairs={{0,6},{1,7},{2,4},{3,5},{4,2},{5,3},{6,0},{7,1},{8,14},{9,15},{10,... | collective-permute-start | bytes 172040 | tf_op jit(solution)/shard_map/ppermute | solution.py:230
  29.7 1.5 %collective-permute-start.9 = (bf16[4,7168]{1,0:T(4,128)(2,1)S(1)}, bf16[4,7168]{1,0:T(4,128)(2,1)S(1)}, u32[]{:S(2)}, u32[]{:S(2)}) collective-permute-start(bf16[4,7168]{1,0:T(4,128)(2,1)S(1)} %get-tuple-element.32), channel_id=1, source_target_pairs={{0,2},{1,3},{2,0},{3,1},{4,6},{5,7},{6,4},{7,5},{8,10},{9,11},{10,... | collective-permute-start | bytes 172040 | tf_op jit(solution)/shard_map/ppermute | solution.py:230
  31.2 0.2 slice_reduce_fusion.3
  31.4 1.9 %shard_map.128 = bf16[4,128,512]{2,1,0:T(8,128)(2,1)S(1)} custom-call(s32[1]{0:T(128)} %bitcast.me_ref, s32[1,16]{1,0:T(1,128)S(1)} %copy-done.3, s32[4]{0:T(128)S(1)} %copy-done.4, bf16[4,128,576]{2,1,0:T(8,128)(2,1)S(1)} %reshape.33.queries_ref, bf16[4,11776]{1,0:T(4,128)(2,1)S(1)} %get-tuple-element.20.refs_0_, ...), custom_call_target="tpu_custom_call" | custom-call | tf_op jit(solution)/shard_map/pallas_call | solution.py:234
  33.3 1.2 %copy.13 = bf16[1,4,128,512]{3,1,2,0:T(4,128)(2,1)} copy(bf16[1,4,128,512]{3,2,1,0:T(8,128)(2,1)S(1)} %bitcast.9) | data formatting | bytes 1048576
  34.6 2.3 %collective-permute-start.12 = (bf16[2,7168]{1,0:T(2,128)(2,1)S(1)}, bf16[2,7168]{1,0:T(2,128)(2,1)S(1)}, u32[]{:S(2)}, u32[]{:S(2)}) collective-permute-start(bf16[2,7168]{1,0:T(2,128)(2,1)S(1)} %slice.85), channel_id=1, source_target_pairs={{0,8},{1,9},{2,10},{3,11},{4,12},{5,13},{6,14},{7,15},{8,0},{9,1},... | collective-permute-start | bytes 86024 | tf_op jit(solution)/shard_map/ppermute | solution.py:230
  36.9 2.8 %collective-permute-done.12 = bf16[2,7168]{1,0:T(2,128)(2,1)S(1)} collective-permute-done((bf16[2,7168]{1,0:T(2,128)(2,1)S(1)}, bf16[2,7168]{1,0:T(2,128)(2,1)S(1)}, u32[]{:S(2)}, u32[]{:S(2)}) %collective-permute-start.12) | collective-permute-done | bytes 28704 | tf_op jit(solution)/shard_map/ppermute | solution.py:230
  39.8 0.8 %add_convert_fusion = bf16[4,7168]{1,0:T(4,128)(2,1)} fusion(f32[7168]{0:T(1024)S(1)} %bitcast.14, f32[4]{0:T(128)S(1)} %get-tuple-element.27, f32[7168]{0:T(1024)S(1)} %bitcast.13, f32[4]{0:T(128)S(1)} %get-tuple-element.28, f32[7168]{0:T(1024)S(1)} %bitcast.12, f32[4]{0:T(128)S(1)} %get-tuple-element.29, f32[7168]{0:T(1024)S(1)} %bitcast.11, ...), kind=kLoop, calls=%fused_computation.4 | loop fusion | flops 229376 | bytes 172096 | tf_op jit(solution)/shard_map/convert_element_type | solution.py:322
  (35 shorter events, 0.7 us)
Async XLA Ops:
  1.6 6.0 %collective-permute-start = (bf16[2,7168]{1,0:T(2,128)(2,1)S(1)}, bf16[2,7168]{1,0:T(2,128)(2,1)S(1)}, u32[]{:S(2)}, u32[]{:S(2)}) collective-permute-start(bf16[2,7168]{1,0:T(2,128)(2,1)S(1)} %get-tuple-element.15), channel_id=1, source_target_pairs={{0,8},{1,9},{2,10},{3,11},{4,12},{5,13},{6,14},{7,15},{8,0},{9,1},... | collective-permute-start | bytes 86024 | tf_op jit(solution)/shard_map/ppermute | solution.py:230
  7.6 10.3 %copy-start = (bf16[7168,256]{1,0:T(8,128)(2,1)S(1)}, bf16[7168,256]{1,0:T(8,128)(2,1)}, u32[]{:S(2)}) copy-start(bf16[7168,256]{1,0:T(8,128)(2,1)} %gate_ref.1) | copy-start | bytes 11010052
  7.6 10.3 %copy-start.1 = (bf16[7168,256]{1,0:T(8,128)(2,1)S(1)}, bf16[7168,256]{1,0:T(8,128)(2,1)}, u32[]{:S(2)}) copy-start(bf16[7168,256]{1,0:T(8,128)(2,1)} %up_ref.1) | copy-start | bytes 11010052
  7.6 10.3 %copy-start.2 = (bf16[256,7168]{1,0:T(8,128)(2,1)S(1)}, bf16[256,7168]{1,0:T(8,128)(2,1)}, u32[]{:S(2)}) copy-start(bf16[256,7168]{1,0:T(8,128)(2,1)} %down_ref.1) | copy-start | bytes 11010052
  7.7 5.2 %collective-permute-start.1 = (bf16[4,11776]{1,0:T(4,128)(2,1)S(1)}, bf16[4,11776]{1,0:T(4,128)(2,1)S(1)}, u32[]{:S(2)}, u32[]{:S(2)}) collective-permute-start(bf16[4,11776]{1,0:T(4,128)(2,1)S(1)} %get-tuple-element.21), channel_id=1, source_target_pairs={{0,2},{1,3},{2,0},{3,1},{4,6},{5,7},{6,4},{7,5},{8,10},{9,11},{10,... | collective-permute-start | bytes 282632 | tf_op jit(solution)/shard_map/ppermute | solution.py:230
  9.7 4.6 %collective-permute-start.2 = (bf16[4,11776]{1,0:T(4,128)(2,1)S(1)}, bf16[4,11776]{1,0:T(4,128)(2,1)S(1)}, u32[]{:S(2)}, u32[]{:S(2)}) collective-permute-start(bf16[4,11776]{1,0:T(4,128)(2,1)S(1)} %get-tuple-element.22), channel_id=1, source_target_pairs={{0,4},{1,5},{2,6},{3,7},{4,0},{5,1},{6,2},{7,3},{8,12},{9,13},{10,... | collective-permute-start | bytes 282632 | tf_op jit(solution)/shard_map/ppermute | solution.py:230
  11.1 5.5 %collective-permute-start.3 = (bf16[4,11776]{1,0:T(4,128)(2,1)S(1)}, bf16[4,11776]{1,0:T(4,128)(2,1)S(1)}, u32[]{:S(2)}, u32[]{:S(2)}) collective-permute-start(bf16[4,11776]{1,0:T(4,128)(2,1)S(1)} %get-tuple-element.23), channel_id=1, source_target_pairs={{0,6},{1,7},{2,4},{3,5},{4,2},{5,3},{6,0},{7,1},{8,14},{9,15},{10,... | collective-permute-start | bytes 282632 | tf_op jit(solution)/shard_map/ppermute | solution.py:230
  11.3 11.8 %copy-start.5 = (bf16[4,73728]{1,0:T(4,128)(2,1)S(1)}, bf16[4,73728]{1,0:T(4,128)(2,1)}, u32[]{:S(2)}) copy-start(bf16[4,73728]{1,0:T(4,128)(2,1)} %param.21) | copy-start | bytes 1769476
  11.3 20.1 %copy-start.3 = (s32[1,16]{1,0:T(1,128)S(1)}, s32[1,16]{1,0:T(1,128)}, u32[]{:S(2)}) copy-start(s32[1,16]{1,0:T(1,128)} %table_ref.1) | copy-start | bytes 196
  11.3 20.1 %copy-start.4 = (s32[4]{0:T(128)S(1)}, s32[4]{0:T(128)}, u32[]{:S(2)}) copy-start(s32[4]{0:T(128)} %lens_ref.1) | copy-start | bytes 52
  11.3 5.3 %collective-permute-start.4 = (bf16[4,11776]{1,0:T(4,128)(2,1)S(1)}, bf16[4,11776]{1,0:T(4,128)(2,1)S(1)}, u32[]{:S(2)}, u32[]{:S(2)}) collective-permute-start(bf16[4,11776]{1,0:T(4,128)(2,1)S(1)} %get-tuple-element.20.refs_0_), channel_id=1, source_target_pairs={{0,1},{1,0},{2,3},{3,2},{4,5},{5,4},{6,7},{7,6},{8,9},{9,8},{10,11... | collective-permute-start | bytes 282632 | tf_op jit(solution)/shard_map/ppermute | solution.py:230
  12.8 3.8 %collective-permute-start.5 = (bf16[4,11776]{1,0:T(4,128)(2,1)S(1)}, bf16[4,11776]{1,0:T(4,128)(2,1)S(1)}, u32[]{:S(2)}, u32[]{:S(2)}) collective-permute-start(bf16[4,11776]{1,0:T(4,128)(2,1)S(1)} %collective-permute-done.1.refs_1_), channel_id=1, source_target_pairs={{0,1},{1,0},{2,3},{3,2},{4,5},{5,4},{6,7},{7,6},{8,9},{9,8},{10,11... | collective-permute-start | bytes 282632 | tf_op jit(solution)/shard_map/ppermute | solution.py:230
  14.3 2.3 %collective-permute-start.6 = (bf16[4,11776]{1,0:T(4,128)(2,1)S(1)}, bf16[4,11776]{1,0:T(4,128)(2,1)S(1)}, u32[]{:S(2)}, u32[]{:S(2)}) collective-permute-start(bf16[4,11776]{1,0:T(4,128)(2,1)S(1)} %collective-permute-done.2.refs_2_), channel_id=1, source_target_pairs={{0,1},{1,0},{2,3},{3,2},{4,5},{5,4},{6,7},{7,6},{8,9},{9,8},{10,11... | collective-permute-start | bytes 282632 | tf_op jit(solution)/shard_map/ppermute | solution.py:230
  16.6 1.3 %collective-permute-start.7 = (bf16[4,11776]{1,0:T(4,128)(2,1)S(1)}, bf16[4,11776]{1,0:T(4,128)(2,1)S(1)}, u32[]{:S(2)}, u32[]{:S(2)}) collective-permute-start(bf16[4,11776]{1,0:T(4,128)(2,1)S(1)} %collective-permute-done.3.refs_3_), channel_id=1, source_target_pairs={{0,1},{1,0},{2,3},{3,2},{4,5},{5,4},{6,7},{7,6},{8,9},{9,8},{10,11... | collective-permute-start | bytes 282632 | tf_op jit(solution)/shard_map/ppermute | solution.py:230
  20.0 7.5 %collective-permute-start.8 = (bf16[16,7168]{1,0:T(8,128)(2,1)S(1)}, bf16[16,7168]{1,0:T(8,128)(2,1)S(1)}, u32[]{:S(2)}, u32[]{:S(2)}) collective-permute-start(bf16[16,7168]{1,0:T(8,128)(2,1)S(1)} %get-tuple-element.25), channel_id=1, source_target_pairs={{0,1},{1,0},{2,3},{3,2},{4,5},{5,4},{6,7},{7,6},{8,9},{9,8},{10,11... | collective-permute-start | bytes 688136 | tf_op jit(solution)/shard_map/ppermute | solution.py:230
  20.2 7.1 %collective-permute-start.13 = (bf16[8,4608]{1,0:T(8,128)(2,1)S(1)}, bf16[8,4608]{1,0:T(8,128)(2,1)S(1)}, u32[]{:S(2)}, u32[]{:S(2)}) collective-permute-start(bf16[8,4608]{1,0:T(8,128)(2,1)S(1)} %shard_map.127), channel_id=1, source_target_pairs={{0,8},{1,9},{2,10},{3,11},{4,12},{5,13},{6,14},{7,15},{8,0},{9,1},... | collective-permute-start | bytes 221192 | tf_op jit(solution)/shard_map/ppermute | solution.py:230
  27.4 4.0 %collective-permute-start.14 = (bf16[8,4608]{1,0:T(8,128)(2,1)S(1)}, bf16[8,4608]{1,0:T(8,128)(2,1)S(1)}, u32[]{:S(2)}, u32[]{:S(2)}) collective-permute-start(bf16[8,4608]{1,0:T(8,128)(2,1)S(1)} %collective-permute-done.13.refs_8_), channel_id=1, source_target_pairs={{0,1},{1,0},{2,3},{3,2},{4,5},{5,4},{6,7},{7,6},{8,9},{9,8},{10,11... | collective-permute-start | bytes 221192 | tf_op jit(solution)/shard_map/ppermute | solution.py:230
  27.6 6.9 %collective-permute-start.10 = (bf16[4,7168]{1,0:T(4,128)(2,1)S(1)}, bf16[4,7168]{1,0:T(4,128)(2,1)S(1)}, u32[]{:S(2)}, u32[]{:S(2)}) collective-permute-start(bf16[4,7168]{1,0:T(4,128)(2,1)S(1)} %get-tuple-element.34), channel_id=1, source_target_pairs={{0,4},{1,5},{2,6},{3,7},{4,0},{5,1},{6,2},{7,3},{8,12},{9,13},{10,... | collective-permute-start | bytes 172040 | tf_op jit(solution)/shard_map/ppermute | solution.py:230
  27.7 6.8 %collective-permute-start.11 = (bf16[4,7168]{1,0:T(4,128)(2,1)S(1)}, bf16[4,7168]{1,0:T(4,128)(2,1)S(1)}, u32[]{:S(2)}, u32[]{:S(2)}) collective-permute-start(bf16[4,7168]{1,0:T(4,128)(2,1)S(1)} %get-tuple-element.33), channel_id=1, source_target_pairs={{0,6},{1,7},{2,4},{3,5},{4,2},{5,3},{6,0},{7,1},{8,14},{9,15},{10,... | collective-permute-start | bytes 172040 | tf_op jit(solution)/shard_map/ppermute | solution.py:230
  29.7 4.8 %collective-permute-start.9 = (bf16[4,7168]{1,0:T(4,128)(2,1)S(1)}, bf16[4,7168]{1,0:T(4,128)(2,1)S(1)}, u32[]{:S(2)}, u32[]{:S(2)}) collective-permute-start(bf16[4,7168]{1,0:T(4,128)(2,1)S(1)} %get-tuple-element.32), channel_id=1, source_target_pairs={{0,2},{1,3},{2,0},{3,1},{4,6},{5,7},{6,4},{7,5},{8,10},{9,11},{10,... | collective-permute-start | bytes 172040 | tf_op jit(solution)/shard_map/ppermute | solution.py:230
  34.6 5.1 %collective-permute-start.12 = (bf16[2,7168]{1,0:T(2,128)(2,1)S(1)}, bf16[2,7168]{1,0:T(2,128)(2,1)S(1)}, u32[]{:S(2)}, u32[]{:S(2)}) collective-permute-start(bf16[2,7168]{1,0:T(2,128)(2,1)S(1)} %slice.85), channel_id=1, source_target_pairs={{0,8},{1,9},{2,10},{3,11},{4,12},{5,13},{6,14},{7,15},{8,0},{9,1},... | collective-permute-start | bytes 86024 | tf_op jit(solution)/shard_map/ppermute | solution.py:230

commit v5 on v4

--- a/solution.py
+++ b/solution.py
@@ -110,38 +110,36 @@
         out_ref[...] = result[m * rows : (m + 1) * rows, :].astype(jnp.bfloat16)
 
 
-def join_kernel(groups, *refs):
-    row_refs, rest = refs[:groups], refs[groups:]
-    block_refs, out_refs = rest[: len(rest) // 2], rest[len(rest) // 2 :]
-    caps, width = row_refs[0].shape
-    for block_ref, out_ref in zip(block_refs, out_refs):
-        for b, row_ref in enumerate(row_refs):
-            out_ref[b * caps : (b + 1) * caps, :width] = row_ref[...]
-        out_ref[:, width:] = block_ref[...]
-
-
-def leaving_kernel(shift, *refs):
+def entry_kernel(
+    caps, shards, mine_ref, routes_ref, me_ref, order_ref, tokens_ref, pool_ref, *out_refs
+):
+    groups = len(out_refs) - shards // 2
+    pack_kernel(caps, mine_ref, routes_ref, tokens_ref, *out_refs[:groups])
+    outgoing_kernel(shards, me_ref, order_ref, pool_ref, *out_refs[groups:])
+
+
+def join_kernel(*refs):
+    *in_refs, out_ref = refs
+    rows = in_refs[0].shape[0]
+    for i, in_ref in enumerate(in_refs):
+        out_ref[i * rows : (i + 1) * rows, :] = in_ref[...]
+
+
+def sorting_kernel(*refs):
     groups = refs[0].shape[0] // 2
-    for b, out_ref in enumerate(refs[len(refs) - groups + 1 :], 1):
-        for m, in_ref in enumerate(refs[: len(refs) - groups + 1]):
-            out_ref[2 * m : 2 * m + 2, :] = in_ref[2 * b : 2 * b + 2, shift:]
-
-
-def attention_kernel(
-    groups, shards, shift, me_ref, table_ref, lens_ref, queries_ref, *refs
-):
+    in_refs, out_refs = refs[:-groups], refs[-groups:]
+    for b, out_ref in enumerate(out_refs):
+        for m, in_ref in enumerate(in_refs):
+            out_ref[2 * m : 2 * m + 2, :] = in_ref[2 * b : 2 * b + 2, :]
+
+
+def attention_kernel(groups, shards, me_ref, table_ref, lens_ref, queries_ref, *refs):
     *arrived_refs, out_ref, arrived = refs
     sequences, heads, entries = queries_ref.shape
     pairs = shards // 2
     side = groups * shards
-    for a in range(2):
-        near_refs = arrived_refs[a * pairs : (a + 1) * pairs]
-        far_refs = arrived_refs[2 * pairs + a * (groups - 1) : 2 * pairs + (a + 1) * (groups - 1)]
-        for m, near_ref in enumerate(near_refs):
-            arrived[a * side + 2 * m : a * side + 2 * m + 2, :] = near_ref[:2, shift:]
-        for b, far_ref in enumerate(far_refs, 1):
-            start = a * side + b * shards
-            arrived[start : start + shards, :] = far_ref[...]
+    for i, arrived_ref in enumerate(arrived_refs):
+        arrived[i * shards : (i + 1) * shards, :] = arrived_ref[...]
     count = side
     half = count // 2
     row = lax.broadcasted_iota(jnp.int32, (count, 2 * count), 0)
@@ -238,49 +236,53 @@
     small = pltpu.CompilerParams(vmem_limit_bytes=8 * 1024 * 1024)
     routes = routes.T
 
-    packed = kernel(
-        functools.partial(pack_kernel, capacity),
-        out_shape=[jax.ShapeDtypeStruct((capacity, width), jnp.bfloat16)] * experts,
-        in_specs=[smem(), smem(), vmem()],
-        out_specs=[vmem()] * experts,
+    block_width = latent_pool.shape[1]
+    pairs = shard_count // 2
+    entry = kernel(
+        functools.partial(entry_kernel, capacity, shard_count),
+        out_shape=[jax.ShapeDtypeStruct((capacity, width), jnp.bfloat16)] * experts
+        + [jax.ShapeDtypeStruct((2 * experts, block_width), jnp.bfloat16)] * pairs,
+        in_specs=[smem()] * 4 + [vmem()] * 2,
+        out_specs=[vmem()] * (experts + pairs),
         compiler_params=small,
-    )(mine, in_hbm(routes), in_hbm(tokens))
+    )(
+        mine,
+        in_hbm(routes),
+        me,
+        in_hbm(send_order),
+        in_hbm(tokens),
+        in_hbm(latent_pool),
+    )
+    packed, outgoing = entry[:experts], entry[experts:]
     crossed = [exchange(packed[b], b * shard_count) for b in range(1, experts)]
     slots = experts * capacity
     assert capacity == 2
 
     compressed_width = LATENT_RANK + ROTARY_WIDTH
-    block_width = latent_pool.shape[1]
-    pairs = shard_count // 2
-    outgoing = kernel(
-        functools.partial(outgoing_kernel, shard_count),
-        out_shape=[jax.ShapeDtypeStruct((2 * experts, block_width), jnp.bfloat16)] * pairs,
-        in_specs=[smem(), smem(), vmem()],
-        out_specs=[vmem()] * pairs,
+    spread = [outgoing[0]] + [exchange(outgoing[m], 2 * m) for m in range(1, pairs)]
+    staying, *leaving = kernel(
+        sorting_kernel,
+        out_shape=[jax.ShapeDtypeStruct((shard_count, block_width), jnp.bfloat16)] * experts,
+        in_specs=[vmem()] * pairs,
+        out_specs=[vmem()] * experts,
         compiler_params=small,
-    )(me, in_hbm(send_order), in_hbm(latent_pool))
-    joined = kernel(
-        functools.partial(join_kernel, experts),
+    )(*spread)
+    entered = [exchange(piece, b * shard_count) for b, piece in enumerate(leaving, 1)]
+    arrived = [staying] + entered
+    arrived = arrived + [exchange(piece, 1) for piece in arrived]
+
+    rows = kernel(
+        join_kernel,
         cost_estimate=pl.CostEstimate(
             flops=8 * 10**9, bytes_accessed=8 * 10**7, transcendentals=0
         ),
-        out_shape=[jax.ShapeDtypeStruct((slots, width + block_width), jnp.bfloat16)] * pairs,
-        in_specs=[vmem()] * (experts + pairs),
-        out_specs=[vmem()] * pairs,
+        out_shape=jax.ShapeDtypeStruct((slots, width), jnp.bfloat16),
+        in_specs=[vmem()] * experts,
+        out_specs=vmem(),
         compiler_params=small,
-    )(packed[0], *crossed, *outgoing)
-    near = [joined[0]] + [exchange(joined[m], 2 * m) for m in range(1, pairs)]
+    )(packed[0], *crossed)
+    near = [rows] + [exchange(rows, 2 * m) for m in range(1, pairs)]
     far = [exchange(piece, 1) for piece in near]
-    leaving = kernel(
-        functools.partial(leaving_kernel, width),
-        out_shape=[jax.ShapeDtypeStruct((shard_count, block_width), jnp.bfloat16)]
-        * (experts - 1),
-        in_specs=[vmem()] * pairs,
-        out_specs=[vmem()] * (experts - 1),
-        compiler_params=small,
-    )(*near)
-    entered = [exchange(leaving[b - 1], b * shard_count) for b in range(1, experts)]
-    arrived = near + far + entered + [exchange(piece, 1) for piece in entered]
 
     half = slots * shard_count // 2
     units = w_gate.shape[1]
@@ -325,7 +327,7 @@
     attention_head_count = queries.shape[1] // compressed_width
     query_rows = queries.reshape(sequence_total, attention_head_count, compressed_width)
     attended = kernel(
-        functools.partial(attention_kernel, experts, shard_count, width),
+        functools.partial(attention_kernel, experts, shard_count),
         out_shape=jax.ShapeDtypeStruct(
             (sequence_total, attention_head_count, LATENT_RANK), jnp.bfloat16
         ),

time: 40.8 us -> 45.6 us (1.12)
  starting transfers between devices: 16.7 us -> 19.9 us
  waiting for transfers between devices: 12.6 us -> 15 us
  Pallas kernels: 7.31 us -> 6.5 us
    ppermute x15 -> x19, starting transfers between devices: 16.7 us -> 19.9 us  [exchange(): lax.ppermute(value, 'ep', [(i, i ^ mask) for i in range(device_count)])]
    ppermute x15 -> x19, waiting for transfers between devices: 12.6 us -> 15 us  [exchange(): lax.ppermute(value, 'ep', [(i, i ^ mask) for i in range(device_count)])]
    pallas_call x7 -> x6, Pallas kernels: 7.31 us -> 6.5 us  [call(): return pl.pallas_call(body, **options)(*operands)]
  transfers between devices with their start and end apart: 15 -> 19, of which waited for: 7 -> 12; matrix products, arithmetic and copies ran while one was open for 6% -> 5% of each run, Pallas kernels for 10% -> 7%
where the time goes in v5:
time: 45.6 us; the launch traced here: 45.5 us
  starting transfers between devices  19.9 us (44%)
  waiting for transfers between devices  15 us (33%)
  Pallas kernels  6.5 us (14%)
  local copies, waits for them, and re-layouts  2.3 us (5%)
  other arithmetic  0.88 us (2%)
  between operations  0.81 us (2%)
    ppermute x19, starting transfers between devices, exchange(): lax.ppermute(value, 'ep', [(i, i ^ mask) for i in range(device_count)])  19.9 us
    ppermute x19, waiting for transfers between devices, exchange(): lax.ppermute(value, 'ep', [(i, i ^ mask) for i in range(device_count)])  15 us
    pallas_call x6, Pallas kernels, call(): return pl.pallas_call(body, **options)(*operands)  6.5 us
    unnamed x13, local copies, waits for them, and re-layouts  1.23 us
  transfers between devices with their start and end apart: 19, of which 12 were waited for; matrix products, arithmetic and copies ran while one was open for 5% of the time, Pallas kernels for 7%

profile of v5, /device:TPU:0, one launch (start us, length us, event | category | flops | bytes accessed | tf_op | source)
XLA Modules:
  0.0 45.5 jit_solution(5495620090932932539)
XLA Ops:
  0.6 1.3 %shard_map.123 = (bf16[2,7168]{1,0:T(2,128)(2,1)S(1)}, bf16[2,7168]{1,0:T(2,128)(2,1)S(1)}, bf16[4,4608]{1,0:T(4,128)(2,1)S(1)}, bf16[4,4608]{1,0:T(4,128)(2,1)S...) custom-call(s32[1]{0:T(128)S(6)} %select_n.5.mine_ref, s32[1,4]{1,0:T(1,128)} %bitcast.16, s32[1]{0:T(128)} %bitcast.me_ref, ...), custom_call_target="tpu_custom_call" | custom-call | tf_op jit(solution)/shard_map/pallas_call | solution.py:232
  2.0 4.1 %collective-permute-start = (bf16[2,7168]{1,0:T(2,128)(2,1)S(1)}, bf16[2,7168]{1,0:T(2,128)(2,1)S(1)}, u32[]{:S(2)}, u32[]{:S(2)}) collective-permute-start(bf16[2,7168]{1,0:T(2,128)(2,1)S(1)} %get-tuple-element.13), channel_id=1, source_target_pairs={{0,8},{1,9},{2,10},{3,11},{4,12},{5,13},{6,14},{7,15},{8,0},{9,1},... | collective-permute-start | bytes 86024 | tf_op jit(solution)/shard_map/ppermute | solution.py:228
  6.1 1.9 %collective-permute-done.refs_1_ = bf16[2,7168]{1,0:T(2,128)(2,1)S(1)} collective-permute-done((bf16[2,7168]{1,0:T(2,128)(2,1)S(1)}, bf16[2,7168]{1,0:T(2,128)(2,1)S(1)}, u32[]{:S(2)}, u32[]{:S(2)}) %collective-permute-start) | collective-permute-done | bytes 28704 | tf_op jit(solution)/shard_map/ppermute | solution.py:228
  8.0 2.9 %collective-permute-start.3 = (bf16[4,7168]{1,0:T(4,128)(2,1)S(1)}, bf16[4,7168]{1,0:T(4,128)(2,1)S(1)}, u32[]{:S(2)}, u32[]{:S(2)}) collective-permute-start(bf16[4,7168]{1,0:T(4,128)(2,1)S(1)} %shard_map.124.refs_0_), channel_id=1, source_target_pairs={{0,6},{1,7},{2,4},{3,5},{4,2},{5,3},{6,0},{7,1},{8,14},{9,15},{10,... | collective-permute-start | bytes 172040 | tf_op jit(solution)/shard_map/ppermute | solution.py:228
  10.9 0.6 %collective-permute-start.2 = (bf16[4,7168]{1,0:T(4,128)(2,1)S(1)}, bf16[4,7168]{1,0:T(4,128)(2,1)S(1)}, u32[]{:S(2)}, u32[]{:S(2)}) collective-permute-start(bf16[4,7168]{1,0:T(4,128)(2,1)S(1)} %shard_map.124.refs_0_), channel_id=1, source_target_pairs={{0,4},{1,5},{2,6},{3,7},{4,0},{5,1},{6,2},{7,3},{8,12},{9,13},{10,... | collective-permute-start | bytes 172040 | tf_op jit(solution)/shard_map/ppermute | solution.py:228
  11.6 1.7 %collective-permute-done.3.refs_3_ = bf16[4,7168]{1,0:T(4,128)(2,1)S(1)} collective-permute-done((bf16[4,7168]{1,0:T(4,128)(2,1)S(1)}, bf16[4,7168]{1,0:T(4,128)(2,1)S(1)}, u32[]{:S(2)}, u32[]{:S(2)}) %collective-permute-start.3) | collective-permute-done | bytes 57376 | tf_op jit(solution)/shard_map/ppermute | solution.py:228
  13.3 1.8 %collective-permute-done.2.refs_2_ = bf16[4,7168]{1,0:T(4,128)(2,1)S(1)} collective-permute-done((bf16[4,7168]{1,0:T(4,128)(2,1)S(1)}, bf16[4,7168]{1,0:T(4,128)(2,1)S(1)}, u32[]{:S(2)}, u32[]{:S(2)}) %collective-permute-start.2) | collective-permute-done | bytes 57376 | tf_op jit(solution)/shard_map/ppermute | solution.py:228
  15.1 0.6 %collective-permute-done.1.refs_1_ = bf16[4,7168]{1,0:T(4,128)(2,1)S(1)} collective-permute-done((bf16[4,7168]{1,0:T(4,128)(2,1)S(1)}, bf16[4,7168]{1,0:T(4,128)(2,1)S(1)}, u32[]{:S(2)}, u32[]{:S(2)}) %collective-permute-start.1) | collective-permute-done | bytes 57376 | tf_op jit(solution)/shard_map/ppermute | solution.py:228
  16.3 0.6 %collective-permute-done.5.refs_5_ = bf16[4,7168]{1,0:T(4,128)(2,1)S(1)} collective-permute-done((bf16[4,7168]{1,0:T(4,128)(2,1)S(1)}, bf16[4,7168]{1,0:T(4,128)(2,1)S(1)}, u32[]{:S(2)}, u32[]{:S(2)}) %collective-permute-start.5) | collective-permute-done | bytes 57376 | tf_op jit(solution)/shard_map/ppermute | solution.py:228
  17.0 2.1 %shard_map.125 = (bf16[16,7168]{1,0:T(8,128)(2,1)S(1)}, bf16[16,7168]{1,0:T(8,128)(2,1)S(1)}) custom-call(bf16[7168,256]{1,0:T(8,128)(2,1)S(1)} %copy-done, bf16[7168,256]{1,0:T(8,128)(2,1)S(1)} %copy-done.1, bf16[256,7168]{1,0:T(8,128)(2,1)S(1)} %copy-done.2, bf16[4,7168]{1,0:T(4,128)(2,1)S(1)} %shard_map.124.refs_0_, ...), custom_call_target="tpu_custom_call" | custom-call | flops 352321536 | bytes 11010048 | tf_op jit(solution)/shard_map/pallas_call | solution.py:232
  19.5 1.7 %collective-permute-start.14 = (bf16[4,4608]{1,0:T(4,128)(2,1)S(1)}, bf16[4,4608]{1,0:T(4,128)(2,1)S(1)}, u32[]{:S(2)}, u32[]{:S(2)}) collective-permute-start(bf16[4,4608]{1,0:T(4,128)(2,1)S(1)} %get-tuple-element.18), channel_id=1, source_target_pairs={{0,4},{1,5},{2,6},{3,7},{4,0},{5,1},{6,2},{7,3},{8,12},{9,13},{10,... | collective-permute-start | bytes 110600 | tf_op jit(solution)/shard_map/ppermute | solution.py:228
  21.2 1.6 %collective-permute-start.15 = (bf16[4,4608]{1,0:T(4,128)(2,1)S(1)}, bf16[4,4608]{1,0:T(4,128)(2,1)S(1)}, u32[]{:S(2)}, u32[]{:S(2)}) collective-permute-start(bf16[4,4608]{1,0:T(4,128)(2,1)S(1)} %get-tuple-element.19), channel_id=1, source_target_pairs={{0,6},{1,7},{2,4},{3,5},{4,2},{5,3},{6,0},{7,1},{8,14},{9,15},{10,... | collective-permute-start | bytes 110600 | tf_op jit(solution)/shard_map/ppermute | solution.py:228
  23.5 2.6 %collective-permute-done.15.refs_3_ = bf16[4,4608]{1,0:T(4,128)(2,1)S(1)} collective-permute-done((bf16[4,4608]{1,0:T(4,128)(2,1)S(1)}, bf16[4,4608]{1,0:T(4,128)(2,1)S(1)}, u32[]{:S(2)}, u32[]{:S(2)}) %collective-permute-start.15) | collective-permute-done | bytes 36896 | tf_op jit(solution)/shard_map/ppermute | solution.py:228
  26.1 2.9 %collective-permute-start.16 = (bf16[8,4608]{1,0:T(8,128)(2,1)S(1)}, bf16[8,4608]{1,0:T(8,128)(2,1)S(1)}, u32[]{:S(2)}, u32[]{:S(2)}) collective-permute-start(bf16[8,4608]{1,0:T(8,128)(2,1)S(1)} %get-tuple-element.21), channel_id=1, source_target_pairs={{0,8},{1,9},{2,10},{3,11},{4,12},{5,13},{6,14},{7,15},{8,0},{9,1},... | collective-permute-start | bytes 221192 | tf_op jit(solution)/shard_map/ppermute | solution.py:228
  29.0 1.2 %shard_map.122 = f32[4,4]{1,0:T(4,128)S(1)} custom-call(s32[1]{0:T(128)S(6)} %select_n.5.mine_ref, s32[1,4]{1,0:T(1,128)} %bitcast.17, bf16[4,7168]{1,0:T(4,128)(2,1)} %tokens_ref.3, bf16[2,7168]{1,0:T(2,128)(2,1)} %bitcast.15), custom_call_target="tpu_custom_call" | custom-call | tf_op jit(solution)/shard_map/pallas_call | solution.py:232
  30.2 0.7 %reshape.33.queries_ref = bf16[4,128,576]{2,1,0:T(8,128)(2,1)S(1)} reshape(bf16[4,73728]{1,0:T(4,128)(2,1)S(1)} %copy-done.5) | data formatting | bytes 1179648 | tf_op jit(solution)/shard_map/reshape | solution.py:328
  31.0 1.1 %collective-permute-done.16.refs_1_ = bf16[8,4608]{1,0:T(8,128)(2,1)S(1)} collective-permute-done((bf16[8,4608]{1,0:T(8,128)(2,1)S(1)}, bf16[8,4608]{1,0:T(8,128)(2,1)S(1)}, u32[]{:S(2)}, u32[]{:S(2)}) %collective-permute-start.16) | collective-permute-done | bytes 73760 | tf_op jit(solution)/shard_map/ppermute | solution.py:228
  32.2 1.7 %collective-permute-start.9 = (bf16[4,7168]{1,0:T(4,128)(2,1)S(1)}, bf16[4,7168]{1,0:T(4,128)(2,1)S(1)}, u32[]{:S(2)}, u32[]{:S(2)}) collective-permute-start(bf16[4,7168]{1,0:T(4,128)(2,1)S(1)} %get-tuple-element.28), channel_id=1, source_target_pairs={{0,2},{1,3},{2,0},{3,1},{4,6},{5,7},{6,4},{7,5},{8,10},{9,11},{10,... | collective-permute-start | bytes 172040 | tf_op jit(solution)/shard_map/ppermute | solution.py:228
  33.9 1.9 %collective-permute-start.10 = (bf16[4,7168]{1,0:T(4,128)(2,1)S(1)}, bf16[4,7168]{1,0:T(4,128)(2,1)S(1)}, u32[]{:S(2)}, u32[]{:S(2)}) collective-permute-start(bf16[4,7168]{1,0:T(4,128)(2,1)S(1)} %get-tuple-element.30), channel_id=1, source_target_pairs={{0,4},{1,5},{2,6},{3,7},{4,0},{5,1},{6,2},{7,3},{8,12},{9,13},{10,... | collective-permute-start | bytes 172040 | tf_op jit(solution)/shard_map/ppermute | solution.py:228
  36.0 1.8 %shard_map.127 = bf16[4,128,512]{2,1,0:T(8,128)(2,1)S(1)} custom-call(s32[1]{0:T(128)} %bitcast.me_ref, s32[1,16]{1,0:T(1,128)S(1)} %copy-done.3, s32[4]{0:T(128)S(1)} %copy-done.4, bf16[4,128,576]{2,1,0:T(8,128)(2,1)S(1)} %reshape.33.queries_ref, bf16[8,4608]{1,0:T(8,128)(2,1)S(1)} %get-tuple-element.20.refs_0_, ...), custom_call_target="tpu_custom_call" | custom-call | tf_op jit(solution)/shard_map/pallas_call | solution.py:232
  37.9 1.2 %copy.13 = bf16[1,4,128,512]{3,1,2,0:T(4,128)(2,1)} copy(bf16[1,4,128,512]{3,2,1,0:T(8,128)(2,1)S(1)} %bitcast.9) | data formatting | bytes 1048576
  39.6 2.1 %collective-permute-start.12 = (bf16[2,7168]{1,0:T(2,128)(2,1)S(1)}, bf16[2,7168]{1,0:T(2,128)(2,1)S(1)}, u32[]{:S(2)}, u32[]{:S(2)}) collective-permute-start(bf16[2,7168]{1,0:T(2,128)(2,1)S(1)} %slice.85), channel_id=1, source_target_pairs={{0,8},{1,9},{2,10},{3,11},{4,12},{5,13},{6,14},{7,15},{8,0},{9,1},... | collective-permute-start | bytes 86024 | tf_op jit(solution)/shard_map/ppermute | solution.py:228
  41.7 2.9 %collective-permute-done.12 = bf16[2,7168]{1,0:T(2,128)(2,1)S(1)} collective-permute-done((bf16[2,7168]{1,0:T(2,128)(2,1)S(1)}, bf16[2,7168]{1,0:T(2,128)(2,1)S(1)}, u32[]{:S(2)}, u32[]{:S(2)}) %collective-permute-start.12) | collective-permute-done | bytes 28704 | tf_op jit(solution)/shard_map/ppermute | solution.py:228
  44.7 0.8 %add_convert_fusion = bf16[4,7168]{1,0:T(4,128)(2,1)} fusion(f32[7168]{0:T(1024)S(1)} %bitcast.14, f32[4]{0:T(128)S(1)} %get-tuple-element.23, f32[7168]{0:T(1024)S(1)} %bitcast.13, f32[4]{0:T(128)S(1)} %get-tuple-element.24, f32[7168]{0:T(1024)S(1)} %bitcast.12, f32[4]{0:T(128)S(1)} %get-tuple-element.25, f32[7168]{0:T(1024)S(1)} %bitcast.11, ...), kind=kLoop, calls=%fused_computation.4 | loop fusion | flops 229376 | bytes 172096 | tf_op jit(solution)/shard_map/convert_element_type | solution.py:324
  (42 shorter events, 3.0 us)
Async XLA Ops:
  2.0 6.0 %collective-permute-start = (bf16[2,7168]{1,0:T(2,128)(2,1)S(1)}, bf16[2,7168]{1,0:T(2,128)(2,1)S(1)}, u32[]{:S(2)}, u32[]{:S(2)}) collective-permute-start(bf16[2,7168]{1,0:T(2,128)(2,1)S(1)} %get-tuple-element.13), channel_id=1, source_target_pairs={{0,8},{1,9},{2,10},{3,11},{4,12},{5,13},{6,14},{7,15},{8,0},{9,1},... | collective-permute-start | bytes 86024 | tf_op jit(solution)/shard_map/ppermute | solution.py:228
  8.0 9.0 %copy-start.1 = (bf16[7168,256]{1,0:T(8,128)(2,1)S(1)}, bf16[7168,256]{1,0:T(8,128)(2,1)}, u32[]{:S(2)}) copy-start(bf16[7168,256]{1,0:T(8,128)(2,1)} %up_ref.1) | copy-start | bytes 11010052
  8.0 9.0 %copy-start.2 = (bf16[256,7168]{1,0:T(8,128)(2,1)S(1)}, bf16[256,7168]{1,0:T(8,128)(2,1)}, u32[]{:S(2)}) copy-start(bf16[256,7168]{1,0:T(8,128)(2,1)} %down_ref.1) | copy-start | bytes 11010052
  8.0 22.2 %copy-start.5 = (bf16[4,73728]{1,0:T(4,128)(2,1)S(1)}, bf16[4,73728]{1,0:T(4,128)(2,1)}, u32[]{:S(2)}) copy-start(bf16[4,73728]{1,0:T(4,128)(2,1)} %param.21) | copy-start | bytes 1769476
  8.0 28.0 %copy-start.3 = (s32[1,16]{1,0:T(1,128)S(1)}, s32[1,16]{1,0:T(1,128)}, u32[]{:S(2)}) copy-start(s32[1,16]{1,0:T(1,128)} %table_ref.1) | copy-start | bytes 196
  8.0 28.0 %copy-start.4 = (s32[4]{0:T(128)S(1)}, s32[4]{0:T(128)}, u32[]{:S(2)}) copy-start(s32[4]{0:T(128)} %lens_ref.1) | copy-start | bytes 52
  8.0 5.3 %collective-permute-start.3 = (bf16[4,7168]{1,0:T(4,128)(2,1)S(1)}, bf16[4,7168]{1,0:T(4,128)(2,1)S(1)}, u32[]{:S(2)}, u32[]{:S(2)}) collective-permute-start(bf16[4,7168]{1,0:T(4,128)(2,1)S(1)} %shard_map.124.refs_0_), channel_id=1, source_target_pairs={{0,6},{1,7},{2,4},{3,5},{4,2},{5,3},{6,0},{7,1},{8,14},{9,15},{10,... | collective-permute-start | bytes 172040 | tf_op jit(solution)/shard_map/ppermute | solution.py:228
  10.9 4.2 %collective-permute-start.2 = (bf16[4,7168]{1,0:T(4,128)(2,1)S(1)}, bf16[4,7168]{1,0:T(4,128)(2,1)S(1)}, u32[]{:S(2)}, u32[]{:S(2)}) collective-permute-start(bf16[4,7168]{1,0:T(4,128)(2,1)S(1)} %shard_map.124.refs_0_), channel_id=1, source_target_pairs={{0,4},{1,5},{2,6},{3,7},{4,0},{5,1},{6,2},{7,3},{8,12},{9,13},{10,... | collective-permute-start | bytes 172040 | tf_op jit(solution)/shard_map/ppermute | solution.py:228
  11.5 4.2 %collective-permute-start.1 = (bf16[4,7168]{1,0:T(4,128)(2,1)S(1)}, bf16[4,7168]{1,0:T(4,128)(2,1)S(1)}, u32[]{:S(2)}, u32[]{:S(2)}) collective-permute-start(bf16[4,7168]{1,0:T(4,128)(2,1)S(1)} %shard_map.124.refs_0_), channel_id=1, source_target_pairs={{0,2},{1,3},{2,0},{3,1},{4,6},{5,7},{6,4},{7,5},{8,10},{9,11},{10,... | collective-permute-start | bytes 172040 | tf_op jit(solution)/shard_map/ppermute | solution.py:228
  11.6 4.1 %collective-permute-start.4 = (bf16[4,7168]{1,0:T(4,128)(2,1)S(1)}, bf16[4,7168]{1,0:T(4,128)(2,1)S(1)}, u32[]{:S(2)}, u32[]{:S(2)}) collective-permute-start(bf16[4,7168]{1,0:T(4,128)(2,1)S(1)} %shard_map.124.refs_0_), channel_id=1, source_target_pairs={{0,1},{1,0},{2,3},{3,2},{4,5},{5,4},{6,7},{7,6},{8,9},{9,8},{10,11... | collective-permute-start | bytes 172040 | tf_op jit(solution)/shard_map/ppermute | solution.py:228
  13.3 2.4 %collective-permute-start.7 = (bf16[4,7168]{1,0:T(4,128)(2,1)S(1)}, bf16[4,7168]{1,0:T(4,128)(2,1)S(1)}, u32[]{:S(2)}, u32[]{:S(2)}) collective-permute-start(bf16[4,7168]{1,0:T(4,128)(2,1)S(1)} %collective-permute-done.3.refs_3_), channel_id=1, source_target_pairs={{0,1},{1,0},{2,3},{3,2},{4,5},{5,4},{6,7},{7,6},{8,9},{9,8},{10,11... | collective-permute-start | bytes 172040 | tf_op jit(solution)/shard_map/ppermute | solution.py:228
  15.1 1.2 %collective-permute-start.6 = (bf16[4,7168]{1,0:T(4,128)(2,1)S(1)}, bf16[4,7168]{1,0:T(4,128)(2,1)S(1)}, u32[]{:S(2)}, u32[]{:S(2)}) collective-permute-start(bf16[4,7168]{1,0:T(4,128)(2,1)S(1)} %collective-permute-done.2.refs_2_), channel_id=1, source_target_pairs={{0,1},{1,0},{2,3},{3,2},{4,5},{5,4},{6,7},{7,6},{8,9},{9,8},{10,11... | collective-permute-start | bytes 172040 | tf_op jit(solution)/shard_map/ppermute | solution.py:228
  15.7 1.2 %collective-permute-start.5 = (bf16[4,7168]{1,0:T(4,128)(2,1)S(1)}, bf16[4,7168]{1,0:T(4,128)(2,1)S(1)}, u32[]{:S(2)}, u32[]{:S(2)}) collective-permute-start(bf16[4,7168]{1,0:T(4,128)(2,1)S(1)} %collective-permute-done.1.refs_1_), channel_id=1, source_target_pairs={{0,1},{1,0},{2,3},{3,2},{4,5},{5,4},{6,7},{7,6},{8,9},{9,8},{10,11... | collective-permute-start | bytes 172040 | tf_op jit(solution)/shard_map/ppermute | solution.py:228
  19.1 13.0 %collective-permute-start.8 = (bf16[16,7168]{1,0:T(8,128)(2,1)S(1)}, bf16[16,7168]{1,0:T(8,128)(2,1)S(1)}, u32[]{:S(2)}, u32[]{:S(2)}) collective-permute-start(bf16[16,7168]{1,0:T(8,128)(2,1)S(1)} %get-tuple-element.15), channel_id=1, source_target_pairs={{0,1},{1,0},{2,3},{3,2},{4,5},{5,4},{6,7},{7,6},{8,9},{9,8},{10,11... | collective-permute-start | bytes 688136 | tf_op jit(solution)/shard_map/ppermute | solution.py:228
  19.3 4.0 %collective-permute-start.13 = (bf16[4,4608]{1,0:T(4,128)(2,1)S(1)}, bf16[4,4608]{1,0:T(4,128)(2,1)S(1)}, u32[]{:S(2)}, u32[]{:S(2)}) collective-permute-start(bf16[4,4608]{1,0:T(4,128)(2,1)S(1)} %get-tuple-element.17), channel_id=1, source_target_pairs={{0,2},{1,3},{2,0},{3,1},{4,6},{5,7},{6,4},{7,5},{8,10},{9,11},{10,... | collective-permute-start | bytes 110600 | tf_op jit(solution)/shard_map/ppermute | solution.py:228
  19.5 4.0 %collective-permute-start.14 = (bf16[4,4608]{1,0:T(4,128)(2,1)S(1)}, bf16[4,4608]{1,0:T(4,128)(2,1)S(1)}, u32[]{:S(2)}, u32[]{:S(2)}) collective-permute-start(bf16[4,4608]{1,0:T(4,128)(2,1)S(1)} %get-tuple-element.18), channel_id=1, source_target_pairs={{0,4},{1,5},{2,6},{3,7},{4,0},{5,1},{6,2},{7,3},{8,12},{9,13},{10,... | collective-permute-start | bytes 110600 | tf_op jit(solution)/shard_map/ppermute | solution.py:228
  21.2 4.9 %collective-permute-start.15 = (bf16[4,4608]{1,0:T(4,128)(2,1)S(1)}, bf16[4,4608]{1,0:T(4,128)(2,1)S(1)}, u32[]{:S(2)}, u32[]{:S(2)}) collective-permute-start(bf16[4,4608]{1,0:T(4,128)(2,1)S(1)} %get-tuple-element.19), channel_id=1, source_target_pairs={{0,6},{1,7},{2,4},{3,5},{4,2},{5,3},{6,0},{7,1},{8,14},{9,15},{10,... | collective-permute-start | bytes 110600 | tf_op jit(solution)/shard_map/ppermute | solution.py:228
  26.1 6.0 %collective-permute-start.16 = (bf16[8,4608]{1,0:T(8,128)(2,1)S(1)}, bf16[8,4608]{1,0:T(8,128)(2,1)S(1)}, u32[]{:S(2)}, u32[]{:S(2)}) collective-permute-start(bf16[8,4608]{1,0:T(8,128)(2,1)S(1)} %get-tuple-element.21), channel_id=1, source_target_pairs={{0,8},{1,9},{2,10},{3,11},{4,12},{5,13},{6,14},{7,15},{8,0},{9,1},... | collective-permute-start | bytes 221192 | tf_op jit(solution)/shard_map/ppermute | solution.py:228
  30.9 5.1 %collective-permute-start.17 = (bf16[8,4608]{1,0:T(8,128)(2,1)S(1)}, bf16[8,4608]{1,0:T(8,128)(2,1)S(1)}, u32[]{:S(2)}, u32[]{:S(2)}) collective-permute-start(bf16[8,4608]{1,0:T(8,128)(2,1)S(1)} %get-tuple-element.20.refs_0_), channel_id=1, source_target_pairs={{0,1},{1,0},{2,3},{3,2},{4,5},{5,4},{6,7},{7,6},{8,9},{9,8},{10,11... | collective-permute-start | bytes 221192 | tf_op jit(solution)/shard_map/ppermute | solution.py:228
  32.1 3.9 %collective-permute-start.18 = (bf16[8,4608]{1,0:T(8,128)(2,1)S(1)}, bf16[8,4608]{1,0:T(8,128)(2,1)S(1)}, u32[]{:S(2)}, u32[]{:S(2)}) collective-permute-start(bf16[8,4608]{1,0:T(8,128)(2,1)S(1)} %collective-permute-done.16.refs_1_), channel_id=1, source_target_pairs={{0,1},{1,0},{2,3},{3,2},{4,5},{5,4},{6,7},{7,6},{8,9},{9,8},{10,11... | collective-permute-start | bytes 221192 | tf_op jit(solution)/shard_map/ppermute | solution.py:228
  32.2 6.8 %collective-permute-start.9 = (bf16[4,7168]{1,0:T(4,128)(2,1)S(1)}, bf16[4,7168]{1,0:T(4,128)(2,1)S(1)}, u32[]{:S(2)}, u32[]{:S(2)}) collective-permute-start(bf16[4,7168]{1,0:T(4,128)(2,1)S(1)} %get-tuple-element.28), channel_id=1, source_target_pairs={{0,2},{1,3},{2,0},{3,1},{4,6},{5,7},{6,4},{7,5},{8,10},{9,11},{10,... | collective-permute-start | bytes 172040 | tf_op jit(solution)/shard_map/ppermute | solution.py:228
  33.9 5.6 %collective-permute-start.11 = (bf16[4,7168]{1,0:T(4,128)(2,1)S(1)}, bf16[4,7168]{1,0:T(4,128)(2,1)S(1)}, u32[]{:S(2)}, u32[]{:S(2)}) collective-permute-start(bf16[4,7168]{1,0:T(4,128)(2,1)S(1)} %get-tuple-element.29), channel_id=1, source_target_pairs={{0,6},{1,7},{2,4},{3,5},{4,2},{5,3},{6,0},{7,1},{8,14},{9,15},{10,... | collective-permute-start | bytes 172040 | tf_op jit(solution)/shard_map/ppermute | solution.py:228
  33.9 5.6 %collective-permute-start.10 = (bf16[4,7168]{1,0:T(4,128)(2,1)S(1)}, bf16[4,7168]{1,0:T(4,128)(2,1)S(1)}, u32[]{:S(2)}, u32[]{:S(2)}) collective-permute-start(bf16[4,7168]{1,0:T(4,128)(2,1)S(1)} %get-tuple-element.30), channel_id=1, source_target_pairs={{0,4},{1,5},{2,6},{3,7},{4,0},{5,1},{6,2},{7,3},{8,12},{9,13},{10,... | collective-permute-start | bytes 172040 | tf_op jit(solution)/shard_map/ppermute | solution.py:228
  39.6 5.0 %collective-permute-start.12 = (bf16[2,7168]{1,0:T(2,128)(2,1)S(1)}, bf16[2,7168]{1,0:T(2,128)(2,1)S(1)}, u32[]{:S(2)}, u32[]{:S(2)}) collective-permute-start(bf16[2,7168]{1,0:T(2,128)(2,1)S(1)} %slice.85), channel_id=1, source_target_pairs={{0,8},{1,9},{2,10},{3,11},{4,12},{5,13},{6,14},{7,15},{8,0},{9,1},... | collective-permute-start | bytes 86024 | tf_op jit(solution)/shard_map/ppermute | solution.py:228
  (1 other events, 9.0 us)

commit v6 on v5

--- a/solution.py
+++ b/solution.py
@@ -102,7 +102,8 @@
     block = lax.broadcasted_iota(jnp.int32, (total, blocks), 1)
     wanted = jnp.zeros((total, blocks), jnp.int32)
     for i in range(total):
-        target = shards * (i % rows // 2) + 2 * (i // rows) + i % 2
+        m, b, r = i // rows, i % rows // 2, i % 2
+        target = shards * b + 2 * m + (r ^ (b > 0) ^ (m > 0))
         wanted = jnp.where(row == i, order_ref[0, me_ref[0] ^ target], wanted)
     picks = jnp.where(block == wanted, 1.0, 0.0).astype(jnp.bfloat16)
     result = jnp.dot(picks, pool_ref[...], preferred_element_type=jnp.float32)
@@ -137,10 +138,9 @@
     *arrived_refs, out_ref, arrived = refs
     sequences, heads, entries = queries_ref.shape
     pairs = shards // 2
-    side = groups * shards
     for i, arrived_ref in enumerate(arrived_refs):
         arrived[i * shards : (i + 1) * shards, :] = arrived_ref[...]
-    count = side
+    count = groups * shards
     half = count // 2
     row = lax.broadcasted_iota(jnp.int32, (count, 2 * count), 0)
     column = lax.broadcasted_iota(jnp.int32, (count, 2 * count), 1)
@@ -153,9 +153,11 @@
     key = lax.broadcasted_iota(jnp.int32, (1, keys), 1)
     token = key // count
     place = key % count
-    source = me_ref[0] ^ (
-        place // half + 2 * (place % pairs) + shards * (place % half // pairs)
-    )
+    side = place // half
+    group = place % half // pairs
+    pair = place % pairs
+    turns = side + jnp.where(group > 0, 1, 0) + jnp.where(pair > 0, 1, 0)
+    source = me_ref[0] ^ (turns % 2 + 2 * pair + shards * group)
     per_sequence = count // sequences
     visible = []
     for s in range(sequences):
@@ -254,12 +256,12 @@
         in_hbm(latent_pool),
     )
     packed, outgoing = entry[:experts], entry[experts:]
-    crossed = [exchange(packed[b], b * shard_count) for b in range(1, experts)]
+    crossed = [exchange(packed[b], b * shard_count + 1) for b in range(1, experts)]
     slots = experts * capacity
     assert capacity == 2
 
     compressed_width = LATENT_RANK + ROTARY_WIDTH
-    spread = [outgoing[0]] + [exchange(outgoing[m], 2 * m) for m in range(1, pairs)]
+    spread = [outgoing[0]] + [exchange(outgoing[m], 2 * m + 1) for m in range(1, pairs)]
     staying, *leaving = kernel(
         sorting_kernel,
         out_shape=[jax.ShapeDtypeStruct((shard_count, block_width), jnp.bfloat16)] * experts,
@@ -267,7 +269,7 @@
         out_specs=[vmem()] * experts,
         compiler_params=small,
     )(*spread)
-    entered = [exchange(piece, b * shard_count) for b, piece in enumerate(leaving, 1)]
+    entered = [exchange(piece, b * shard_count + 1) for b, piece in enumerate(leaving, 1)]
     arrived = [staying] + entered
     arrived = arrived + [exchange(piece, 1) for piece in arrived]
 
@@ -281,7 +283,7 @@
         out_specs=vmem(),
         compiler_params=small,
     )(packed[0], *crossed)
-    near = [rows] + [exchange(rows, 2 * m) for m in range(1, pairs)]
+    near = [rows] + [exchange(rows, 2 * m + 1) for m in range(1, pairs)]
     far = [exchange(piece, 1) for piece in near]
 
     half = slots * shard_count // 2
@@ -299,14 +301,29 @@
         ),
     )(w_gate, w_up, w_down, *near, *far)
 
+    sequence_total = seq_lens.shape[0]
+    attention_head_count = queries.shape[1] // compressed_width
+    query_rows = queries.reshape(sequence_total, attention_head_count, compressed_width)
+    attended = kernel(
+        functools.partial(attention_kernel, experts, shard_count),
+        out_shape=jax.ShapeDtypeStruct(
+            (sequence_total, attention_head_count, LATENT_RANK), jnp.bfloat16
+        ),
+        in_specs=[smem()] * 3 + [vmem()] * (1 + len(arrived)),
+        out_specs=vmem(),
+        scratch_shapes=[pltpu.VMEM((2 * device_count, block_width), jnp.bfloat16)],
+        compiler_params=pltpu.CompilerParams(vmem_limit_bytes=32 * 1024 * 1024),
+    )(me, block_table, seq_lens, query_rows, *arrived)
     paired = keep.astype(jnp.float32) + exchange(send, 1).astype(jnp.float32)
     paired = paired.reshape(shard_count // 2, slots, width)
     total = paired[0]
     for k in range(1, shard_count // 2):
-        total = total + exchange(paired[k].astype(jnp.bfloat16), 2 * k).astype(jnp.float32)
+        total = total + exchange(paired[k].astype(jnp.bfloat16), 2 * k + 1).astype(jnp.float32)
+    total, attended = lax.optimization_barrier((total, attended))
+    attended = attended.reshape(sequence_total, attention_head_count * LATENT_RANK)
     total = total.reshape(experts, capacity, width)
     summed = [total[0]] + [
-        exchange(total[b].astype(jnp.bfloat16), b * shard_count).astype(jnp.float32)
+        exchange(total[b].astype(jnp.bfloat16), b * shard_count + 1).astype(jnp.float32)
         for b in range(1, experts)
     ]
     mixing = kernel(
@@ -323,20 +340,6 @@
             expert_out = expert_out + mixing[:, r : r + 1] * summed[b][c : c + 1, :]
     expert_out = expert_out.astype(jnp.bfloat16)
 
-    sequence_total = seq_lens.shape[0]
-    attention_head_count = queries.shape[1] // compressed_width
-    query_rows = queries.reshape(sequence_total, attention_head_count, compressed_width)
-    attended = kernel(
-        functools.partial(attention_kernel, experts, shard_count),
-        out_shape=jax.ShapeDtypeStruct(
-            (sequence_total, attention_head_count, LATENT_RANK), jnp.bfloat16
-        ),
-        in_specs=[smem()] * 3 + [vmem()] * (1 + len(arrived)),
-        out_specs=vmem(),
-        scratch_shapes=[pltpu.VMEM((2 * device_count, block_width), jnp.bfloat16)],
-        compiler_params=pltpu.CompilerParams(vmem_limit_bytes=32 * 1024 * 1024),
-    )(me, block_table, seq_lens, query_rows, *arrived)
-    attended = attended.reshape(sequence_total, attention_head_count * LATENT_RANK)
     return (expert_out, attended)
 
 

time: 45.6 us -> 44.4 us (0.974)
  waiting for transfers between devices: 15 us -> 13.6 us
    ppermute x19, waiting for transfers between devices: 15 us -> 13.6 us  [exchange(): lax.ppermute(value, 'ep', [(i, i ^ mask) for i in range(device_count)])]
where the time goes in v6:
time: 44.4 us; the launch traced here: 44 us
  starting transfers between devices  20 us (45%)
  waiting for transfers between devices  13.6 us (31%)
  Pallas kernels  6.5 us (15%)
  local copies, waits for them, and re-layouts  2.29 us (5%)
  other arithmetic  0.87 us (2%)
  between operations  0.8 us (2%)
    ppermute x19, starting transfers between devices, exchange(): lax.ppermute(value, 'ep', [(i, i ^ mask) for i in range(device_count)])  20 us
    ppermute x19, waiting for transfers between devices, exchange(): lax.ppermute(value, 'ep', [(i, i ^ mask) for i in range(device_count)])  13.6 us
    pallas_call x6, Pallas kernels, call(): return pl.pallas_call(body, **options)(*operands)  6.5 us
    unnamed x13, local copies, waits for them, and re-layouts  1.23 us
  transfers between devices with their start and end apart: 19, of which 12 were waited for; matrix products, arithmetic and copies ran while one was open for 5% of the time, Pallas kernels for 7%

profile of v6, /device:TPU:0, one launch (start us, length us, event | category | flops | bytes accessed | tf_op | source)
XLA Modules:
  0.0 44.0 jit_solution(6264566505287588739)
XLA Ops:
  0.6 1.3 %shard_map.123 = (bf16[2,7168]{1,0:T(2,128)(2,1)S(1)}, bf16[2,7168]{1,0:T(2,128)(2,1)S(1)}, bf16[4,4608]{1,0:T(4,128)(2,1)S(1)}, bf16[4,4608]{1,0:T(4,128)(2,1)S...) custom-call(s32[1]{0:T(128)S(6)} %select_n.5.mine_ref, s32[1,4]{1,0:T(1,128)} %bitcast.16, s32[1]{0:T(128)} %bitcast.me_ref, ...), custom_call_target="tpu_custom_call" | custom-call | tf_op jit(solution)/shard_map/pallas_call | solution.py:234
  2.0 3.6 %collective-permute-start = (bf16[2,7168]{1,0:T(2,128)(2,1)S(1)}, bf16[2,7168]{1,0:T(2,128)(2,1)S(1)}, u32[]{:S(2)}, u32[]{:S(2)}) collective-permute-start(bf16[2,7168]{1,0:T(2,128)(2,1)S(1)} %get-tuple-element.15), channel_id=1, source_target_pairs={{0,9},{1,8},{2,11},{3,10},{4,13},{5,12},{6,15},{7,14},{8,1},{9,0},... | collective-permute-start | bytes 86024 | tf_op jit(solution)/shard_map/ppermute | solution.py:230
  5.5 1.7 %collective-permute-done.refs_1_ = bf16[2,7168]{1,0:T(2,128)(2,1)S(1)} collective-permute-done((bf16[2,7168]{1,0:T(2,128)(2,1)S(1)}, bf16[2,7168]{1,0:T(2,128)(2,1)S(1)}, u32[]{:S(2)}, u32[]{:S(2)}) %collective-permute-start) | collective-permute-done | bytes 28704 | tf_op jit(solution)/shard_map/ppermute | solution.py:230
  7.3 1.8 %collective-permute-start.1 = (bf16[4,7168]{1,0:T(4,128)(2,1)S(1)}, bf16[4,7168]{1,0:T(4,128)(2,1)S(1)}, u32[]{:S(2)}, u32[]{:S(2)}) collective-permute-start(bf16[4,7168]{1,0:T(4,128)(2,1)S(1)} %shard_map.124.refs_0_), channel_id=1, source_target_pairs={{0,3},{1,2},{2,1},{3,0},{4,7},{5,6},{6,5},{7,4},{8,11},{9,10},{10,... | collective-permute-start | bytes 172040 | tf_op jit(solution)/shard_map/ppermute | solution.py:230
  9.1 1.6 %collective-permute-start.2 = (bf16[4,7168]{1,0:T(4,128)(2,1)S(1)}, bf16[4,7168]{1,0:T(4,128)(2,1)S(1)}, u32[]{:S(2)}, u32[]{:S(2)}) collective-permute-start(bf16[4,7168]{1,0:T(4,128)(2,1)S(1)} %shard_map.124.refs_0_), channel_id=1, source_target_pairs={{0,5},{1,4},{2,7},{3,6},{4,1},{5,0},{6,3},{7,2},{8,13},{9,12},{10,... | collective-permute-start | bytes 172040 | tf_op jit(solution)/shard_map/ppermute | solution.py:230
  11.5 1.5 %collective-permute-done.2.refs_2_ = bf16[4,7168]{1,0:T(4,128)(2,1)S(1)} collective-permute-done((bf16[4,7168]{1,0:T(4,128)(2,1)S(1)}, bf16[4,7168]{1,0:T(4,128)(2,1)S(1)}, u32[]{:S(2)}, u32[]{:S(2)}) %collective-permute-start.2) | collective-permute-done | bytes 57376 | tf_op jit(solution)/shard_map/ppermute | solution.py:230
  13.1 2.4 %collective-permute-done.3.refs_3_ = bf16[4,7168]{1,0:T(4,128)(2,1)S(1)} collective-permute-done((bf16[4,7168]{1,0:T(4,128)(2,1)S(1)}, bf16[4,7168]{1,0:T(4,128)(2,1)S(1)}, u32[]{:S(2)}, u32[]{:S(2)}) %collective-permute-start.3) | collective-permute-done | bytes 57376 | tf_op jit(solution)/shard_map/ppermute | solution.py:230
  15.6 1.1 %collective-permute-done.7.refs_7_ = bf16[4,7168]{1,0:T(4,128)(2,1)S(1)} collective-permute-done((bf16[4,7168]{1,0:T(4,128)(2,1)S(1)}, bf16[4,7168]{1,0:T(4,128)(2,1)S(1)}, u32[]{:S(2)}, u32[]{:S(2)}) %collective-permute-start.7) | collective-permute-done | bytes 57376 | tf_op jit(solution)/shard_map/ppermute | solution.py:230
  16.8 2.1 %shard_map.125 = (bf16[16,7168]{1,0:T(8,128)(2,1)S(1)}, bf16[16,7168]{1,0:T(8,128)(2,1)S(1)}) custom-call(bf16[7168,256]{1,0:T(8,128)(2,1)S(1)} %copy-done, bf16[7168,256]{1,0:T(8,128)(2,1)S(1)} %copy-done.1, bf16[256,7168]{1,0:T(8,128)(2,1)S(1)} %copy-done.2, bf16[4,7168]{1,0:T(4,128)(2,1)S(1)} %shard_map.124.refs_0_, ...), custom_call_target="tpu_custom_call" | custom-call | flops 352321536 | bytes 11010048 | tf_op jit(solution)/shard_map/pallas_call | solution.py:234
  19.5 1.0 %collective-permute-start.13 = (bf16[4,4608]{1,0:T(4,128)(2,1)S(1)}, bf16[4,4608]{1,0:T(4,128)(2,1)S(1)}, u32[]{:S(2)}, u32[]{:S(2)}) collective-permute-start(bf16[4,4608]{1,0:T(4,128)(2,1)S(1)} %get-tuple-element.20), channel_id=1, source_target_pairs={{0,5},{1,4},{2,7},{3,6},{4,1},{5,0},{6,3},{7,2},{8,13},{9,12},{10,... | collective-permute-start | bytes 110600 | tf_op jit(solution)/shard_map/ppermute | solution.py:230
  20.5 1.7 %collective-permute-start.14 = (bf16[4,4608]{1,0:T(4,128)(2,1)S(1)}, bf16[4,4608]{1,0:T(4,128)(2,1)S(1)}, u32[]{:S(2)}, u32[]{:S(2)}) collective-permute-start(bf16[4,4608]{1,0:T(4,128)(2,1)S(1)} %get-tuple-element.21), channel_id=1, source_target_pairs={{0,7},{1,6},{2,5},{3,4},{4,3},{5,2},{6,1},{7,0},{8,15},{9,14},{10,... | collective-permute-start | bytes 110600 | tf_op jit(solution)/shard_map/ppermute | solution.py:230
  23.0 1.9 %collective-permute-done.14.refs_3_ = bf16[4,4608]{1,0:T(4,128)(2,1)S(1)} collective-permute-done((bf16[4,4608]{1,0:T(4,128)(2,1)S(1)}, bf16[4,4608]{1,0:T(4,128)(2,1)S(1)}, u32[]{:S(2)}, u32[]{:S(2)}) %collective-permute-start.14) | collective-permute-done | bytes 36896 | tf_op jit(solution)/shard_map/ppermute | solution.py:230
  24.9 3.2 %collective-permute-start.15 = (bf16[8,4608]{1,0:T(8,128)(2,1)S(1)}, bf16[8,4608]{1,0:T(8,128)(2,1)S(1)}, u32[]{:S(2)}, u32[]{:S(2)}) collective-permute-start(bf16[8,4608]{1,0:T(8,128)(2,1)S(1)} %get-tuple-element.23), channel_id=1, source_target_pairs={{0,9},{1,8},{2,11},{3,10},{4,13},{5,12},{6,15},{7,14},{8,1},{9,0},... | collective-permute-start | bytes 221192 | tf_op jit(solution)/shard_map/ppermute | solution.py:230
  28.8 1.2 %shard_map.122 = f32[4,4]{1,0:T(4,128)S(1)} custom-call(s32[1]{0:T(128)S(6)} %select_n.5.mine_ref, s32[1,4]{1,0:T(1,128)} %bitcast.17, bf16[4,7168]{1,0:T(4,128)(2,1)} %tokens_ref.3, bf16[2,7168]{1,0:T(2,128)(2,1)} %bitcast.15), custom_call_target="tpu_custom_call" | custom-call | tf_op jit(solution)/shard_map/pallas_call | solution.py:234
  30.4 1.6 %collective-permute-done.15.refs_1_ = bf16[8,4608]{1,0:T(8,128)(2,1)S(1)} collective-permute-done((bf16[8,4608]{1,0:T(8,128)(2,1)S(1)}, bf16[8,4608]{1,0:T(8,128)(2,1)S(1)}, u32[]{:S(2)}, u32[]{:S(2)}) %collective-permute-start.15) | collective-permute-done | bytes 73760 | tf_op jit(solution)/shard_map/ppermute | solution.py:230
  32.5 1.3 %collective-permute-start.11 = (bf16[4,7168]{1,0:T(4,128)(2,1)S(1)}, bf16[4,7168]{1,0:T(4,128)(2,1)S(1)}, u32[]{:S(2)}, u32[]{:S(2)}) collective-permute-start(bf16[4,7168]{1,0:T(4,128)(2,1)S(1)} %get-tuple-element.33), channel_id=1, source_target_pairs={{0,7},{1,6},{2,5},{3,4},{4,3},{5,2},{6,1},{7,0},{8,15},{9,14},{10,... | collective-permute-start | bytes 172040 | tf_op jit(solution)/shard_map/ppermute | solution.py:230
  33.7 0.7 %collective-permute-start.10 = (bf16[4,7168]{1,0:T(4,128)(2,1)S(1)}, bf16[4,7168]{1,0:T(4,128)(2,1)S(1)}, u32[]{:S(2)}, u32[]{:S(2)}) collective-permute-start(bf16[4,7168]{1,0:T(4,128)(2,1)S(1)} %get-tuple-element.34), channel_id=1, source_target_pairs={{0,5},{1,4},{2,7},{3,6},{4,1},{5,0},{6,3},{7,2},{8,13},{9,12},{10,... | collective-permute-start | bytes 172040 | tf_op jit(solution)/shard_map/ppermute | solution.py:230
  34.4 1.1 %collective-permute-start.9 = (bf16[4,7168]{1,0:T(4,128)(2,1)S(1)}, bf16[4,7168]{1,0:T(4,128)(2,1)S(1)}, u32[]{:S(2)}, u32[]{:S(2)}) collective-permute-start(bf16[4,7168]{1,0:T(4,128)(2,1)S(1)} %get-tuple-element.32), channel_id=1, source_target_pairs={{0,3},{1,2},{2,1},{3,0},{4,7},{5,6},{6,5},{7,4},{8,11},{9,10},{10,... | collective-permute-start | bytes 172040 | tf_op jit(solution)/shard_map/ppermute | solution.py:230
  35.8 1.8 %shard_map.127 = bf16[4,128,512]{2,1,0:T(8,128)(2,1)S(1)} custom-call(s32[1]{0:T(128)} %bitcast.me_ref, s32[1,16]{1,0:T(1,128)S(1)} %copy-done.3, s32[4]{0:T(128)S(1)} %copy-done.4, bf16[4,128,576]{2,1,0:T(8,128)(2,1)S(1)} %reshape.33.queries_ref, bf16[8,4608]{1,0:T(8,128)(2,1)S(1)} %get-tuple-element.22.refs_0_, ...), custom_call_target="tpu_custom_call" | custom-call | tf_op jit(solution)/shard_map/pallas_call | solution.py:234
  38.0 0.9 %collective-permute-done.9 = bf16[4,7168]{1,0:T(4,128)(2,1)S(1)} collective-permute-done((bf16[4,7168]{1,0:T(4,128)(2,1)S(1)}, bf16[4,7168]{1,0:T(4,128)(2,1)S(1)}, u32[]{:S(2)}, u32[]{:S(2)}) %collective-permute-start.9) | collective-permute-done | bytes 57376 | tf_op jit(solution)/shard_map/ppermute | solution.py:230
  38.9 1.9 %collective-permute-start.18 = (bf16[2,7168]{1,0:T(2,128)(2,1)S(1)}, bf16[2,7168]{1,0:T(2,128)(2,1)S(1)}, u32[]{:S(2)}, u32[]{:S(2)}) collective-permute-start(bf16[2,7168]{1,0:T(2,128)(2,1)S(1)} %slice.83), channel_id=1, source_target_pairs={{0,9},{1,8},{2,11},{3,10},{4,13},{5,12},{6,15},{7,14},{8,1},{9,0},... | collective-permute-start | bytes 86024 | tf_op jit(solution)/shard_map/ppermute | solution.py:230
  40.9 1.2 %copy.13 = bf16[1,4,128,512]{3,1,2,0:T(4,128)(2,1)} copy(bf16[1,4,128,512]{3,2,1,0:T(8,128)(2,1)S(1)} %bitcast.9) | data formatting | bytes 1048576
  42.1 1.1 %collective-permute-done.18 = bf16[2,7168]{1,0:T(2,128)(2,1)S(1)} collective-permute-done((bf16[2,7168]{1,0:T(2,128)(2,1)S(1)}, bf16[2,7168]{1,0:T(2,128)(2,1)S(1)}, u32[]{:S(2)}, u32[]{:S(2)}) %collective-permute-start.18) | collective-permute-done | bytes 28704 | tf_op jit(solution)/shard_map/ppermute | solution.py:230
  43.3 0.8 %add_convert_fusion = bf16[4,7168]{1,0:T(4,128)(2,1)} fusion(f32[7168]{0:T(1024)S(1)} %bitcast.14, f32[4]{0:T(128)S(1)} %get-tuple-element.27, f32[7168]{0:T(1024)S(1)} %bitcast.13, f32[4]{0:T(128)S(1)} %get-tuple-element.28, f32[7168]{0:T(1024)S(1)} %bitcast.12, f32[4]{0:T(128)S(1)} %get-tuple-element.29, f32[7168]{0:T(1024)S(1)} %bitcast.11, ...), kind=kLoop, calls=%fused_computation.4 | loop fusion | flops 229376 | bytes 172096 | tf_op jit(solution)/shard_map/convert_element_type | solution.py:341
  (42 shorter events, 4.9 us)
Async XLA Ops:
  2.0 5.3 %collective-permute-start = (bf16[2,7168]{1,0:T(2,128)(2,1)S(1)}, bf16[2,7168]{1,0:T(2,128)(2,1)S(1)}, u32[]{:S(2)}, u32[]{:S(2)}) collective-permute-start(bf16[2,7168]{1,0:T(2,128)(2,1)S(1)} %get-tuple-element.15), channel_id=1, source_target_pairs={{0,9},{1,8},{2,11},{3,10},{4,13},{5,12},{6,15},{7,14},{8,1},{9,0},... | collective-permute-start | bytes 86024 | tf_op jit(solution)/shard_map/ppermute | solution.py:230
  7.2 9.5 %copy-start.1 = (bf16[7168,256]{1,0:T(8,128)(2,1)S(1)}, bf16[7168,256]{1,0:T(8,128)(2,1)}, u32[]{:S(2)}) copy-start(bf16[7168,256]{1,0:T(8,128)(2,1)} %up_ref.1) | copy-start | bytes 11010052
  7.2 9.5 %copy-start.2 = (bf16[256,7168]{1,0:T(8,128)(2,1)S(1)}, bf16[256,7168]{1,0:T(8,128)(2,1)}, u32[]{:S(2)}) copy-start(bf16[256,7168]{1,0:T(8,128)(2,1)} %down_ref.1) | copy-start | bytes 11010052
  7.3 20.8 %copy-start.5 = (bf16[4,73728]{1,0:T(4,128)(2,1)S(1)}, bf16[4,73728]{1,0:T(4,128)(2,1)}, u32[]{:S(2)}) copy-start(bf16[4,73728]{1,0:T(4,128)(2,1)} %param.21) | copy-start | bytes 1769476
  7.3 28.5 %copy-start.3 = (s32[1,16]{1,0:T(1,128)S(1)}, s32[1,16]{1,0:T(1,128)}, u32[]{:S(2)}) copy-start(s32[1,16]{1,0:T(1,128)} %table_ref.1) | copy-start | bytes 196
  7.3 28.5 %copy-start.4 = (s32[4]{0:T(128)S(1)}, s32[4]{0:T(128)}, u32[]{:S(2)}) copy-start(s32[4]{0:T(128)} %lens_ref.1) | copy-start | bytes 52
  7.3 3.8 %collective-permute-start.1 = (bf16[4,7168]{1,0:T(4,128)(2,1)S(1)}, bf16[4,7168]{1,0:T(4,128)(2,1)S(1)}, u32[]{:S(2)}, u32[]{:S(2)}) collective-permute-start(bf16[4,7168]{1,0:T(4,128)(2,1)S(1)} %shard_map.124.refs_0_), channel_id=1, source_target_pairs={{0,3},{1,2},{2,1},{3,0},{4,7},{5,6},{6,5},{7,4},{8,11},{9,10},{10,... | collective-permute-start | bytes 172040 | tf_op jit(solution)/shard_map/ppermute | solution.py:230
  9.1 3.9 %collective-permute-start.2 = (bf16[4,7168]{1,0:T(4,128)(2,1)S(1)}, bf16[4,7168]{1,0:T(4,128)(2,1)S(1)}, u32[]{:S(2)}, u32[]{:S(2)}) collective-permute-start(bf16[4,7168]{1,0:T(4,128)(2,1)S(1)} %shard_map.124.refs_0_), channel_id=1, source_target_pairs={{0,5},{1,4},{2,7},{3,6},{4,1},{5,0},{6,3},{7,2},{8,13},{9,12},{10,... | collective-permute-start | bytes 172040 | tf_op jit(solution)/shard_map/ppermute | solution.py:230
  10.7 4.8 %collective-permute-start.3 = (bf16[4,7168]{1,0:T(4,128)(2,1)S(1)}, bf16[4,7168]{1,0:T(4,128)(2,1)S(1)}, u32[]{:S(2)}, u32[]{:S(2)}) collective-permute-start(bf16[4,7168]{1,0:T(4,128)(2,1)S(1)} %shard_map.124.refs_0_), channel_id=1, source_target_pairs={{0,7},{1,6},{2,5},{3,4},{4,3},{5,2},{6,1},{7,0},{8,15},{9,14},{10,... | collective-permute-start | bytes 172040 | tf_op jit(solution)/shard_map/ppermute | solution.py:230
  10.7 4.9 %collective-permute-start.4 = (bf16[4,7168]{1,0:T(4,128)(2,1)S(1)}, bf16[4,7168]{1,0:T(4,128)(2,1)S(1)}, u32[]{:S(2)}, u32[]{:S(2)}) collective-permute-start(bf16[4,7168]{1,0:T(4,128)(2,1)S(1)} %shard_map.124.refs_0_), channel_id=1, source_target_pairs={{0,1},{1,0},{2,3},{3,2},{4,5},{5,4},{6,7},{7,6},{8,9},{9,8},{10,11... | collective-permute-start | bytes 172040 | tf_op jit(solution)/shard_map/ppermute | solution.py:230
  11.1 4.5 %collective-permute-start.5 = (bf16[4,7168]{1,0:T(4,128)(2,1)S(1)}, bf16[4,7168]{1,0:T(4,128)(2,1)S(1)}, u32[]{:S(2)}, u32[]{:S(2)}) collective-permute-start(bf16[4,7168]{1,0:T(4,128)(2,1)S(1)} %collective-permute-done.1.refs_1_), channel_id=1, source_target_pairs={{0,1},{1,0},{2,3},{3,2},{4,5},{5,4},{6,7},{7,6},{8,9},{9,8},{10,11... | collective-permute-start | bytes 172040 | tf_op jit(solution)/shard_map/ppermute | solution.py:230
  13.0 2.6 %collective-permute-start.6 = (bf16[4,7168]{1,0:T(4,128)(2,1)S(1)}, bf16[4,7168]{1,0:T(4,128)(2,1)S(1)}, u32[]{:S(2)}, u32[]{:S(2)}) collective-permute-start(bf16[4,7168]{1,0:T(4,128)(2,1)S(1)} %collective-permute-done.2.refs_2_), channel_id=1, source_target_pairs={{0,1},{1,0},{2,3},{3,2},{4,5},{5,4},{6,7},{7,6},{8,9},{9,8},{10,11... | collective-permute-start | bytes 172040 | tf_op jit(solution)/shard_map/ppermute | solution.py:230
  15.5 1.2 %collective-permute-start.7 = (bf16[4,7168]{1,0:T(4,128)(2,1)S(1)}, bf16[4,7168]{1,0:T(4,128)(2,1)S(1)}, u32[]{:S(2)}, u32[]{:S(2)}) collective-permute-start(bf16[4,7168]{1,0:T(4,128)(2,1)S(1)} %collective-permute-done.3.refs_3_), channel_id=1, source_target_pairs={{0,1},{1,0},{2,3},{3,2},{4,5},{5,4},{6,7},{7,6},{8,9},{9,8},{10,11... | collective-permute-start | bytes 172040 | tf_op jit(solution)/shard_map/ppermute | solution.py:230
  18.8 13.5 %collective-permute-start.8 = (bf16[16,7168]{1,0:T(8,128)(2,1)S(1)}, bf16[16,7168]{1,0:T(8,128)(2,1)S(1)}, u32[]{:S(2)}, u32[]{:S(2)}) collective-permute-start(bf16[16,7168]{1,0:T(8,128)(2,1)S(1)} %get-tuple-element.17), channel_id=1, source_target_pairs={{0,1},{1,0},{2,3},{3,2},{4,5},{5,4},{6,7},{7,6},{8,9},{9,8},{10,11... | collective-permute-start | bytes 688136 | tf_op jit(solution)/shard_map/ppermute | solution.py:230
  19.1 3.4 %collective-permute-start.12 = (bf16[4,4608]{1,0:T(4,128)(2,1)S(1)}, bf16[4,4608]{1,0:T(4,128)(2,1)S(1)}, u32[]{:S(2)}, u32[]{:S(2)}) collective-permute-start(bf16[4,4608]{1,0:T(4,128)(2,1)S(1)} %get-tuple-element.19), channel_id=1, source_target_pairs={{0,3},{1,2},{2,1},{3,0},{4,7},{5,6},{6,5},{7,4},{8,11},{9,10},{10,... | collective-permute-start | bytes 110600 | tf_op jit(solution)/shard_map/ppermute | solution.py:230
  19.5 3.4 %collective-permute-start.13 = (bf16[4,4608]{1,0:T(4,128)(2,1)S(1)}, bf16[4,4608]{1,0:T(4,128)(2,1)S(1)}, u32[]{:S(2)}, u32[]{:S(2)}) collective-permute-start(bf16[4,4608]{1,0:T(4,128)(2,1)S(1)} %get-tuple-element.20), channel_id=1, source_target_pairs={{0,5},{1,4},{2,7},{3,6},{4,1},{5,0},{6,3},{7,2},{8,13},{9,12},{10,... | collective-permute-start | bytes 110600 | tf_op jit(solution)/shard_map/ppermute | solution.py:230
  20.5 4.3 %collective-permute-start.14 = (bf16[4,4608]{1,0:T(4,128)(2,1)S(1)}, bf16[4,4608]{1,0:T(4,128)(2,1)S(1)}, u32[]{:S(2)}, u32[]{:S(2)}) collective-permute-start(bf16[4,4608]{1,0:T(4,128)(2,1)S(1)} %get-tuple-element.21), channel_id=1, source_target_pairs={{0,7},{1,6},{2,5},{3,4},{4,3},{5,2},{6,1},{7,0},{8,15},{9,14},{10,... | collective-permute-start | bytes 110600 | tf_op jit(solution)/shard_map/ppermute | solution.py:230
  24.9 7.1 %collective-permute-start.15 = (bf16[8,4608]{1,0:T(8,128)(2,1)S(1)}, bf16[8,4608]{1,0:T(8,128)(2,1)S(1)}, u32[]{:S(2)}, u32[]{:S(2)}) collective-permute-start(bf16[8,4608]{1,0:T(8,128)(2,1)S(1)} %get-tuple-element.23), channel_id=1, source_target_pairs={{0,9},{1,8},{2,11},{3,10},{4,13},{5,12},{6,15},{7,14},{8,1},{9,0},... | collective-permute-start | bytes 221192 | tf_op jit(solution)/shard_map/ppermute | solution.py:230
  30.0 5.8 %collective-permute-start.16 = (bf16[8,4608]{1,0:T(8,128)(2,1)S(1)}, bf16[8,4608]{1,0:T(8,128)(2,1)S(1)}, u32[]{:S(2)}, u32[]{:S(2)}) collective-permute-start(bf16[8,4608]{1,0:T(8,128)(2,1)S(1)} %get-tuple-element.22.refs_0_), channel_id=1, source_target_pairs={{0,1},{1,0},{2,3},{3,2},{4,5},{5,4},{6,7},{7,6},{8,9},{9,8},{10,11... | collective-permute-start | bytes 221192 | tf_op jit(solution)/shard_map/ppermute | solution.py:230
  32.0 3.8 %collective-permute-start.17 = (bf16[8,4608]{1,0:T(8,128)(2,1)S(1)}, bf16[8,4608]{1,0:T(8,128)(2,1)S(1)}, u32[]{:S(2)}, u32[]{:S(2)}) collective-permute-start(bf16[8,4608]{1,0:T(8,128)(2,1)S(1)} %collective-permute-done.15.refs_1_), channel_id=1, source_target_pairs={{0,1},{1,0},{2,3},{3,2},{4,5},{5,4},{6,7},{7,6},{8,9},{9,8},{10,11... | collective-permute-start | bytes 221192 | tf_op jit(solution)/shard_map/ppermute | solution.py:230
  32.5 5.1 %collective-permute-start.11 = (bf16[4,7168]{1,0:T(4,128)(2,1)S(1)}, bf16[4,7168]{1,0:T(4,128)(2,1)S(1)}, u32[]{:S(2)}, u32[]{:S(2)}) collective-permute-start(bf16[4,7168]{1,0:T(4,128)(2,1)S(1)} %get-tuple-element.33), channel_id=1, source_target_pairs={{0,7},{1,6},{2,5},{3,4},{4,3},{5,2},{6,1},{7,0},{8,15},{9,14},{10,... | collective-permute-start | bytes 172040 | tf_op jit(solution)/shard_map/ppermute | solution.py:230
  33.7 4.2 %collective-permute-start.10 = (bf16[4,7168]{1,0:T(4,128)(2,1)S(1)}, bf16[4,7168]{1,0:T(4,128)(2,1)S(1)}, u32[]{:S(2)}, u32[]{:S(2)}) collective-permute-start(bf16[4,7168]{1,0:T(4,128)(2,1)S(1)} %get-tuple-element.34), channel_id=1, source_target_pairs={{0,5},{1,4},{2,7},{3,6},{4,1},{5,0},{6,3},{7,2},{8,13},{9,12},{10,... | collective-permute-start | bytes 172040 | tf_op jit(solution)/shard_map/ppermute | solution.py:230
  34.4 4.4 %collective-permute-start.9 = (bf16[4,7168]{1,0:T(4,128)(2,1)S(1)}, bf16[4,7168]{1,0:T(4,128)(2,1)S(1)}, u32[]{:S(2)}, u32[]{:S(2)}) collective-permute-start(bf16[4,7168]{1,0:T(4,128)(2,1)S(1)} %get-tuple-element.32), channel_id=1, source_target_pairs={{0,3},{1,2},{2,1},{3,0},{4,7},{5,6},{6,5},{7,4},{8,11},{9,10},{10,... | collective-permute-start | bytes 172040 | tf_op jit(solution)/shard_map/ppermute | solution.py:230
  38.9 4.3 %collective-permute-start.18 = (bf16[2,7168]{1,0:T(2,128)(2,1)S(1)}, bf16[2,7168]{1,0:T(2,128)(2,1)S(1)}, u32[]{:S(2)}, u32[]{:S(2)}) collective-permute-start(bf16[2,7168]{1,0:T(2,128)(2,1)S(1)} %slice.83), channel_id=1, source_target_pairs={{0,9},{1,8},{2,11},{3,10},{4,13},{5,12},{6,15},{7,14},{8,1},{9,0},... | collective-permute-start | bytes 86024 | tf_op jit(solution)/shard_map/ppermute | solution.py:230
  (1 other events, 9.5 us)
